TPU v7x, 32 devices: a whole 2x2x4 slice. The times are simulated.
32 devices in a mesh: dp: 8 (over y, x, core), tp: 4 (over z).
Axes of the slice: x: 2, y: 2, z: 4, core: 2. Of those that a mesh axis runs over, the one named last changes fastest.
Arguments:
- tokens: bfloat16 [4096, 1536], P(('dp', 'tp')), may hold values from -6 to 6
- positions: int32 [4096], P('dp'), may hold values from 0 to 1023, as said below
- attn_gain: float32 [1536], replicated, may hold values from 0.5 to 1.5
- w_query: bfloat16 [1536, 1536], P('dp', 'tp'), may hold values from -1 to 1
- w_key: bfloat16 [1536, 768], P('dp', 'tp'), may hold values from -1 to 1
- w_value: bfloat16 [1536, 768], P('dp', 'tp'), may hold values from -0.15625 to 0.15625
- w_out: bfloat16 [1536, 1536], P('tp', 'dp'), may hold values from -1.25 to 1.25
- ffn_gain: float32 [1536], replicated, may hold values from 0.5 to 1.5
- w_gate: bfloat16 [1536, 4096], P('dp', 'tp'), may hold values from -0.15625 to 0.15625
- w_up: bfloat16 [1536, 4096], P('dp', 'tp'), may hold values from -0.15625 to 0.15625
- w_down: bfloat16 [4096, 1536], P('tp', 'dp'), may hold values from -0.09375 to 0.09375
- out_grad: bfloat16 [4096, 1536], P(('dp', 'tp')), may hold values from -18 to 18
Outputs:
- output: bfloat16 [4096, 1536], P(('dp', 'tp'))
- tokens_grad: float32 [4096, 1536], P(('dp', 'tp'))
- attn_gain_grad: float32 [1536], replicated
- w_query_grad: float32 [1536, 1536], P('dp', 'tp')
- w_key_grad: float32 [1536, 768], P('dp', 'tp')
- w_value_grad: float32 [1536, 768], P('dp', 'tp')
- w_out_grad: float32 [1536, 1536], P('tp', 'dp')
- ffn_gain_grad: float32 [1536], replicated
- w_gate_grad: float32 [1536, 4096], P('dp', 'tp')
- w_up_grad: float32 [1536, 4096], P('dp', 'tp')
- w_down_grad: float32 [4096, 1536], P('tp', 'dp')
Inputs may be any that keep to these rules, and one draw needn't show every extreme that they name: `positions`: documents are runs of consecutive tokens; a token at position 0 begins a document, any other follows the token before it in the same document; no document is longer than 1024 tokens and one has exactly 1024.
All inputs are finite; a program needn't handle non-finite values.
Results may differ from a plain program's by a relative error of at most 0.014.
The roundings to bfloat16 on the way count: a program that leaves them out, or rounds other values in their place, can miss the bound.
Values may be sent and summed in bfloat16 or wider, within the bound.
A program may use at most 128 MiB of HBM per device.

v0:
```python
import math

import jax
import jax.numpy as jnp
from jax import lax
from jax.sharding import PartitionSpec as P

HD = 96


norm_eps = 1e-05
rope_base = 100000.0
masked_score = -1e30


def passed_along(block, axis, distance):
    devices = range(lax.axis_size(axis))
    route = [(i - distance, i) for i in devices if i - distance in devices]
    return lax.ppermute(block, axis, route)


def rope_tables(position_ids, head_size):
    half_size = head_size // 2
    inverse = rope_base ** (-(jnp.arange(half_size, dtype=jnp.float32) * 2.0 / head_size))
    angles = position_ids.astype(jnp.float32)[:, None] * inverse[None, :]
    return (jnp.cos(angles), jnp.sin(angles))


def rotate_fwd(values, cosine, sine_part):
    half_size = values.shape[-1] // 2
    first_half = values[..., :half_size]
    second_half = values[..., half_size:]
    cos_rows = cosine[:, None, :]
    sin_rows = sine_part[:, None, :]
    return jnp.concatenate(
        [
            first_half * cos_rows - second_half * sin_rows,
            second_half * cos_rows + first_half * sin_rows,
        ],
        axis=-1,
    )


def rotate_back(grad_in, cosine, sine_part):
    half_size = grad_in.shape[-1] // 2
    first_half = grad_in[..., :half_size]
    second_half = grad_in[..., half_size:]
    cos_rows = cosine[:, None, :]
    sin_rows = sine_part[:, None, :]
    return jnp.concatenate(
        [
            first_half * cos_rows + second_half * sin_rows,
            second_half * cos_rows - first_half * sin_rows,
        ],
        axis=-1,
    )


def rms_parts(values):
    inverse = lax.rsqrt(jnp.mean(values * values, axis=-1, keepdims=True) + norm_eps)
    return (values * inverse, inverse)


def rms_back(grad_in, normed, inverse, gain_vec):
    scaled = grad_in * gain_vec
    return inverse * (scaled - normed * jnp.mean(scaled * normed, axis=-1, keepdims=True))


def block_scores(query_block, key_window, query_ids, doc_starts, key_ids):
    scale_factor = 1.0 / math.sqrt(query_block.shape[-1])
    scores = (
        jnp.einsum("rkgd,skd->kgrs", query_block, key_window, preferred_element_type=jnp.float32)
        * scale_factor
    )
    allowed = (key_ids[None, :] >= doc_starts[:, None]) & (key_ids[None, :] <= query_ids[:, None])
    return jnp.where(allowed[None, None], scores, masked_score)


def attend_fwd(query_block, key_window, value_window, query_ids, doc_starts, key_ids):
    scores = block_scores(query_block, key_window, query_ids, doc_starts, key_ids)
    row_max = jnp.max(scores, axis=-1, keepdims=True)
    weights = jnp.exp(scores - row_max)
    row_total = jnp.sum(weights, axis=-1, keepdims=True)
    probs_low = (weights / row_total).astype(jnp.bfloat16)
    log_total = (row_max + jnp.log(row_total))[..., 0]
    context = jnp.einsum(
        "kgrs,skd->rkgd", probs_low, value_window, preferred_element_type=jnp.float32
    )
    return (context.astype(jnp.bfloat16), log_total)


def attend_back(
    query_block,
    key_window,
    value_window,
    context,
    log_total,
    context_grad,
    query_ids,
    doc_starts,
    key_ids,
):
    scale_factor = 1.0 / math.sqrt(query_block.shape[-1])
    scores = block_scores(query_block, key_window, query_ids, doc_starts, key_ids)
    probs = jnp.exp(scores - log_total[..., None])
    probs_low = probs.astype(jnp.bfloat16)
    prob_grad = jnp.einsum(
        "rkgd,skd->kgrs", context_grad, value_window, preferred_element_type=jnp.float32
    )
    row_delta = jnp.transpose(
        jnp.sum(context_grad.astype(jnp.float32) * context.astype(jnp.float32), axis=-1), (1, 2, 0)
    )
    score_low = (probs * (prob_grad - row_delta[..., None])).astype(jnp.bfloat16)
    query_grad = scale_factor * jnp.einsum(
        "kgrs,skd->rkgd", score_low, key_window, preferred_element_type=jnp.float32
    )
    key_grad = scale_factor * jnp.einsum(
        "kgrs,rkgd->skd", score_low, query_block, preferred_element_type=jnp.float32
    )
    value_grad = jnp.einsum(
        "kgrs,rkgd->skd", probs_low, context_grad, preferred_element_type=jnp.float32
    )
    return (query_grad, key_grad, value_grad)


def on_device(
    tokens,
    positions,
    attn_gain,
    w_query,
    w_key,
    w_value,
    w_out,
    ffn_gain,
    w_gate,
    w_up,
    w_down,
    out_grad,
):
    tp_count = lax.axis_size("tp")
    span_rows = tokens.shape[0] * tp_count
    head_size = HD
    query_heads = w_query.shape[1] // head_size
    kv_heads = w_key.shape[1] // head_size
    group_size = query_heads // kv_heads
    kv_width = kv_heads * head_size
    block_rows = min(512, span_rows)
    block_count = span_rows // block_rows
    span_begin = lax.axis_index("dp") * span_rows
    full_weights = (
        lax.all_gather(w_query, "dp", axis=0, tiled=True),
        lax.all_gather(w_key, "dp", axis=0, tiled=True),
        lax.all_gather(w_value, "dp", axis=0, tiled=True),
        lax.all_gather(w_out, "dp", axis=1, tiled=True),
        lax.all_gather(w_gate, "dp", axis=0, tiled=True),
        lax.all_gather(w_up, "dp", axis=0, tiled=True),
        lax.all_gather(w_down, "dp", axis=1, tiled=True),
    )
    query_full, key_full, value_full, out_full, gate_full, up_full, down_full = full_weights
    tokens_f = tokens.astype(jnp.float32)
    normed1, inverse1 = rms_parts(tokens_f)
    hidden1 = lax.all_gather((normed1 * attn_gain).astype(jnp.bfloat16), "tp", axis=0, tiled=True)
    queries = jnp.dot(hidden1, query_full, preferred_element_type=jnp.float32)
    keys_raw = jnp.dot(hidden1, key_full, preferred_element_type=jnp.float32)
    values_raw = jnp.dot(hidden1, value_full, preferred_element_type=jnp.float32)
    cosine, sine_part = rope_tables(positions, head_size)
    query_rot = (
        rotate_fwd(queries.reshape(span_rows, query_heads, head_size), cosine, sine_part)
        .astype(jnp.bfloat16)
        .reshape(span_rows, kv_heads, group_size, head_size)
    )
    key_rot = (
        rotate_fwd(keys_raw.reshape(span_rows, kv_heads, head_size), cosine, sine_part)
        .astype(jnp.bfloat16)
        .reshape(span_rows, kv_width)
    )
    value_low = values_raw.astype(jnp.bfloat16)
    kv_pieces = [jnp.concatenate([key_rot, value_low], axis=1)]
    for hop_index in range(2):
        kv_pieces.append(passed_along(kv_pieces[-1], "dp", 1))
    kv_window = jnp.concatenate([kv_pieces[2], kv_pieces[1], kv_pieces[0]], axis=0)
    key_window = kv_window[:, :kv_width].reshape(3 * span_rows, kv_heads, head_size)
    value_window = kv_window[:, kv_width:].reshape(3 * span_rows, kv_heads, head_size)
    key_ids = span_begin - 2 * span_rows + jnp.arange(3 * span_rows, dtype=jnp.int32)
    doc_begin = span_begin + jnp.arange(span_rows, dtype=jnp.int32) - positions

    def block_inputs(block_index):
        row_start = block_index * block_rows
        query_block = lax.dynamic_slice_in_dim(query_rot, row_start, block_rows, 0)
        query_ids = span_begin + row_start + jnp.arange(block_rows, dtype=jnp.int32)
        doc_starts = lax.dynamic_slice_in_dim(doc_begin, row_start, block_rows, 0)
        return (row_start, query_block, query_ids, doc_starts)

    def forward_block(block_index):
        row_start, query_block, query_ids, doc_starts = block_inputs(block_index)
        return attend_fwd(query_block, key_window, value_window, query_ids, doc_starts, key_ids)

    contexts, log_totals = lax.map(forward_block, jnp.arange(block_count, dtype=jnp.int32))
    context = contexts.reshape(span_rows, query_heads * head_size)
    attn_out = lax.psum_scatter(
        jnp.dot(context, out_full, preferred_element_type=jnp.float32),
        "tp",
        scatter_dimension=0,
        tiled=True,
    )
    residual = tokens_f + attn_out
    normed2, inverse2 = rms_parts(residual)
    hidden2 = lax.all_gather((normed2 * ffn_gain).astype(jnp.bfloat16), "tp", axis=0, tiled=True)
    gate_pre = jnp.dot(hidden2, gate_full, preferred_element_type=jnp.float32)
    up_proj = jnp.dot(hidden2, up_full, preferred_element_type=jnp.float32)
    sigmoid_gate = jax.nn.sigmoid(gate_pre)
    inner_act = (gate_pre * sigmoid_gate * up_proj).astype(jnp.bfloat16)
    ffn_out = lax.psum_scatter(
        jnp.dot(inner_act, down_full, preferred_element_type=jnp.float32).astype(jnp.bfloat16),
        "tp",
        scatter_dimension=0,
        tiled=True,
    ).astype(jnp.float32)
    output = (residual + ffn_out).astype(jnp.bfloat16)
    query_back, key_back, value_back, out_back, gate_back, up_back, down_back = (
        lax.all_gather(w_query, "dp", axis=0, tiled=True),
        lax.all_gather(w_key, "dp", axis=0, tiled=True),
        lax.all_gather(w_value, "dp", axis=0, tiled=True),
        lax.all_gather(w_out, "dp", axis=1, tiled=True),
        lax.all_gather(w_gate, "dp", axis=0, tiled=True),
        lax.all_gather(w_up, "dp", axis=0, tiled=True),
        lax.all_gather(w_down, "dp", axis=1, tiled=True),
    )
    grad_rows = lax.all_gather(out_grad, "tp", axis=0, tiled=True)
    inner_grad = jnp.dot(grad_rows, down_back.T, preferred_element_type=jnp.float32)
    w_down_grad = jnp.dot(inner_act.T, grad_rows, preferred_element_type=jnp.float32)
    silu_slope = sigmoid_gate * (1.0 + gate_pre * (1.0 - sigmoid_gate))
    gate_low = (inner_grad * up_proj * silu_slope).astype(jnp.bfloat16)
    up_low = (inner_grad * gate_pre * sigmoid_gate).astype(jnp.bfloat16)
    w_gate_grad = jnp.dot(hidden2.T, gate_low, preferred_element_type=jnp.float32)
    w_up_grad = jnp.dot(hidden2.T, up_low, preferred_element_type=jnp.float32)
    hidden2_part = jnp.dot(gate_low, gate_back.T, preferred_element_type=jnp.float32) + jnp.dot(
        up_low, up_back.T, preferred_element_type=jnp.float32
    )
    hidden2_grad = lax.psum_scatter(hidden2_part, "tp", scatter_dimension=0, tiled=True)
    ffn_gain_part = jnp.sum(hidden2_grad * normed2, axis=0)
    residual_grad = out_grad.astype(jnp.float32) + rms_back(
        hidden2_grad, normed2, inverse2, ffn_gain
    )
    residual_rows = lax.all_gather(residual_grad.astype(jnp.bfloat16), "tp", axis=0, tiled=True)
    w_out_grad = jnp.dot(context.T, residual_rows, preferred_element_type=jnp.float32)
    context_grad = (
        jnp.dot(residual_rows, out_back.T, preferred_element_type=jnp.float32)
        .astype(jnp.bfloat16)
        .reshape(span_rows, kv_heads, group_size, head_size)
    )
    context_heads = contexts.reshape(span_rows, kv_heads, group_size, head_size)

    def backward_block(carry, block_index):
        key_acc, value_acc = carry
        row_start, query_block, query_ids, doc_starts = block_inputs(block_index)
        context_block = lax.dynamic_slice_in_dim(context_heads, row_start, block_rows, 0)
        grad_block = lax.dynamic_slice_in_dim(context_grad, row_start, block_rows, 0)
        query_grad, key_grad, value_grad = attend_back(
            query_block,
            key_window,
            value_window,
            context_block,
            log_totals[block_index],
            grad_block,
            query_ids,
            doc_starts,
            key_ids,
        )
        return ((key_acc + key_grad, value_acc + value_grad), query_grad)

    zero_acc = jnp.zeros((3 * span_rows, kv_heads, head_size), jnp.float32)
    (key_acc, value_acc), query_grads = lax.scan(
        backward_block, (zero_acc, zero_acc), jnp.arange(block_count, dtype=jnp.int32)
    )
    kv_grads = jnp.concatenate(
        [key_acc.reshape(3 * span_rows, kv_width), value_acc.reshape(3 * span_rows, kv_width)],
        axis=1,
    )
    carried = kv_grads[:span_rows]
    for hop_index in range(2):
        carried = passed_along(carried, "dp", -1)
        if hop_index == 0:
            carried = carried + kv_grads[span_rows : 2 * span_rows]
    kv_total = kv_grads[2 * span_rows :] + carried
    key_low = (
        rotate_back(
            kv_total[:, :kv_width].reshape(span_rows, kv_heads, head_size), cosine, sine_part
        )
        .astype(jnp.bfloat16)
        .reshape(span_rows, kv_width)
    )
    value_grad_low = kv_total[:, kv_width:].astype(jnp.bfloat16)
    query_low = (
        rotate_back(query_grads.reshape(span_rows, query_heads, head_size), cosine, sine_part)
        .astype(jnp.bfloat16)
        .reshape(span_rows, query_heads * head_size)
    )
    w_query_grad = jnp.dot(hidden1.T, query_low, preferred_element_type=jnp.float32)
    w_key_grad = jnp.dot(hidden1.T, key_low, preferred_element_type=jnp.float32)
    w_value_grad = jnp.dot(hidden1.T, value_grad_low, preferred_element_type=jnp.float32)
    hidden1_part = (
        jnp.dot(query_low, query_back.T, preferred_element_type=jnp.float32)
        + jnp.dot(key_low, key_back.T, preferred_element_type=jnp.float32)
        + jnp.dot(value_grad_low, value_back.T, preferred_element_type=jnp.float32)
    )
    hidden1_grad = lax.psum_scatter(hidden1_part, "tp", scatter_dimension=0, tiled=True)
    attn_gain_part = jnp.sum(hidden1_grad * normed1, axis=0)
    tokens_grad = residual_grad + rms_back(hidden1_grad, normed1, inverse1, attn_gain)
    weight_sums = (
        lax.psum_scatter(w_query_grad, "dp", scatter_dimension=0, tiled=True),
        lax.psum_scatter(w_key_grad, "dp", scatter_dimension=0, tiled=True),
        lax.psum_scatter(w_value_grad, "dp", scatter_dimension=0, tiled=True),
        lax.psum_scatter(w_out_grad, "dp", scatter_dimension=1, tiled=True),
        lax.psum_scatter(w_gate_grad, "dp", scatter_dimension=0, tiled=True),
        lax.psum_scatter(w_up_grad, "dp", scatter_dimension=0, tiled=True),
        lax.psum_scatter(w_down_grad, "dp", scatter_dimension=1, tiled=True),
    )
    gain_sums = lax.psum((attn_gain_part, ffn_gain_part), ("dp", "tp"))
    return (
        output,
        tokens_grad,
        gain_sums[0],
        weight_sums[0],
        weight_sums[1],
        weight_sums[2],
        weight_sums[3],
        gain_sums[1],
        weight_sums[4],
        weight_sums[5],
        weight_sums[6],
    )


def solution(mesh):
    return jax.shard_map(
        on_device,
        mesh=mesh,
        in_specs=(
            P(("dp", "tp"), None),
            P("dp"),
            P(),
            P("dp", "tp"),
            P("dp", "tp"),
            P("dp", "tp"),
            P("tp", "dp"),
            P(),
            P("dp", "tp"),
            P("dp", "tp"),
            P("tp", "dp"),
            P(("dp", "tp"), None),
        ),
        out_specs=(
            P(("dp", "tp"), None),
            P(("dp", "tp"), None),
            P(),
            P("dp", "tp"),
            P("dp", "tp"),
            P("dp", "tp"),
            P("tp", "dp"),
            P(),
            P("dp", "tp"),
            P("dp", "tp"),
            P("tp", "dp"),
        ),
        check_vma=False,
    )
```

profile of v0, /device:TPU:1, one launch (start us, length us, event | category | flops | bytes accessed | tf_op | source)
XLA Modules:
  0.0 987.4 jit_solution(4722919047417117280)
XLA Ops:
  13.2 12.1 %all_gather.41 = bf16[1536,192]{1,0:T(8,128)(2,1)S(1)} all-gather(bf16[192,192]{1,0:T(8,128)(2,1)} %param.16), channel_id=1, replica_groups=mesh['dp'=8,'tp'=4] {'dp'}, dimensions={0}, use_global_device_ids=true | all-gather | bytes 663552 | tf_op jit(solution)/shard_map/all_gather | solution.py:152
  25.3 10.0 %all_gather.42 = bf16[1536,192]{1,0:T(8,128)(2,1)S(1)} all-gather(bf16[192,192]{1,0:T(8,128)(2,1)S(1)} %copy-done.31), channel_id=1, replica_groups=mesh['dp'=8,'tp'=4] {'dp'}, dimensions={0}, use_global_device_ids=true | all-gather | bytes 663552 | tf_op jit(solution)/shard_map/all_gather | solution.py:153
  35.7 13.5 %all-gather.10.cloned.1.call-done = bf16[512,1536]{1,0:T(8,128)(2,1)} async-done(((bf16[128,1536]{1,0:T(8,128)(2,1)}), bf16[512,1536]{1,0:T(8,128)(2,1)}) %all-gather.10.cloned.1.call-update) | async-done | bytes 1572880 | tf_op jit(solution)/shard_map/all_gather | solution.py:162
  68.3 9.3 all-gather.12.cloned.1.call-done
  91.4 12.3 %all-gather.14.cloned.1.call-done = bf16[384,1536]{0,1:T(8,128)(2,1)} async-done(((bf16[384,192]{0,1:T(8,128)(2,1)}), bf16[384,1536]{0,1:T(8,128)(2,1)}) %all-gather.14.cloned.1.call-update) | async-done | bytes 1179664 | tf_op jit(solution)/shard_map/all_gather | solution.py:154
  108.4 59.0 %reduce-scatter.12.cloned.1.call-done = f32[128,1536]{1,0:T(8,128)} async-done(((f32[512,1536]{1,0:T(8,128)}), f32[128,1536]{1,0:T(8,128)}) %reduce-scatter.12.cloned.1.call-update) | async-done | bytes 786448 | tf_op jit(solution)/shard_map/reduce_scatter | solution.py:200
  171.9 30.1 %all-gather.20.cloned.1.call-done = bf16[1536,1024]{1,0:T(8,128)(2,1)} async-done(((bf16[192,1024]{1,0:T(8,128)(2,1)}), bf16[1536,1024]{1,0:T(8,128)(2,1)}) %all-gather.20.cloned.1.call-update) | async-done | bytes 3145744 | tf_op jit(solution)/shard_map/all_gather | solution.py:156
  202.1 37.8 %all-gather.16.cloned.1.call-done = bf16[512,1536]{1,0:T(8,128)(2,1)} async-done(((bf16[128,1536]{1,0:T(8,128)(2,1)}), bf16[512,1536]{1,0:T(8,128)(2,1)}) %all-gather.16.cloned.1.call-update) | async-done | bytes 1572880 | tf_op jit(solution)/shard_map/all_gather | solution.py:208
  239.8 5.5 fusion.36
  245.4 28.7 %all-gather.18.cloned.1.call-done = bf16[1536,1024]{1,0:T(8,128)(2,1)} async-done(((bf16[192,1024]{1,0:T(8,128)(2,1)}), bf16[1536,1024]{1,0:T(8,128)(2,1)}) %all-gather.18.cloned.1.call-update) | async-done | bytes 3145744 | tf_op jit(solution)/shard_map/all_gather | solution.py:155
  274.1 5.5 fusion.35
  279.6 31.8 %all-gather.24.cloned.1.call-done = bf16[512,1536]{1,0:T(8,128)(2,1)} async-done(((bf16[128,1536]{1,0:T(8,128)(2,1)}), bf16[512,1536]{1,0:T(8,128)(2,1)}) %all-gather.24.cloned.1.call-update) | async-done | bytes 1572880 | tf_op jit(solution)/shard_map/all_gather | solution.py:229
  311.4 34.3 %all-gather.22.cloned.1.call-done = bf16[1024,1536]{0,1:T(8,128)(2,1)} async-done(((bf16[1024,192]{0,1:T(8,128)(2,1)}), bf16[1024,1536]{0,1:T(8,128)(2,1)}) %all-gather.22.cloned.1.call-update) | async-done | bytes 3145744 | tf_op jit(solution)/shard_map/all_gather | solution.py:157
  345.7 7.2 multiply_convert_fusion
  359.1 59.7 %reduce-scatter.16.cloned.1.call-done = f32[128,1536]{1,0:T(8,128)} async-done(((f32[512,1536]{1,0:T(8,128)}), f32[128,1536]{1,0:T(8,128)}) %reduce-scatter.16.cloned.1.call-update) | async-done | bytes 786448 | tf_op jit(solution)/shard_map/reduce_scatter | solution.py:240
  424.7 35.6 %all-gather.26.cloned.1.call-done = bf16[512,1536]{1,0:T(8,128)(2,1)} async-done(((bf16[128,1536]{1,0:T(8,128)(2,1)}), bf16[512,1536]{1,0:T(8,128)(2,1)}) %all-gather.26.cloned.1.call-update) | async-done | bytes 1572880 | tf_op jit(solution)/shard_map/all_gather | solution.py:245
  463.0 6.8 fusion.4
  469.9 6.0 fusion.1
  481.7 10.7 %collective-permute-done.2 = f32[512,384]{0,1:T(8,128)S(1)} collective-permute-done((f32[512,384]{0,1:T(8,128)S(1)}, f32[512,384]{0,1:T(8,128)S(1)}, u32[]{:S(2)}, u32[]{:S(2)}) %collective-permute-start.2) | collective-permute-done | bytes 786464 | tf_op jit(solution)/shard_map/ppermute | solution.py:19
  498.2 7.8 collective-permute-done.3
  515.0 6.5 fusion.44
  521.6 6.3 fusion.43
  528.0 6.1 fusion.42
  545.6 23.4 %reduce-scatter.18.cloned.1.call-done = f32[128,1536]{1,0:T(8,128)} async-done(((f32[512,1536]{1,0:T(8,128)}), f32[128,1536]{1,0:T(8,128)}) %reduce-scatter.18.cloned.1.call-update) | async-done | bytes 786448 | tf_op jit(solution)/shard_map/reduce_scatter | solution.py:307
  570.4 42.9 %all-reduce = (f32[1536]{0:T(1024)}, f32[1536]{0:T(1024)}) all-reduce(f32[1536]{0:T(1024)S(1)} %get-tuple-element.66, f32[1536]{0:T(1024)S(1)} %copy-done.35), channel_id=1, replica_groups=mesh['dp'=8,'tp'=4] {'dp','tp'}, use_global_device_ids=true, to_apply=%region_12.13 | all-reduce | flops 3072 | bytes 24576 | tf_op jit(solution)/shard_map/psum | solution.py:319
  615.9 56.5 %reduce-scatter.32.cloned.1.call-done = f32[1024,192]{0,1:T(8,128)} async-done(((f32[1024,1536]{0,1:T(8,128)}), f32[1024,192]{0,1:T(8,128)}) %reduce-scatter.32.cloned.1.call-update) | async-done | bytes 786448 | tf_op jit(solution)/shard_map/reduce_scatter | solution.py:317
  672.3 65.6 %reduce-scatter.30.cloned.1.call-done = f32[192,1024]{1,0:T(8,128)} async-done(((f32[1536,1024]{1,0:T(8,128)}), f32[192,1024]{1,0:T(8,128)}) %reduce-scatter.30.cloned.1.call-update) | async-done | bytes 786448 | tf_op jit(solution)/shard_map/reduce_scatter | solution.py:316
  737.9 65.6 %reduce-scatter.28.cloned.1.call-done = f32[192,1024]{1,0:T(8,128)} async-done(((f32[1536,1024]{1,0:T(8,128)}), f32[192,1024]{1,0:T(8,128)}) %reduce-scatter.28.cloned.1.call-update) | async-done | bytes 786448 | tf_op jit(solution)/shard_map/reduce_scatter | solution.py:315
  803.5 42.0 %reduce-scatter.22.cloned.1.call-done = f32[192,192]{1,0:T(8,128)} async-done(((f32[1536,192]{1,0:T(8,128)}), f32[192,192]{1,0:T(8,128)}) %reduce-scatter.22.cloned.1.call-update) | async-done | bytes 147472 | tf_op jit(solution)/shard_map/reduce_scatter | solution.py:312
  845.5 42.1 %reduce-scatter.24.cloned.1.call-done = f32[192,192]{1,0:T(8,128)} async-done(((f32[1536,192]{1,0:T(8,128)}), f32[192,192]{1,0:T(8,128)}) %reduce-scatter.24.cloned.1.call-update) | async-done | bytes 147472 | tf_op jit(solution)/shard_map/reduce_scatter | solution.py:313
  887.6 46.3 %reduce-scatter.26.cloned.1.call-done = f32[384,192]{0,1:T(8,128)} async-done(((f32[384,1536]{0,1:T(8,128)}), f32[384,192]{0,1:T(8,128)}) %reduce-scatter.26.cloned.1.call-update) | async-done | bytes 294928 | tf_op jit(solution)/shard_map/reduce_scatter | solution.py:314
  934.0 46.1 %reduce-scatter.20.cloned.1.call-done = f32[192,384]{1,0:T(8,128)} async-done(((f32[1536,384]{1,0:T(8,128)}), f32[192,384]{1,0:T(8,128)}) %reduce-scatter.20.cloned.1.call-update) | async-done | bytes 294928 | tf_op jit(solution)/shard_map/reduce_scatter | solution.py:311
  (192 shorter events, 98.8 us)
Async XLA Ops:
  7.2 42.1 %all-gather.10.cloned.1.call-start = ((), (), s32[]{:S(2)}) async-start(), calls=%async_computation.11 | async-start | bytes 1966080 | tf_op jit(solution)/shard_map/all_gather | solution.py:162
  10.9 66.7 %all-gather.12.cloned.1.call-start = ((), (), s32[]{:S(2)}) async-start(), calls=%async_computation.12 | async-start | bytes 1327104 | tf_op jit(solution)/shard_map/all_gather | solution.py:151
  11.6 92.0 %all-gather.14.cloned.1.call-start = ((), (), s32[]{:S(2)}) async-start(), calls=%async_computation.13 | async-start | bytes 1327104 | tf_op jit(solution)/shard_map/all_gather | solution.py:154
  12.4 155.0 %reduce-scatter.12.cloned.1.call-start = ((), (), s32[]{:S(2)}) async-start(), calls=%async_computation.14 | async-start | bytes 3932160 | tf_op jit(solution)/shard_map/reduce_scatter | solution.py:200
  35.7 44.0 %copy-start.13 = (f32[512,48]{0,1:T(8,128)}, f32[512,48]{0,1:T(8,128)S(1)}, u32[]{:S(2)}) copy-start(f32[512,48]{0,1:T(8,128)S(1)} %get-tuple-element.100) | copy-start | bytes 294916
  53.0 10.8 %collective-permute-start = (bf16[512,384]{0,1:T(8,128)(2,1)S(1)}, bf16[512,384]{0,1:T(8,128)(2,1)}, u32[]{:S(2)}, u32[]{:S(2)}) collective-permute-start(bf16[512,384]{0,1:T(8,128)(2,1)S(1)} %pad_maximum_fusion.1), channel_id=1, source_target_pairs={{0,4},{4,8},{8,12},{12,16},{16,20},{20,24},{24,28},{1,5},{5,9},{9,... | collective-permute-start | bytes 1179656 | tf_op jit(solution)/shard_map/ppermute | solution.py:19
  63.8 16.1 %collective-permute-start.1 = (bf16[512,384]{0,1:T(8,128)(2,1)}, bf16[512,384]{0,1:T(8,128)(2,1)}, u32[]{:S(2)}, u32[]{:S(2)}) collective-permute-start(bf16[512,384]{0,1:T(8,128)(2,1)} %collective-permute-done), channel_id=1, source_target_pairs={{0,4},{4,8},{8,12},{12,16},{16,20},{20,24},{24,28},{1,5},{5,9},{9,... | collective-permute-start | bytes 1179656 | tf_op jit(solution)/shard_map/ppermute | solution.py:19
  107.6 59.8 %copy-start.2 = (bf16[128,1536]{1,0:T(8,128)(2,1)S(1)}, bf16[128,1536]{1,0:T(8,128)(2,1)}, u32[]{:S(2)}) copy-start(bf16[128,1536]{1,0:T(8,128)(2,1)} %param.12) | copy-start | bytes 1179652
  107.6 61.1 %copy-start.30 = (f32[1536]{0:T(1024)S(1)}, f32[1536]{0:T(1024)}, u32[]{:S(2)}) copy-start(f32[1536]{0:T(1024)} %param.19) | copy-start | bytes 18436
  107.6 94.4 %all-gather.20.cloned.1.call-start = ((), (), s32[]{:S(2)}) async-start(), calls=%async_computation.17 | async-start | bytes 3538944 | tf_op jit(solution)/shard_map/all_gather | solution.py:156
  108.2 131.6 %all-gather.16.cloned.1.call-start = ((), (), s32[]{:S(2)}) async-start(), calls=%async_computation.15 | async-start | bytes 1966080 | tf_op jit(solution)/shard_map/all_gather | solution.py:208
  168.7 252.1 %copy-start.36 = (f32[128]{0:T(128)}, f32[128]{0:T(128)S(1)}, u32[]{:S(2)}) copy-start(f32[128]{0:T(128)S(1)} %add_rsqrt_fusion) | copy-start | bytes 1540
  169.7 104.4 %all-gather.18.cloned.1.call-start = ((), (), s32[]{:S(2)}) async-start(), calls=%async_computation.16 | async-start | bytes 3538944 | tf_op jit(solution)/shard_map/all_gather | solution.py:155
  170.4 141.0 %all-gather.24.cloned.1.call-start = ((), (), s32[]{:S(2)}) async-start(), calls=%async_computation.20 | async-start | bytes 1966080 | tf_op jit(solution)/shard_map/all_gather | solution.py:229
  171.2 174.5 %all-gather.22.cloned.1.call-start = ((), (), s32[]{:S(2)}) async-start(), calls=%async_computation.18 | async-start | bytes 3538944 | tf_op jit(solution)/shard_map/all_gather | solution.py:157
  171.9 246.9 %reduce-scatter.16.cloned.1.call-start = ((), (), s32[]{:S(2)}) async-start(), calls=%async_computation.21 | async-start | bytes 3932160 | tf_op jit(solution)/shard_map/reduce_scatter | solution.py:240
  359.1 101.2 %all-gather.26.cloned.1.call-start = ((), (), s32[]{:S(2)}) async-start(), calls=%async_computation.22 | async-start | bytes 1966080 | tf_op jit(solution)/shard_map/all_gather | solution.py:245
  423.7 145.3 %reduce-scatter.18.cloned.1.call-start = ((), (), s32[]{:S(2)}) async-start(), calls=%async_computation.23 | async-start | bytes 3932160 | tf_op jit(solution)/shard_map/reduce_scatter | solution.py:307
  478.0 14.3 %collective-permute-start.2 = (f32[512,384]{0,1:T(8,128)S(1)}, f32[512,384]{0,1:T(8,128)S(1)}, u32[]{:S(2)}, u32[]{:S(2)}) collective-permute-start(f32[512,384]{0,1:T(8,128)S(1)} %fusion.21), channel_id=1, source_target_pairs={{4,0},{8,4},{12,8},{16,12},{20,16},{24,20},{28,24},{5,1},{9,5},{13... | collective-permute-start | bytes 2359304 | tf_op jit(solution)/shard_map/ppermute | solution.py:19
  492.5 13.4 %collective-permute-start.3 = (f32[512,384]{0,1:T(8,128)S(1)}, f32[512,384]{0,1:T(8,128)S(1)}, u32[]{:S(2)}, u32[]{:S(2)}) collective-permute-start(f32[512,384]{0,1:T(8,128)S(1)} %fusion.24), channel_id=1, source_target_pairs={{4,0},{8,4},{12,8},{16,12},{20,16},{24,20},{28,24},{5,1},{9,5},{13... | collective-permute-start | bytes 2359304 | tf_op jit(solution)/shard_map/ppermute | solution.py:19
  509.4 103.8 %reduce-scatter.14.cloned.1.call-start = ((), (), s32[]{:S(2)}) async-start(), calls=%async_computation.19 | async-start | bytes 1966080 | tf_op jit(solution)/shard_map/reduce_scatter | solution.py:213
  514.7 157.6 %reduce-scatter.32.cloned.1.call-start = ((), (), s32[]{:S(2)}) async-start(), calls=%async_computation.30 | async-start | bytes 7077888 | tf_op jit(solution)/shard_map/reduce_scatter | solution.py:317
  521.6 216.3 %reduce-scatter.30.cloned.1.call-start = ((), (), s32[]{:S(2)}) async-start(), calls=%async_computation.29 | async-start | bytes 7077888 | tf_op jit(solution)/shard_map/reduce_scatter | solution.py:316
  527.9 275.6 %reduce-scatter.28.cloned.1.call-start = ((), (), s32[]{:S(2)}) async-start(), calls=%async_computation.28 | async-start | bytes 7077888 | tf_op jit(solution)/shard_map/reduce_scatter | solution.py:315
  534.1 311.4 %reduce-scatter.22.cloned.1.call-start = ((), (), s32[]{:S(2)}) async-start(), calls=%async_computation.25 | async-start | bytes 1769472 | tf_op jit(solution)/shard_map/reduce_scatter | solution.py:312
  537.0 350.6 %reduce-scatter.24.cloned.1.call-start = ((), (), s32[]{:S(2)}) async-start(), calls=%async_computation.26 | async-start | bytes 1769472 | tf_op jit(solution)/shard_map/reduce_scatter | solution.py:313
  538.8 395.1 %reduce-scatter.26.cloned.1.call-start = ((), (), s32[]{:S(2)}) async-start(), calls=%async_computation.27 | async-start | bytes 2654208 | tf_op jit(solution)/shard_map/reduce_scatter | solution.py:314
  542.9 437.2 %reduce-scatter.20.cloned.1.call-start = ((), (), s32[]{:S(2)}) async-start(), calls=%async_computation.24 | async-start | bytes 2654208 | tf_op jit(solution)/shard_map/reduce_scatter | solution.py:311
  545.5 67.7 %copy-start.5 = (f32[128,1536]{1,0:T(8,128)S(1)}, f32[128,1536]{1,0:T(8,128)}, u32[]{:S(2)}) copy-start(f32[128,1536]{1,0:T(8,128)} %reduce-scatter.16.cloned.1.call-done) | copy-start | bytes 2359300
  545.5 67.7 %copy-start.10 = (bf16[128,1536]{1,0:T(8,128)(2,1)S(1)}, bf16[128,1536]{1,0:T(8,128)(2,1)}, u32[]{:S(2)}) copy-start(bf16[128,1536]{1,0:T(8,128)(2,1)} %param.23) | copy-start | bytes 1179652
  545.5 67.7 %copy-start.37 = (f32[128]{0:T(128)S(1)}, f32[128]{0:T(128)}, u32[]{:S(2)}) copy-start(f32[128]{0:T(128)} %copy-done.36) | copy-start | bytes 1540
  545.5 67.7 %copy-start.41 = (f32[128]{0:T(128)S(1)}, f32[128]{0:T(128)}, u32[]{:S(2)}) copy-start(f32[128]{0:T(128)} %copy-done.40) | copy-start | bytes 1540
  (38 other events, 308.7 us)
Sparse Core Ops, SparseCore 0:
  11.0 38.1 all-gather.9
  51.1 26.4 all-gather.11
  79.5 24.1 all-gather.13
  107.8 59.6 reduce-scatter.11
  169.1 32.8 all-gather.19
  204.0 35.7 all-gather.15
  241.7 32.3 all-gather.17
  275.6 35.7 all-gather.23
  313.3 32.3 all-gather.21
  359.2 59.5 reduce-scatter.15
  423.8 36.4 all-gather.25
  509.6 59.3 reduce-scatter.17
  571.2 36.3 reduce-scatter.13
  611.5 60.8 reduce-scatter.31
  676.1 61.7 reduce-scatter.29
  741.7 61.7 reduce-scatter.27
  807.2 38.2 reduce-scatter.21
  849.2 38.3 reduce-scatter.23
  891.5 42.3 reduce-scatter.25
  937.7 42.3 reduce-scatter.19
where the time goes:
time: 997 us; the launch traced here: 987 us
  waiting for transfers between devices  767 us (77%)
  matrix products  95.3 us (10%)
  blocking collectives  64.9 us (7%)
  other arithmetic  21.3 us (2%)
  starting transfers between devices  16.1 us (2%)
  between operations  15.5 us (2%)
    reduce_scatter x1, waiting for transfers between devices, on_device(): lax.psum_scatter(w_gate_grad, 'dp', scatter_dimension=0, tiled=True)  65.6 us
    reduce_scatter x1, waiting for transfers between devices, on_device(): lax.psum_scatter(w_up_grad, 'dp', scatter_dimension=0, tiled=True)  65.6 us
    reduce_scatter x1, waiting for transfers between devices, on_device(): lax.psum_scatter(hidden2_part, 'tp', scatter_dimension=0, tiled=True)  59.7 us
    reduce_scatter x1, waiting for transfers between devices, on_device(): lax.psum_scatter(jnp.dot(context, out_full, preferred_element_type=jnp.fl...  59 us
    reduce_scatter x1, waiting for transfers between devices, on_device(): lax.psum_scatter(w_down_grad, 'dp', scatter_dimension=1, tiled=True)  56.5 us
    reduce_scatter x1, waiting for transfers between devices, on_device(): lax.psum_scatter(w_out_grad, 'dp', scatter_dimension=1, tiled=True)  46.3 us
    reduce_scatter x1, waiting for transfers between devices, on_device(): lax.psum_scatter(w_query_grad, 'dp', scatter_dimension=0, tiled=True)  46.1 us
    psum x1, blocking collectives, on_device(): gain_sums = lax.psum((attn_gain_part, ffn_gain_part), ('dp', 'tp'))  42.9 us
  transfers between devices with their start and end apart: 24, of which 22 were waited for; matrix products, arithmetic and copies ran while one was open for 7% of the time, Pallas kernels for 0%

commit v1 on v0

v1 whole, which is shorter than its diff:
```python
import functools
import math

import jax
import jax.numpy as jnp
from jax import lax
from jax.experimental import pallas as pl
from jax.experimental.pallas import tpu as pltpu
from jax.sharding import PartitionSpec as P

HD = 96
norm_eps = 1e-05
rope_base = 100000.0
masked_score = -1e30

MESH = pl.DeviceIdType.MESH
VMEM = pltpu.VMEM
DMA = pltpu.SemaphoreType.DMA
LEVELS = 32000.0


class Stage:
    def __init__(self, name, cid, nd, nt):
        self.name, self.cid, self.nd, self.nt = name, cid, nd, nt
        self.ins, self.outs, self.scr, self.tasks, self.links = [], [], [], [], set()

    def inp(self, x, space=VMEM):
        self.ins.append((x, space))
        return ("i", len(self.ins) - 1)

    def out(self, shape, dtype, space=VMEM):
        self.outs.append((shape, dtype, space))
        return ("o", len(self.outs) - 1)

    def scratch(self, spec):
        self.scr.append(spec)
        return ("s", len(self.scr) - 1)

    def task(self, links, gen):
        self.links |= set(links)
        self.tasks.append(gen)

    def _barrier(self):
        d, t = lax.axis_index("dp"), lax.axis_index("tp")
        nd, nt = self.nd, self.nt
        sem = pltpu.get_barrier_semaphore()
        count = 0

        def greet(ok, where):
            if ok is True:
                pl.semaphore_signal(sem, inc=1, device_id=where, device_id_type=MESH)
                return 1

            @pl.when(ok)
            def _():
                pl.semaphore_signal(sem, inc=1, device_id=where, device_id_type=MESH)

            return ok.astype(jnp.int32)

        if "line" in self.links:
            count += greet(t > 0, {"tp": t - 1})
            count += greet(t < nt - 1, {"tp": t + 1})
        if "chips" in self.links:
            for i in range(1, nd // 2):
                count += greet(True, {"dp": lax.rem(d + 2 * i, nd)})
        if "twin" in self.links:
            count += greet(True, {"dp": d + 1 - 2 * lax.rem(d, 2)})
        if "near" in self.links:
            for i in (1, 2):
                count += greet(d >= i, {"dp": d - i})
                count += greet(d < nd - i, {"dp": d + i})
        if "tp" in self.links:
            for i in range(1, nt):
                count += greet(True, {"tp": lax.rem(t + i, nt)})
        if "dp" in self.links:
            for i in range(1, nd):
                count += greet(True, {"dp": lax.rem(d + i, nd)})
        pl.semaphore_wait(sem, count)

    def run(self):
        n_in, n_out = len(self.ins), len(self.outs)

        def kernel(*refs):
            def get(h):
                kind, i = h
                return refs[i + {"i": 0, "o": n_in, "s": n_in + n_out}[kind]]

            self._barrier()
            live = [g(get) for g in self.tasks]
            while live:
                still = []
                for g in live:
                    try:
                        next(g)
                        still.append(g)
                    except StopIteration:
                        pass
                live = still

        return pl.pallas_call(
            kernel,
            out_shape=[jax.ShapeDtypeStruct(s, t) for s, t, _ in self.outs],
            in_specs=[pl.BlockSpec(memory_space=sp) for _, sp in self.ins],
            out_specs=[pl.BlockSpec(memory_space=sp) for _, _, sp in self.outs],
            scratch_shapes=self.scr,
            compiler_params=pltpu.CompilerParams(
                collective_id=self.cid, has_side_effects=True, vmem_limit_bytes=48 << 20
            ),
            name=self.name,
        )(*[x for x, _ in self.ins])


def remote(src, dst, send, recv, where):
    return pltpu.make_async_remote_copy(
        src_ref=src, dst_ref=dst, send_sem=send, recv_sem=recv, device_id=where, device_id_type=MESH
    )


def when(ok, fn):
    if ok is True:
        fn()
    elif ok is not False:
        pl.when(ok)(fn)


def over_cols(width, fn):
    def body(c, _):
        fn(pl.ds(pl.multiple_of(c * 128, 128), 128))
        return 0

    lax.fori_loop(0, width // 128, body, 0)
    if width % 128:
        fn(pl.ds(width // 128 * 128, width % 128))


def row_encode(read, code, scale, rows):
    step = 16

    def body(i, held):
        r = pl.multiple_of(i * step, step)
        x = read(r, step)
        top = jnp.max(jnp.abs(x), axis=-1, keepdims=True)
        code[pl.ds(r, step), :] = jnp.round(x * (LEVELS / jnp.maximum(top, 1e-30))).astype(jnp.int32).astype(jnp.int16)
        lane = lax.broadcasted_iota(jnp.int32, (step, 128), 1)
        row = lax.broadcasted_iota(jnp.int32, (step, 128), 0) + r
        mine = jnp.sum(jnp.where(lane == row, jnp.maximum(top, 1e-30) * (1.0 / LEVELS), 0.0), axis=0, keepdims=True)
        return held + jnp.broadcast_to(mine, (8, 128))

    scale[...] = lax.fori_loop(0, rows // step, body, jnp.zeros((8, 128), jnp.float32))


def row_decode(code, scale, r, step):
    lane = lax.broadcasted_iota(jnp.int32, (step, 128), 1)
    row = lax.broadcasted_iota(jnp.int32, (step, 128), 0) + r
    col = jnp.sum(jnp.where(lane == row, jnp.broadcast_to(scale[0:1, :], (step, 128)), 0.0), axis=-1, keepdims=True)
    return code[pl.ds(r, step), :].astype(jnp.int32).astype(jnp.float32) * col


def col_encode(x, code, scale, cols):
    top = jnp.maximum(jnp.max(jnp.abs(x), axis=0, keepdims=True), 1e-30)
    code[:, cols] = jnp.round(x * (LEVELS / top)).astype(jnp.int32).astype(jnp.int16)
    scale[:, cols] = top * (1.0 / LEVELS)


def col_decode(code, scale, cols):
    return code[:, cols].astype(jnp.int32).astype(jnp.float32) * scale[:, cols]


def line_gather(st, x):
    nt = st.nt
    rows, width = x.shape
    hx = st.inp(x)
    ho = st.out((nt, rows, width), x.dtype, pl.ANY)
    parts = 2
    hs = st.scratch(DMA((2, nt, parts)))
    hr = st.scratch(DMA((2, nt, parts)))
    hl = st.scratch(DMA((1,)))

    def gen(get):
        x_ref, o_ref, ss, rs, ls = get(hx), get(ho), get(hs), get(hr), get(hl)
        t = lax.axis_index("tp")
        chunk = rows // parts
        own = pltpu.make_async_copy(x_ref, o_ref.at[t], ls.at[0])
        own.start()

        def hop(src, owner, k, s, p, where):
            piece = pl.ds(p * chunk, chunk)
            return remote(src.at[piece], o_ref.at[owner, piece], ss.at[k, s, p], rs.at[k, s, p], {"tp": where})

        def send(s, p, k, way):
            owner, where = t - s * way, t + way
            ok = (owner >= 0) & (owner < nt) & (where >= 0) & (where < nt)
            src = x_ref if s == 0 else o_ref.at[owner]
            when(ok, lambda: hop(src, owner, k, s, p, where).start())

        for p in range(parts):
            for k, way in enumerate((1, -1)):
                send(0, p, k, way)
        yield
        for s in range(nt - 1):
            for p in range(parts):
                for k, way in enumerate((1, -1)):
                    owner = t - way * (s + 1)
                    ok = (owner >= 0) & (owner < nt)
                    when(ok, lambda: hop(x_ref, owner, k, s, p, t).wait_recv())
                    if s < nt - 2:
                        send(s + 1, p, k, way)
                yield
        for s in range(nt - 1):
            for p in range(parts):
                for k, way in enumerate((1, -1)):
                    owner, where = t - s * way, t + way
                    ok = (owner >= 0) & (owner < nt) & (where >= 0) & (where < nt)
                    when(ok, lambda: hop(x_ref, owner, k, s, p, where).wait_send())
        own.wait()

    st.task(("line",), gen)
    return ho


def line_scatter(st, part):
    nt = st.nt
    total, width = part.shape
    rows = total // nt
    parts = 2
    chunk = rows // parts
    hx = st.inp(part)
    ho = st.out((rows, width), jnp.float32)
    hcs = st.scratch(VMEM((2, nt - 1, parts, chunk, width), jnp.int16))
    hcr = st.scratch(VMEM((2, nt - 1, parts, chunk, width), jnp.int16))
    hss = st.scratch(VMEM((2, nt - 1, parts, 8, 128), jnp.float32))
    hsr = st.scratch(VMEM((2, nt - 1, parts, 8, 128), jnp.float32))
    hs = st.scratch(DMA((2, nt - 1, parts, 2)))
    hr = st.scratch(DMA((2, nt - 1, parts, 2)))

    def gen(get):
        x_ref, o_ref, cs, cr, sc, sr, ss, rs = (get(h) for h in (hx, ho, hcs, hcr, hss, hsr, hs, hr))
        t = lax.axis_index("tp")

        def hops(k, s, p, where):
            return (
                remote(cs.at[k, s, p], cr.at[k, s, p], ss.at[k, s, p, 0], rs.at[k, s, p, 0], {"tp": where}),
                remote(sc.at[k, s, p], sr.at[k, s, p], ss.at[k, s, p, 1], rs.at[k, s, p, 1], {"tp": where}),
            )

        def mine(base, r, n):
            return x_ref[pl.ds(pl.multiple_of(base + r, n), n), :]

        for s in range(nt - 1):
            for p in range(parts):
                for k, way in enumerate((1, -1)):
                    j = nt - 1 - s if way == 1 else s
                    base = j * rows + p * chunk
                    first = t == (0 if way == 1 else nt - 1)
                    passing = (t < j) if way == 1 else (t > j)

                    def send():
                        for c in hops(k, s, p, t + way):
                            c.start()

                    def start():
                        row_encode(lambda r, n: mine(base, r, n), cs.at[k, s, p], sc.at[k, s, p], chunk)
                        send()

                    def relay():
                        for c in hops(k, s, p, t):
                            c.wait_recv()
                        row_encode(
                            lambda r, n: mine(base, r, n) + row_decode(cr.at[k, s, p], sr.at[k, s, p], r, n),
                            cs.at[k, s, p],
                            sc.at[k, s, p],
                            chunk,
                        )
                        send()

                    when(first, start)
                    when(passing & jnp.logical_not(first), relay)
                yield
        base = t * rows
        for p in range(parts):
            for k, way in enumerate((1, -1)):
                for s in range(nt - 1):
                    j = nt - 1 - s if way == 1 else s
                    ok = (t == j) & (t > 0 if way == 1 else t < nt - 1)

                    def arrive():
                        for c in hops(k, s, p, t):
                            c.wait_recv()

                    when(ok, arrive)
            s_right, s_left = nt - 1 - t, t

            def total_of(i, _):
                r = pl.multiple_of(i * 16, 16)
                x = mine(base + p * chunk, r, 16)
                o_ref[pl.ds(p * chunk + r, 16), :] = x
                return 0

            lax.fori_loop(0, chunk // 16, total_of, 0)
            for k, way in enumerate((1, -1)):
                at = s_right if way == 1 else s_left

                def add():
                    def body(i, _):
                        r = pl.multiple_of(i * 16, 16)
                        o_ref[pl.ds(p * chunk + r, 16), :] += row_decode(cr.at[k, at, p], sr.at[k, at, p], r, 16)
                        return 0

                    lax.fori_loop(0, chunk // 16, body, 0)

                when(t > 0 if way == 1 else t < nt - 1, add)
            yield
        for s in range(nt - 1):
            for p in range(parts):
                for k, way in enumerate((1, -1)):
                    j = nt - 1 - s if way == 1 else s
                    passing = (t < j) if way == 1 else (t > j)

                    def drain():
                        for c in hops(k, s, p, t + way):
                            c.wait_send()

                    when(passing, drain)

    st.task(("line",), gen)
    return ho


def chip_gather(st, w):
    nd = st.nd
    nc = nd // 2
    hx = st.inp(w)
    ho = st.out((nd,) + w.shape, w.dtype, pl.ANY)
    hs = st.scratch(DMA((nd,)))
    hr = st.scratch(DMA((nd,)))
    hl = st.scratch(DMA((1,)))

    def gen(get):
        x_ref, o_ref, ss, rs, ls = get(hx), get(ho), get(hs), get(hr), get(hl)
        d = lax.axis_index("dp")
        twin = d + 1 - 2 * lax.rem(d, 2)
        own = pltpu.make_async_copy(x_ref, o_ref.at[d], ls.at[0])
        own.start()
        out, fwd = [], []
        for i in range(1, nc):
            out.append(remote(x_ref, o_ref.at[d], ss.at[i], rs.at[i], {"dp": lax.rem(d + 2 * i, nd)}))
            out[-1].start()
        fwd.append(remote(x_ref, o_ref.at[d], ss.at[0], rs.at[0], {"dp": twin}))
        fwd[-1].start()
        yield
        for i in range(1, nc):
            out[i - 1].wait_recv()
            src = lax.rem(d - 2 * i + nd, nd)
            fwd.append(remote(o_ref.at[src], o_ref.at[src], ss.at[nc + i], rs.at[nc + i], {"dp": twin}))
            fwd[-1].start()
            yield
        for c in fwd:
            c.wait()
        for c in out:
            c.wait_send()
        own.wait()

    st.task(("chips", "twin"), gen)
    return ho


def chip_scatter(st, g):
    nd = st.nd
    nc = nd // 2
    _, rows, width = g.shape
    hx = st.inp(g, pl.ANY)
    ho = st.out((rows, width), jnp.float32)
    hm = st.scratch(VMEM((nc, rows, width), jnp.float32))
    ht = st.scratch(VMEM((nc, rows, width), jnp.float32))
    hcs = st.scratch(VMEM((nc - 1, rows, width), jnp.int16))
    hcr = st.scratch(VMEM((nc - 1, rows, width), jnp.int16))
    hss = st.scratch(VMEM((nc - 1, 1, width), jnp.float32))
    hsr = st.scratch(VMEM((nc - 1, 1, width), jnp.float32))
    hl = st.scratch(DMA((nc,)))
    hts = st.scratch(DMA((2, nc)))
    hs = st.scratch(DMA((nc - 1, 2)))
    hr = st.scratch(DMA((nc - 1, 2)))

    def gen(get):
        x_ref, o_ref, m, tw, cs, cr, sc, sr, ls, ts, ss, rs = (
            get(h) for h in (hx, ho, hm, ht, hcs, hcr, hss, hsr, hl, hts, hs, hr)
        )
        d = lax.axis_index("dp")
        core = lax.rem(d, 2)
        chip = d // 2
        twin = d + 1 - 2 * core
        loads, give = [], []
        for i in range(nc):
            g_i = lax.rem(chip + 1 + i, nc)
            loads.append(pltpu.make_async_copy(x_ref.at[2 * g_i + core], m.at[i], ls.at[i]))
            loads[-1].start()
            give.append(remote(x_ref.at[2 * g_i + 1 - core], tw.at[i], ts.at[0, i], ts.at[1, i], {"dp": twin}))
            give[-1].start()
        yield
        sends = []
        for i in range(nc - 1):
            loads[i].wait()
            give[i].wait_recv()

            def body(cols):
                col_encode(m[i, :, cols] + tw[i, :, cols], cs.at[i], sc.at[i], cols)

            over_cols(width, body)
            where = {"dp": lax.rem(d + 2 * (i + 1), nd)}
            pair = (
                remote(cs.at[i], cr.at[i], ss.at[i, 0], rs.at[i, 0], where),
                remote(sc.at[i], sr.at[i], ss.at[i, 1], rs.at[i, 1], where),
            )
            for c in pair:
                c.start()
            sends.append(pair)
            yield
        loads[nc - 1].wait()
        give[nc - 1].wait_recv()
        for i in range(nc - 1):
            for c in sends[i]:
                c.wait_recv()

        def total(cols):
            x = m[nc - 1, :, cols] + tw[nc - 1, :, cols]
            for i in range(nc - 1):
                x = x + col_decode(cr.at[i], sr.at[i], cols)
            o_ref[:, cols] = x

        over_cols(width, total)
        for i in range(nc - 1):
            for c in sends[i]:
                c.wait_send()
        for c in give:
            c.wait_send()

    st.task(("chips", "twin"), gen)
    return ho


def window_gather(st, kv):
    nd = st.nd
    hx = st.inp(kv)
    ho = st.out((3,) + kv.shape, kv.dtype, pl.ANY)
    hz = st.scratch(VMEM(kv.shape, kv.dtype))
    hs = st.scratch(DMA((2,)))
    hr = st.scratch(DMA((2,)))
    hl = st.scratch(DMA((3,)))

    def gen(get):
        x_ref, o_ref, z, ss, rs, ls = (get(h) for h in (hx, ho, hz, hs, hr, hl))
        d = lax.axis_index("dp")
        own = pltpu.make_async_copy(x_ref, o_ref.at[2], ls.at[2])
        own.start()

        def ahead(i):
            return remote(x_ref, o_ref.at[2 - i], ss.at[i - 1], rs.at[i - 1], {"dp": d + i})

        for i in (2, 1):
            when(d + i < nd, lambda: ahead(i).start())
        z[...] = jnp.zeros_like(z)
        for i in (1, 2):
            blank = pltpu.make_async_copy(z, o_ref.at[2 - i], ls.at[2 - i])
            when(d < i, lambda: blank.start())
        yield
        for i in (1, 2):
            blank = pltpu.make_async_copy(z, o_ref.at[2 - i], ls.at[2 - i])
            when(d < i, lambda: blank.wait())
            when(d >= i, lambda: ahead(i).wait_recv())
        for i in (1, 2):
            when(d + i < nd, lambda: ahead(i).wait_send())
        own.wait()

    st.task(("near",), gen)
    return ho


def window_scatter(st, g):
    nd = st.nd
    _, rows, width = g.shape
    hx = st.inp(g)
    ho = st.out((rows, width), jnp.float32)
    hcs = st.scratch(VMEM((2, rows, width), jnp.int16))
    hcr = st.scratch(VMEM((2, rows, width), jnp.int16))
    hss = st.scratch(VMEM((2, 1, width), jnp.float32))
    hsr = st.scratch(VMEM((2, 1, width), jnp.float32))
    hs = st.scratch(DMA((2, 2)))
    hr = st.scratch(DMA((2, 2)))

    def gen(get):
        x_ref, o_ref, cs, cr, sc, sr, ss, rs = (get(h) for h in (hx, ho, hcs, hcr, hss, hsr, hs, hr))
        d = lax.axis_index("dp")

        def back(i):
            where = {"dp": d - i}
            return (
                remote(cs.at[i - 1], cr.at[i - 1], ss.at[i - 1, 0], rs.at[i - 1, 0], where),
                remote(sc.at[i - 1], sr.at[i - 1], ss.at[i - 1, 1], rs.at[i - 1, 1], where),
            )

        for i in (2, 1):

            def send():
                def body(cols):
                    col_encode(x_ref[2 - i, :, cols], cs.at[i - 1], sc.at[i - 1], cols)

                over_cols(width, body)
                for c in back(i):
                    c.start()

            when(d >= i, send)
        yield
        o_ref[...] = x_ref[2]
        for i in (1, 2):

            def take():
                for c in back(i):
                    c.wait_recv()

                def body(cols):
                    o_ref[:, cols] += col_decode(cr.at[i - 1], sr.at[i - 1], cols)

                over_cols(width, body)

            when(d + i < nd, take)
            yield
        for i in (1, 2):

            def drain():
                for c in back(i):
                    c.wait_send()

            when(d >= i, drain)

    st.task(("near",), gen)
    return ho


def full_sum(st, x):
    nd, nt = st.nd, st.nt
    hx = st.inp(x)
    ho = st.out(x.shape, jnp.float32)
    ha = st.scratch(VMEM((nt,) + x.shape, jnp.float32))
    hm = st.scratch(VMEM(x.shape, jnp.float32))
    hb = st.scratch(VMEM((nd,) + x.shape, jnp.float32))
    hs = st.scratch(DMA((2, max(nd, nt))))
    hr = st.scratch(DMA((2, max(nd, nt))))

    def gen(get):
        x_ref, o_ref, a, m, b, ss, rs = (get(h) for h in (hx, ho, ha, hm, hb, hs, hr))
        for k, (axis, n, src, got, dst) in enumerate((("tp", nt, x_ref, a, m), ("dp", nd, m, b, o_ref))):
            me = lax.axis_index(axis)
            cs = [
                remote(src, got.at[me], ss.at[k, i], rs.at[k, i], {axis: lax.rem(me + i, n)})
                for i in range(1, n)
            ]
            for c in cs:
                c.start()
            got[me] = src[...]
            yield
            for c in cs:
                c.wait()
            total = got[0]
            for i in range(1, n):
                total = total + got[i]
            dst[...] = total

    st.task(("tp", "dp"), gen)
    return ho


def rope_tables(position_ids, head_size):
    half_size = head_size // 2
    inverse = rope_base ** (-(jnp.arange(half_size, dtype=jnp.float32) * 2.0 / head_size))
    angles = position_ids.astype(jnp.float32)[:, None] * inverse[None, :]
    return (jnp.cos(angles), jnp.sin(angles))


def rotate_fwd(values, cosine, sine_part):
    half_size = values.shape[-1] // 2
    first_half = values[..., :half_size]
    second_half = values[..., half_size:]
    cos_rows = cosine[:, None, :]
    sin_rows = sine_part[:, None, :]
    return jnp.concatenate(
        [
            first_half * cos_rows - second_half * sin_rows,
            second_half * cos_rows + first_half * sin_rows,
        ],
        axis=-1,
    )


def rms_parts(values):
    inverse = lax.rsqrt(jnp.mean(values * values, axis=-1, keepdims=True) + norm_eps)
    return (values * inverse, inverse)


def rms_back(grad_in, normed, inverse, gain_vec):
    scaled = grad_in * gain_vec
    return inverse * (scaled - normed * jnp.mean(scaled * normed, axis=-1, keepdims=True))


def block_scores(query_block, key_window, query_ids, doc_starts, key_ids):
    scale_factor = 1.0 / math.sqrt(query_block.shape[-1])
    scores = (
        jnp.einsum("rkgd,skd->kgrs", query_block, key_window, preferred_element_type=jnp.float32)
        * scale_factor
    )
    allowed = (key_ids[None, :] >= doc_starts[:, None]) & (key_ids[None, :] <= query_ids[:, None])
    return jnp.where(allowed[None, None], scores, masked_score)


def attend_fwd(query_block, key_window, value_window, query_ids, doc_starts, key_ids):
    scores = block_scores(query_block, key_window, query_ids, doc_starts, key_ids)
    row_max = jnp.max(scores, axis=-1, keepdims=True)
    weights = jnp.exp(scores - row_max)
    row_total = jnp.sum(weights, axis=-1, keepdims=True)
    probs_low = (weights / row_total).astype(jnp.bfloat16)
    log_total = (row_max + jnp.log(row_total))[..., 0]
    context = jnp.einsum("kgrs,skd->rkgd", probs_low, value_window, preferred_element_type=jnp.float32)
    return (context.astype(jnp.bfloat16), log_total)


def attend_back(
    query_block, key_window, value_window, context, log_total, context_grad, query_ids, doc_starts, key_ids
):
    scale_factor = 1.0 / math.sqrt(query_block.shape[-1])
    scores = block_scores(query_block, key_window, query_ids, doc_starts, key_ids)
    probs = jnp.exp(scores - log_total[..., None])
    probs_low = probs.astype(jnp.bfloat16)
    prob_grad = jnp.einsum("rkgd,skd->kgrs", context_grad, value_window, preferred_element_type=jnp.float32)
    row_delta = jnp.transpose(
        jnp.sum(context_grad.astype(jnp.float32) * context.astype(jnp.float32), axis=-1), (1, 2, 0)
    )
    score_low = (probs * (prob_grad - row_delta[..., None])).astype(jnp.bfloat16)
    query_grad = scale_factor * jnp.einsum(
        "kgrs,skd->rkgd", score_low, key_window, preferred_element_type=jnp.float32
    )
    key_grad = scale_factor * jnp.einsum(
        "kgrs,rkgd->skd", score_low, query_block, preferred_element_type=jnp.float32
    )
    value_grad = jnp.einsum("kgrs,rkgd->skd", probs_low, context_grad, preferred_element_type=jnp.float32)
    return (query_grad, key_grad, value_grad)


def dot(a, b):
    return jnp.dot(a, b, preferred_element_type=jnp.float32)


def on_device(
    nd, nt, tokens, positions, attn_gain, w_query, w_key, w_value, w_out, ffn_gain, w_gate, w_up, w_down, out_grad
):
    own_rows, width = tokens.shape
    span_rows = own_rows * nt
    query_heads = w_query.shape[1] // HD
    kv_heads = w_key.shape[1] // HD
    group_size = query_heads // kv_heads
    kv_width = kv_heads * HD
    q_width = query_heads * HD
    units = w_gate.shape[1]
    shard = w_query.shape[0]
    span_begin = lax.axis_index("dp") * span_rows
    low = jnp.bfloat16

    def stage(name, cid):
        return Stage(name, cid, nd, nt)

    def full(w):
        return w.reshape(nd * shard, w.shape[-1])

    def rows_of(x):
        return x.reshape(span_rows, x.shape[-1])

    def blocks(g):
        return g.reshape(nd, shard, g.shape[-1])

    tokens_f = tokens.astype(jnp.float32)
    normed1, inverse1 = rms_parts(tokens_f)
    w_attn = jnp.concatenate([w_query, w_key, w_value, w_out.T], axis=1)
    w_down_t = w_down.T

    st = stage("stage1", 1)
    line_gather(st, (normed1 * attn_gain).astype(low))
    chip_gather(st, w_attn)
    hidden1, attn_full = st.run()
    hidden1, attn_full = rows_of(hidden1), full(attn_full)
    qkv_full = attn_full[:, : q_width + 2 * kv_width]
    out_full_t = attn_full[:, q_width + 2 * kv_width :]

    qkv = dot(hidden1, qkv_full)
    cosine, sine_part = rope_tables(positions, HD)
    query_rot = (
        rotate_fwd(qkv[:, :q_width].reshape(span_rows, query_heads, HD), cosine, sine_part)
        .astype(low)
        .reshape(span_rows, kv_heads, group_size, HD)
    )
    key_rot = (
        rotate_fwd(qkv[:, q_width : q_width + kv_width].reshape(span_rows, kv_heads, HD), cosine, sine_part)
        .astype(low)
        .reshape(span_rows, kv_width)
    )
    value_low = qkv[:, q_width + kv_width :].astype(low)

    st = stage("stage2", 2)
    window_gather(st, jnp.concatenate([key_rot, value_low], axis=1))
    (kv_window,) = st.run()
    kv_window = kv_window.reshape(3 * span_rows, 2 * kv_width)
    key_window = kv_window[:, :kv_width].reshape(3 * span_rows, kv_heads, HD)
    value_window = kv_window[:, kv_width:].reshape(3 * span_rows, kv_heads, HD)
    key_ids = span_begin - 2 * span_rows + jnp.arange(3 * span_rows, dtype=jnp.int32)
    query_ids = span_begin + jnp.arange(span_rows, dtype=jnp.int32)
    doc_begin = query_ids - positions

    context4, log_total = attend_fwd(query_rot, key_window, value_window, query_ids, doc_begin, key_ids)
    context = context4.reshape(span_rows, q_width)
    attn_part = lax.dot_general(context, out_full_t, (((1,), (1,)), ((), ())), preferred_element_type=jnp.float32)

    st = stage("stage3", 3)
    line_scatter(st, attn_part)
    line_gather(st, out_grad)
    chip_gather(st, w_gate)
    chip_gather(st, w_up)
    attn_out, grad_rows, gate_full, up_full = st.run()
    grad_rows, gate_full, up_full = rows_of(grad_rows), full(gate_full), full(up_full)

    residual = tokens_f + attn_out
    normed2, inverse2 = rms_parts(residual)

    st = stage("stage4", 4)
    line_gather(st, (normed2 * ffn_gain).astype(low))
    chip_gather(st, w_down_t)
    hidden2, down_full_t = st.run()
    hidden2, down_full_t = rows_of(hidden2), full(down_full_t)

    gate_pre = dot(hidden2, gate_full)
    up_proj = dot(hidden2, up_full)
    sigmoid_gate = jax.nn.sigmoid(gate_pre)
    inner_act = (gate_pre * sigmoid_gate * up_proj).astype(low)
    inner_grad = dot(grad_rows, down_full_t)
    silu_slope = sigmoid_gate * (1.0 + gate_pre * (1.0 - sigmoid_gate))
    gate_low = (inner_grad * up_proj * silu_slope).astype(low)
    up_low = (inner_grad * gate_pre * sigmoid_gate).astype(low)
    hidden2_part = dot(gate_low, gate_full.T) + dot(up_low, up_full.T)
    down_grad_t = dot(grad_rows.T, inner_act)

    st = stage("stage5", 5)
    line_scatter(st, hidden2_part)
    chip_scatter(st, blocks(down_grad_t))
    hidden2_grad, down_sum_t = st.run()

    ffn_gain_part = jnp.sum(hidden2_grad * normed2, axis=0)
    residual_grad = out_grad.astype(jnp.float32) + rms_back(hidden2_grad, normed2, inverse2, ffn_gain)
    ffn_part = dot(inner_act, down_full_t.T)
    gate_grad = dot(hidden2.T, gate_low)
    up_grad = dot(hidden2.T, up_low)

    st = stage("stage6", 6)
    line_scatter(st, ffn_part)
    line_gather(st, residual_grad.astype(low))
    chip_scatter(st, blocks(gate_grad))
    ffn_out, residual_rows, gate_sum = st.run()
    residual_rows = rows_of(residual_rows)
    output = (residual + ffn_out).astype(low)

    context_grad = dot(residual_rows, out_full_t).astype(low).reshape(span_rows, kv_heads, group_size, HD)
    query_grad, key_grad, value_grad = attend_back(
        query_rot, key_window, value_window, context4, log_total, context_grad, query_ids, doc_begin, key_ids
    )
    kv_grads = jnp.concatenate(
        [key_grad.reshape(3, span_rows, kv_width), value_grad.reshape(3, span_rows, kv_width)], axis=2
    )
    st = stage("stage7", 7)
    window_scatter(st, kv_grads)
    (kv_total,) = st.run()

    key_low = (
        rotate_fwd(kv_total[:, :kv_width].reshape(span_rows, kv_heads, HD), cosine, -sine_part)
        .astype(low)
        .reshape(span_rows, kv_width)
    )
    value_grad_low = kv_total[:, kv_width:].astype(low)
    query_low = (
        rotate_fwd(query_grad.reshape(span_rows, query_heads, HD), cosine, -sine_part)
        .astype(low)
        .reshape(span_rows, q_width)
    )
    qkv_low = jnp.concatenate([query_low, key_low, value_grad_low], axis=1)
    hidden1_part = dot(qkv_low, qkv_full.T)
    qkv_grad = dot(hidden1.T, qkv_low)
    out_grad_t = dot(residual_rows.T, context)
    attn_grad = jnp.concatenate([qkv_grad, out_grad_t], axis=1)

    st = stage("stage8", 8)
    line_scatter(st, hidden1_part)
    chip_scatter(st, blocks(up_grad))
    chip_scatter(st, blocks(attn_grad))
    hidden1_grad, up_sum, attn_sum = st.run()

    attn_gain_part = jnp.sum(hidden1_grad * normed1, axis=0)
    tokens_grad = residual_grad + rms_back(hidden1_grad, normed1, inverse1, attn_gain)
    gains = jnp.concatenate(
        [attn_gain_part[None], ffn_gain_part[None], jnp.zeros((6, width), jnp.float32)], axis=0
    )
    st = stage("stage9", 9)
    full_sum(st, gains)
    (gains,) = st.run()
    cuts = (q_width, q_width + kv_width, q_width + 2 * kv_width)
    return (
        output,
        tokens_grad,
        gains[0],
        attn_sum[:, : cuts[0]],
        attn_sum[:, cuts[0] : cuts[1]],
        attn_sum[:, cuts[1] : cuts[2]],
        attn_sum[:, cuts[2] :].T,
        gains[1],
        gate_sum,
        up_sum,
        down_sum_t.T,
    )


def solution(mesh):
    return jax.shard_map(
        functools.partial(on_device, mesh.shape["dp"], mesh.shape["tp"]),
        mesh=mesh,
        in_specs=(
            P(("dp", "tp"), None),
            P("dp"),
            P(),
            P("dp", "tp"),
            P("dp", "tp"),
            P("dp", "tp"),
            P("tp", "dp"),
            P(),
            P("dp", "tp"),
            P("dp", "tp"),
            P("tp", "dp"),
            P(("dp", "tp"), None),
        ),
        out_specs=(
            P(("dp", "tp"), None),
            P(("dp", "tp"), None),
            P(),
            P("dp", "tp"),
            P("dp", "tp"),
            P("dp", "tp"),
            P("tp", "dp"),
            P(),
            P("dp", "tp"),
            P("dp", "tp"),
            P("tp", "dp"),
        ),
        check_vma=False,
    )
```

time: 997 us -> 516 us (0.52)
  waiting for transfers between devices: 767 us -> 0 us
  Pallas kernels: 0 us -> 370 us
  blocking collectives: 64.9 us -> 0 us
  local copies, waits for them, and re-layouts: 7.17 us -> 46.6 us
  matrix products: 95.3 us -> 71.5 us
  starting transfers between devices: 16.1 us -> 0 us
  between operations: 15.5 us -> 2.01 us
    reduce_scatter x11 -> x0, waiting for transfers between devices: 506 us -> none  [the longest x1 65.6 us: on_device(): lax.psum_scatter(w_gate_grad, 'dp', scatter_dimension=0, tiled=True)]
    pallas_call x0 -> x9, Pallas kernels: none -> 370 us  [run(): pl.pallas_call(kernel, out_shape=[jax.ShapeDtypeStruct(s, t) for s, t, _...]
    all_gather x9 -> x0, waiting for transfers between devices: 233 us -> none  [the longest x1 37.8 us: on_device(): lax.all_gather((normed2 * ffn_gain).astype(jnp.bfloat16), 'tp', axis=0, t...]
    psum x1 -> x0, blocking collectives: 42.9 us -> none  [on_device(): gain_sums = lax.psum((attn_gain_part, ffn_gain_part), ('dp', 'tp'))]
    dot_general x21 -> x15, matrix products: 74.3 us -> 45.3 us  [the longest x14 41.2 us: dot(): return jnp.dot(a, b, preferred_element_type=jnp.float32)]
    ppermute x4 -> x0, waiting for transfers between devices: 23.2 us -> none  [passed_along(): return lax.ppermute(block, axis, route)]
    all_gather x2 -> x0, blocking collectives: 22.1 us -> none  [the longest x1 12.1 us: on_device(): lax.all_gather(w_key, 'dp', axis=0, tiled=True)]
    ppermute x4 -> x0, starting transfers between devices: 14.7 us -> none  [passed_along(): return lax.ppermute(block, axis, route)]
  transfers between devices with their start and end apart: 24 -> 0, of which waited for: 22 -> 0; matrix products, arithmetic and copies ran while one was open for 7% -> 0% of each run, Pallas kernels for 0% -> 0%
where the time goes in v1:
time: 516 us; the launch traced here: 506 us
  Pallas kernels  370 us (72%)
  matrix products  71.5 us (14%)
  local copies, waits for them, and re-layouts  46.6 us (9%)
  other arithmetic  16.3 us (3%)
    pallas_call x9, Pallas kernels, run(): pl.pallas_call(kernel, out_shape=[jax.ShapeDtypeStruct(s, t) for s, t, _...  370 us
    dot_general x14, matrix products, dot(): return jnp.dot(a, b, preferred_element_type=jnp.float32)  41.2 us
    unnamed x123, local copies, waits for them, and re-layouts  14.8 us

profile of v1, /device:TPU:1, one launch (start us, length us, event | category | flops | bytes accessed | tf_op | source)
XLA Modules:
  0.0 506.3 jit_solution(18154169169082946903)
XLA Ops:
  4.2 32.9 %stage1.1 = (bf16[4,128,1536]{2,1,0:T(8,128)(2,1)S(1)}, bf16[8,192,1152]{2,1,0:T(8,128)(2,1)S(1)}) custom-call(bf16[128,1536]{1,0:T(8,128)(2,1)S(1)} %fusion.31.refs_0_, bf16[192,1152]{1,0:T(8,128)(2,1)S(1)} %concatenate.39.refs_1_), custom_call_target="tpu_custom_call" | custom-call | tf_op jit(solution)/shard_map/stage1/pallas_call | solution.py:100
  42.2 15.4 %stage2.1 = bf16[3,512,384]{2,1,0:T(8,128)(2,1)S(1)} custom-call(bf16[512,384]{1,0:T(8,128)(2,1)S(1)} %pad_maximum_fusion.3.refs_0_), custom_call_target="tpu_custom_call" | custom-call | tf_op jit(solution)/shard_map/stage2/pallas_call | solution.py:100
  61.1 2.5 fusion.48
  65.5 2.8 copy-done.19
  68.4 2.5 fusion.17
  71.0 4.2 fusion.29.refs_0_
  75.2 65.4 %stage3.1 = (f32[128,1536]{1,0:T(8,128)S(1)}, bf16[4,128,1536]{2,1,0:T(8,128)(2,1)S(1)}, bf16[8,192,1024]{2,1,0:T(8,128)(2,1)}, bf16[8,192,1024]{2,1,0:T(8,128)(2,1)}) custom-call(f32[512,1536]{1,0:T(8,128)} %fusion.29.refs_0_, bf16[128,1536]{1,0:T(8,128)(2,1)S(1)} %copy-done, bf16[192,1024]{1,0:T(8,128)(2,1)S(1)} %copy-done.12, bf16[192,1024]{1,0:T(8,128)(2,1)S(1)} %copy-done.13), custom_call_target="tpu_custom_call" | custom-call | tf_op jit(solution)/shard_map/stage3/pallas_call | solution.py:100
  141.0 31.0 %stage4.1 = (bf16[4,128,1536]{2,1,0:T(8,128)(2,1)S(1)}, bf16[8,192,1024]{2,1,0:T(8,128)(2,1)S(1)}) custom-call(bf16[128,1536]{1,0:T(8,128)(2,1)S(1)} %multiply_convert_fusion.3.refs_0_, bf16[192,1024]{1,0:T(8,128)(2,1)S(1)} %bitcast.121), custom_call_target="tpu_custom_call" | custom-call | tf_op jit(solution)/shard_map/stage4/pallas_call | solution.py:100
  175.7 2.6 multiply_convert_fusion
  178.3 3.6 fusion.51.refs_0_
  183.7 3.5 convolution_add_fusion.refs_0_
  187.2 2.6 copy.44
  189.8 6.3 %fusion.26.refs_1_ = f32[8,192,1024]{2,1,0:T(8,128)} fusion(bf16[8,192,512]{2,1,0:T(8,128)(2,1)} %bitcast.144, bf16[512,1024]{1,0:T(8,128)(2,1)} %copy-done.59), kind=kOutput, calls=%fused_computation.42 | convolution fusion | flops 1610612736 | bytes 8912896 | tf_op jit(solution)/shard_map/dot_general | solution.py:648
  196.1 35.7 %stage5.1 = (f32[128,1536]{1,0:T(8,128)S(1)}, f32[192,1024]{1,0:T(8,128)S(1)}) custom-call(f32[512,1536]{1,0:T(8,128)S(1)} %copy-done.1, f32[8,192,1024]{2,1,0:T(8,128)} %fusion.26.refs_1_), custom_call_target="tpu_custom_call" | custom-call | tf_op jit(solution)/shard_map/stage5/pallas_call | solution.py:100
  235.7 6.1 %fusion.24.refs_2_ = f32[8,192,1024]{2,1,0:T(8,128)} fusion(bf16[8,192,512]{2,1,0:T(8,128)(2,1)} %bitcast.142, bf16[512,1024]{1,0:T(8,128)(2,1)} %copy-done.58), kind=kOutput, calls=%fused_computation.40 | convolution fusion | flops 1610612736 | bytes 8912896 | tf_op jit(solution)/shard_map/dot_general | solution.py:648
  241.8 67.5 %stage6.1 = (f32[128,1536]{1,0:T(8,128)S(1)}, bf16[4,128,1536]{2,1,0:T(8,128)(2,1)S(1)}, f32[192,1024]{1,0:T(8,128)S(1)}) custom-call(f32[512,1536]{1,0:T(8,128)} %fusion.51.refs_0_, bf16[128,1536]{1,0:T(8,128)(2,1)S(1)} %fusion.45.refs_1_, f32[8,192,1024]{2,1,0:T(8,128)} %fusion.24.refs_2_), custom_call_target="tpu_custom_call" | custom-call | tf_op jit(solution)/shard_map/stage6/pallas_call | solution.py:100
  311.1 2.7 convolution_convert_fusion
  313.8 7.7 %fusion.10 = f32[1536,2,96]{0,2,1:T(8,128)} fusion(bf16[512,2,2,96]{0,3,2,1:T(8,128)(2,1)S(1)} %bitcast.133, f32[2,2,512,1536]{2,3,1,0:T(8,128)} %copy-done.19, f32[2,2,512]{2,1,0:T(2,128)S(1)} %log_add_fusion), kind=kOutput, calls=%fused_computation.18 | convolution fusion | flops 610271232 | bytes 14163968 | tf_op jit(solution)/shard_map/kgrs,rkgd->skd/dot_general | solution.py:643
  321.6 2.9 reshape.290
  326.3 6.3 %fusion.1 = bf16[2,2,512,1536]{2,3,1,0:T(8,128)(2,1)S(1)} fusion(f32[2,2,512,1536]{2,3,1,0:T(8,128)} %copy-done.19, bf16[1536,2,96,1]{0,2,3,1:T(8,128)(2,1)} %bitcast.139, bf16[512,2,2,96]{0,3,2,1:T(8,128)(2,1)S(1)} %bitcast.135, f32[2,2,512]{2,1,0:T(2,128)S(1)} %bitcast.157, f32[2,2,512]{2,1,0:T(2,128)S(1)} %log_add_fusion), kind=kOutput, calls=%fused_computation.2 | convolution fusion | flops 616562688 | bytes 19873792 | tf_op jit(solution)/shard_map/rkgd,skd->kgrs/dot_general | solution.py:632
  332.7 2.7 copy-done.20
  335.3 3.1 fusion.9
  338.4 2.8 reshape.289
  341.2 2.6 copy.49
  345.7 31.2 %stage7.1 = f32[512,384]{1,0:T(8,128)S(1)} custom-call(f32[3,512,384]{2,1,0:T(8,128)S(1)} %pad_maximum_fusion.1.refs_0_), custom_call_target="tpu_custom_call" | custom-call | tf_op jit(solution)/shard_map/stage7/pallas_call | solution.py:100
  380.1 4.1 convolution_multiply_fusion
  384.4 3.2 fusion.13.refs_0_
  387.6 4.4 fusion.22.refs_1_
  394.7 3.5 pad_maximum_fusion
  398.2 8.0 %copy.53 = f32[1536,1152]{1,0:T(8,128)} copy(f32[1536,1152]{0,1:T(8,128)} %pad_maximum_fusion) | data formatting | bytes 14155776 | tf_op jit(solution)/shard_map/concatenate | solution.py:792
  408.2 47.0 %stage8.1 = (f32[128,1536]{1,0:T(8,128)S(1)}, f32[192,1024]{1,0:T(8,128)S(1)}, f32[192,1152]{1,0:T(8,128)S(1)}) custom-call(f32[512,1536]{1,0:T(8,128)S(1)} %copy-done.2, f32[8,192,1024]{2,1,0:T(8,128)} %fusion.22.refs_1_, f32[8,192,1152]{2,1,0:T(8,128)} %bitcast.130), custom_call_target="tpu_custom_call" | custom-call | tf_op jit(solution)/shard_map/stage8/pallas_call | solution.py:100
  457.2 43.8 %stage9.1 = f32[8,1536]{1,0:T(8,128)S(1)} custom-call(f32[8,1536]{1,0:T(8,128)S(1)} %maximum_maximum_fusion.refs_0_), custom_call_target="tpu_custom_call" | custom-call | tf_op jit(solution)/shard_map/stage9/pallas_call | solution.py:100
  (180 shorter events, 43.9 us)
Async XLA Ops:
  41.8 18.4 %copy-start.27 = (f32[512,48]{0,1:T(8,128)}, f32[512,48]{0,1:T(8,128)S(1)}, u32[]{:S(2)}) copy-start(f32[512,48]{0,1:T(8,128)S(1)} %get-tuple-element.72) | copy-start | bytes 294916
  58.3 7.2 %copy-start.29 = (bf16[1536,192]{0,1:T(8,128)(2,1)}, bf16[1536,192]{0,1:T(8,128)(2,1)S(1)}, u32[]{:S(2)}) copy-start(bf16[1536,192]{0,1:T(8,128)(2,1)S(1)} %copy.40) | copy-start | bytes 1769476
  58.6 5.1 %copy-start.30 = (bf16[1536,192]{0,1:T(8,128)(2,1)}, bf16[1536,192]{0,1:T(8,128)(2,1)S(1)}, u32[]{:S(2)}) copy-start(bf16[1536,192]{0,1:T(8,128)(2,1)S(1)} %copy.41) | copy-start | bytes 1769476
  63.7 4.6 copy-start.19
  63.7 4.7 copy-start.42
  70.9 69.6 %copy-start.25 = (bf16[2,96,2,512]{3,1,2,0:T(8,128)(2,1)}, bf16[2,96,2,512]{3,1,2,0:T(8,128)(2,1)S(1)}, u32[]{:S(2)}) copy-start(bf16[2,96,2,512]{3,1,2,0:T(8,128)(2,1)S(1)} %fusion.17) | copy-start | bytes 1179652
  75.1 65.4 %copy-start.23 = (bf16[128,1536]{1,0:T(8,128)(2,1)S(1)}, bf16[128,1536]{1,0:T(8,128)(2,1)}, u32[]{:S(2)}) copy-start(bf16[128,1536]{1,0:T(8,128)(2,1)} %param.12) | copy-start | bytes 1179652
  75.2 65.6 %copy-start.40 = (f32[1536]{0:T(1024)S(1)}, f32[1536]{0:T(1024)}, u32[]{:S(2)}) copy-start(f32[1536]{0:T(1024)} %param.19) | copy-start | bytes 18436
  75.2 65.8 %copy-start.14 = (bf16[1024,192]{0,1:T(8,128)(2,1)S(1)}, bf16[1024,192]{0,1:T(8,128)(2,1)}, u32[]{:S(2)}) copy-start(bf16[1024,192]{0,1:T(8,128)(2,1)} %param.22) | copy-start | bytes 1179652
  140.6 35.1 %copy-start.3 = (bf16[4,128,1536]{2,1,0:T(8,128)(2,1)}, bf16[4,128,1536]{2,1,0:T(8,128)(2,1)S(1)}, u32[]{:S(2)}) copy-start(bf16[4,128,1536]{2,1,0:T(8,128)(2,1)S(1)} %get-tuple-element.34) | copy-start | bytes 4718596
  140.6 31.4 %copy-start.55 = (bf16[8,192,1024]{2,1,0:T(8,128)(2,1)S(1)}, bf16[8,192,1024]{2,1,0:T(8,128)(2,1)}, u32[]{:S(2)}) copy-start(bf16[8,192,1024]{2,1,0:T(8,128)(2,1)} %get-tuple-element.31) | copy-start | bytes 9437188
  140.8 91.0 %copy-start.21 = (f32[128,1536]{1,0:T(8,128)}, f32[128,1536]{1,0:T(8,128)S(1)}, u32[]{:S(2)}) copy-start(f32[128,1536]{1,0:T(8,128)S(1)} %get-tuple-element.50) | copy-start | bytes 2359300
  140.8 91.9 %copy-start.47 = (f32[128]{0:T(128)}, f32[128]{0:T(128)S(1)}, u32[]{:S(2)}) copy-start(f32[128]{0:T(128)S(1)} %add_rsqrt_fusion) | copy-start | bytes 1540
  178.3 5.4 %copy-start.56 = (bf16[512,1024]{1,0:T(8,128)(2,1)}, bf16[512,1024]{1,0:T(8,128)(2,1)S(1)}, u32[]{:S(2)}) copy-start(bf16[512,1024]{1,0:T(8,128)(2,1)S(1)} %get-tuple-element.51) | copy-start | bytes 3145732
  189.8 6.3 %copy-start.1 = (f32[512,1536]{1,0:T(8,128)S(1)}, f32[512,1536]{1,0:T(8,128)}, u32[]{:S(2)}) copy-start(f32[512,1536]{1,0:T(8,128)} %convolution_add_fusion.refs_0_) | copy-start | bytes 9437188
  232.7 9.1 %copy-start.51 = (f32[128]{0:T(128)}, f32[128]{0:T(128)S(1)}, u32[]{:S(2)}) copy-start(f32[128]{0:T(128)S(1)} %broadcast_multiply_fusion.1) | copy-start | bytes 1540
  311.1 10.5 %copy-start.4 = (bf16[4,128,1536]{2,1,0:T(8,128)(2,1)}, bf16[4,128,1536]{2,1,0:T(8,128)(2,1)S(1)}, u32[]{:S(2)}) copy-start(bf16[4,128,1536]{2,1,0:T(8,128)(2,1)S(1)} %get-tuple-element.37) | copy-start | bytes 4718596
  321.6 4.6 copy-start.26
  326.3 9.0 %copy-start.36 = (bf16[512,4,48]{0,2,1:T(8,128)(2,1)S(1)}, bf16[512,4,48]{0,2,1:T(8,128)(2,1)}, u32[]{:S(2)}) copy-start(bf16[512,4,48]{0,2,1:T(8,128)(2,1)} %copy-done.35) | copy-start | bytes 589828
  326.3 9.0 %copy-start.38 = (bf16[512,4,48]{0,2,1:T(8,128)(2,1)S(1)}, bf16[512,4,48]{0,2,1:T(8,128)(2,1)}, u32[]{:S(2)}) copy-start(bf16[512,4,48]{0,2,1:T(8,128)(2,1)} %copy-done.37) | copy-start | bytes 589828
  345.7 34.3 %copy-start.28 = (f32[512,48]{0,1:T(8,128)S(1)}, f32[512,48]{0,1:T(8,128)}, u32[]{:S(2)}) copy-start(f32[512,48]{0,1:T(8,128)} %copy-done.27) | copy-start | bytes 294916
  345.7 34.3 %copy-start.34 = (f32[512,48]{0,1:T(8,128)S(1)}, f32[512,48]{0,1:T(8,128)}, u32[]{:S(2)}) copy-start(f32[512,48]{0,1:T(8,128)} %get-tuple-element.70) | copy-start | bytes 294916
  345.7 34.3 %copy-start.31 = (bf16[1536,192]{0,1:T(8,128)(2,1)S(1)}, bf16[1536,192]{0,1:T(8,128)(2,1)}, u32[]{:S(2)}) copy-start(bf16[1536,192]{0,1:T(8,128)(2,1)} %copy-done.30) | copy-start | bytes 1769476
  408.2 47.1 %copy-start.24 = (bf16[128,1536]{1,0:T(8,128)(2,1)S(1)}, bf16[128,1536]{1,0:T(8,128)(2,1)}, u32[]{:S(2)}) copy-start(bf16[128,1536]{1,0:T(8,128)(2,1)} %param.12) | copy-start | bytes 1179652
  408.2 47.1 %copy-start.41 = (f32[1536]{0:T(1024)S(1)}, f32[1536]{0:T(1024)}, u32[]{:S(2)}) copy-start(f32[1536]{0:T(1024)} %param.14) | copy-start | bytes 18436
  408.2 47.1 %copy-start.50 = (f32[128]{0:T(128)S(1)}, f32[128]{0:T(128)}, u32[]{:S(2)}) copy-start(f32[128]{0:T(128)} %copy-done.49) | copy-start | bytes 1540
  408.2 47.4 %copy-start.7 = (f32[128,1536]{1,0:T(8,128)S(1)}, f32[128,1536]{1,0:T(8,128)}, u32[]{:S(2)}) copy-start(f32[128,1536]{1,0:T(8,128)} %copy-done.6) | copy-start | bytes 2359300
  408.2 47.4 %copy-start.22 = (f32[128,1536]{1,0:T(8,128)S(1)}, f32[128,1536]{1,0:T(8,128)}, u32[]{:S(2)}) copy-start(f32[128,1536]{1,0:T(8,128)} %copy-done.21) | copy-start | bytes 2359300
  408.2 47.4 %copy-start.48 = (f32[128]{0:T(128)S(1)}, f32[128]{0:T(128)}, u32[]{:S(2)}) copy-start(f32[128]{0:T(128)} %copy-done.47) | copy-start | bytes 1540
  408.2 47.4 %copy-start.52 = (f32[128]{0:T(128)S(1)}, f32[128]{0:T(128)}, u32[]{:S(2)}) copy-start(f32[128]{0:T(128)} %copy-done.51) | copy-start | bytes 1540
  455.6 47.6 %copy-start.11 = (f32[192,1024]{1,0:T(8,128)S(1)}, f32[192,1024]{1,0:T(8,128)}, u32[]{:S(2)}) copy-start(f32[192,1024]{1,0:T(8,128)} %copy-done.10) | copy-start | bytes 2359300
  457.0 48.0 %copy-start.9 = (f32[192,1024]{1,0:T(8,128)S(1)}, f32[192,1024]{1,0:T(8,128)}, u32[]{:S(2)}) copy-start(f32[192,1024]{1,0:T(8,128)} %copy-done.8) | copy-start | bytes 2359300
  (28 other events, 75.8 us)

commit v2 on v0

v2 whole, which is shorter than its diff:
```python
import functools
import math

import jax
import jax.numpy as jnp
from jax import lax
from jax.experimental import pallas as pl
from jax.experimental.pallas import tpu as pltpu
from jax.sharding import PartitionSpec as P

HD = 96
norm_eps = 1e-05
rope_base = 100000.0
masked_score = -1e30

MESH = pl.DeviceIdType.MESH
VMEM = pltpu.VMEM
DMA = pltpu.SemaphoreType.DMA
LEVELS = 32000.0


class Stage:
    def __init__(self, name, cid, nd, nt):
        self.name, self.cid, self.nd, self.nt = name, cid, nd, nt
        self.ins, self.outs, self.scr, self.tasks, self.links = [], [], [], [], set()

    def inp(self, x, space=VMEM):
        self.ins.append((x, space))
        return ("i", len(self.ins) - 1)

    def out(self, shape, dtype, space=VMEM):
        self.outs.append((shape, dtype, space))
        return ("o", len(self.outs) - 1)

    def scratch(self, spec):
        self.scr.append(spec)
        return ("s", len(self.scr) - 1)

    def task(self, links, gen):
        self.links |= set(links)
        self.tasks.append(gen)

    def _barrier(self):
        d, t = lax.axis_index("dp"), lax.axis_index("tp")
        nd, nt = self.nd, self.nt
        sem = pltpu.get_barrier_semaphore()
        count = 0

        def greet(ok, where):
            if ok is True:
                pl.semaphore_signal(sem, inc=1, device_id=where, device_id_type=MESH)
                return 1

            @pl.when(ok)
            def _():
                pl.semaphore_signal(sem, inc=1, device_id=where, device_id_type=MESH)

            return ok.astype(jnp.int32)

        if "line" in self.links:
            count += greet(t > 0, {"tp": t - 1})
            count += greet(t < nt - 1, {"tp": t + 1})
        if "chips" in self.links:
            for i in range(1, nd // 2):
                count += greet(True, {"dp": lax.rem(d + 2 * i, nd)})
        if "twin" in self.links:
            count += greet(True, {"dp": d + 1 - 2 * lax.rem(d, 2)})
        if "near" in self.links:
            for i in (1, 2):
                count += greet(d >= i, {"dp": d - i})
                count += greet(d < nd - i, {"dp": d + i})
        if "tp" in self.links:
            for i in range(1, nt):
                count += greet(True, {"tp": lax.rem(t + i, nt)})
        if "dp" in self.links:
            for i in range(1, nd):
                count += greet(True, {"dp": lax.rem(d + i, nd)})
        pl.semaphore_wait(sem, count)

    def run(self):
        n_in, n_out = len(self.ins), len(self.outs)

        def kernel(*refs):
            def get(h):
                kind, i = h
                return refs[i + {"i": 0, "o": n_in, "s": n_in + n_out}[kind]]

            self._barrier()
            live = [g(get) for g in self.tasks]
            while live:
                still = []
                for g in live:
                    try:
                        next(g)
                        still.append(g)
                    except StopIteration:
                        pass
                live = still

        return pl.pallas_call(
            kernel,
            out_shape=[jax.ShapeDtypeStruct(s, t) for s, t, _ in self.outs],
            in_specs=[pl.BlockSpec(memory_space=sp) for _, sp in self.ins],
            out_specs=[pl.BlockSpec(memory_space=sp) for _, _, sp in self.outs],
            scratch_shapes=self.scr,
            compiler_params=pltpu.CompilerParams(
                collective_id=self.cid, has_side_effects=True, vmem_limit_bytes=63 << 20
            ),
            name=self.name,
        )(*[x for x, _ in self.ins])


def remote(src, dst, send, recv, where):
    return pltpu.make_async_remote_copy(
        src_ref=src, dst_ref=dst, send_sem=send, recv_sem=recv, device_id=where, device_id_type=MESH
    )


def when(ok, fn):
    if ok is True:
        fn()
    elif ok is not False:
        pl.when(ok)(fn)


def over_cols(width, fn):
    def body(c, _):
        fn(pl.ds(pl.multiple_of(c * 128, 128), 128))
        return 0

    lax.fori_loop(0, width // 128, body, 0)
    if width % 128:
        fn(pl.ds(width // 128 * 128, width % 128))


def row_encode(read, code, scale, rows):
    step = 16

    def body(i, held):
        r = pl.multiple_of(i * step, step)
        x = read(r, step)
        top = jnp.max(jnp.abs(x), axis=-1, keepdims=True)
        code[pl.ds(r, step), :] = jnp.round(x * (LEVELS / jnp.maximum(top, 1e-30))).astype(jnp.int32).astype(jnp.int16)
        lane = lax.broadcasted_iota(jnp.int32, (step, 128), 1)
        row = lax.broadcasted_iota(jnp.int32, (step, 128), 0) + r
        mine = jnp.sum(jnp.where(lane == row, jnp.maximum(top, 1e-30) * (1.0 / LEVELS), 0.0), axis=0, keepdims=True)
        return held + jnp.broadcast_to(mine, (8, 128))

    scale[...] = lax.fori_loop(0, rows // step, body, jnp.zeros((8, 128), jnp.float32))


def row_decode(code, scale, r, step):
    lane = lax.broadcasted_iota(jnp.int32, (step, 128), 1)
    row = lax.broadcasted_iota(jnp.int32, (step, 128), 0) + r
    col = jnp.sum(jnp.where(lane == row, jnp.broadcast_to(scale[0:1, :], (step, 128)), 0.0), axis=-1, keepdims=True)
    return code[pl.ds(r, step), :].astype(jnp.int32).astype(jnp.float32) * col


def col_encode(x, code, scale, cols):
    top = jnp.maximum(jnp.max(jnp.abs(x), axis=0, keepdims=True), 1e-30)
    code[:, cols] = jnp.round(x * (LEVELS / top)).astype(jnp.int32).astype(jnp.int16)
    scale[:, cols] = top * (1.0 / LEVELS)


def col_decode(code, scale, cols):
    return code[:, cols].astype(jnp.int32).astype(jnp.float32) * scale[:, cols]


class LineGather:
    def __init__(self, st, full, rows, parts):
        self.st, self.full, self.rows, self.parts = st, full, rows, parts
        self.hs = st.scratch(DMA((2, st.nt, parts)))
        self.hr = st.scratch(DMA((2, st.nt, parts)))
        st.links.add("line")

    def bind(self, get):
        self.ref, self.ss, self.rs = get(self.full), get(self.hs), get(self.hr)
        self.t = lax.axis_index("tp")
        return self

    def piece(self, owner, p):
        chunk = self.rows // self.parts
        return self.ref.at[pl.ds(pl.multiple_of(owner * self.rows + p * chunk, chunk), chunk)]

    def hop(self, owner, k, s, p, where):
        at = self.piece(owner, p)
        return remote(at, at, self.ss.at[k, s, p], self.rs.at[k, s, p], {"tp": where})

    def _send(self, s, p, k, way):
        nt, t = self.st.nt, self.t
        owner, where = t - s * way, t + way
        ok = (owner >= 0) & (owner < nt) & (where >= 0) & (where < nt)
        when(ok, lambda: self.hop(owner, k, s, p, where).start())

    def start(self, p):
        for k, way in enumerate((1, -1)):
            self._send(0, p, k, way)

    def arrive(self, s, p):
        nt, t = self.st.nt, self.t
        for k, way in enumerate((1, -1)):
            owner = t - way * (s + 1)
            ok = (owner >= 0) & (owner < nt)
            when(ok, lambda: self.hop(owner, k, s, p, t).wait_recv())
            if s < nt - 2:
                self._send(s + 1, p, k, way)

    def arrivals(self):
        return [
            functools.partial(self.arrive, s, p) for s in range(self.st.nt - 1) for p in range(self.parts)
        ]

    def finish(self):
        nt, t = self.st.nt, self.t
        for s in range(nt - 1):
            for p in range(self.parts):
                for k, way in enumerate((1, -1)):
                    owner, where = t - s * way, t + way
                    ok = (owner >= 0) & (owner < nt) & (where >= 0) & (where < nt)
                    when(ok, lambda: self.hop(owner, k, s, p, where).wait_send())


class LineScatter:
    def __init__(self, st, part, rows, width, parts):
        self.st, self.part, self.rows, self.width, self.parts = st, part, rows, width, parts
        nt = st.nt
        self.chunk = rows // parts
        shape = (2, (nt - 1) * parts, self.chunk, width)
        self.kept = min(2, nt - 1) * parts
        few = (2, self.kept, self.chunk, width)
        self.hc = [st.scratch(VMEM(x, jnp.int16)) for x in (few, shape)]
        self.hk = [st.scratch(VMEM(x[:2] + (8, 128), jnp.float32)) for x in (few, shape)]
        self.hd = [st.scratch(DMA((2, 2, (nt - 1) * parts))) for _ in range(2)]
        st.links.add("line")

    def bind(self, get):
        self.x = get(self.part)
        (self.cs, self.cr), (self.sc, self.sr), (self.ss, self.rs) = (
            [get(h) for h in hs] for hs in (self.hc, self.hk, self.hd)
        )
        self.t = lax.axis_index("tp")
        return self

    def hops(self, k, u, where):
        w = lax.rem(u, self.kept)
        return (
            remote(self.cs.at[k, w], self.cr.at[k, u], self.ss.at[0, k, u], self.rs.at[0, k, u], {"tp": where}),
            remote(self.sc.at[k, w], self.sr.at[k, u], self.ss.at[1, k, u], self.rs.at[1, k, u], {"tp": where}),
        )

    def _rows(self, base, r, n):
        return self.x[pl.ds(pl.multiple_of(base + r, n), n), :]

    def slots(self):
        return 4 * (self.st.nt - 1)

    def step(self, v, produce=None):
        nt, t, chunk = self.st.nt, self.t, self.chunk
        p, v = v // self.slots(), lax.rem(v, self.slots())
        k = lax.rem(v, 2)
        s = v // 2 - jnp.where(k == 0, t, nt - 1 - t)
        j = jnp.where(k == 0, nt - 1 - s, s)
        way = 1 - 2 * k
        u = s * self.parts + p
        first = t == jnp.where(k == 0, 0, nt - 1)
        passing = (s >= 0) & (s < nt - 1) & jnp.where(k == 0, t < j, t > j)

        @pl.when(passing)
        def _():
            if produce is not None:
                pl.when(p == 0)(lambda: produce(j))

            @pl.when(first)
            def _():
                self.cr[k, u] = jnp.zeros((chunk, self.width), jnp.int16)
                self.sr[k, u] = jnp.zeros((8, 128), jnp.float32)

            @pl.when(jnp.logical_not(first))
            def _():
                for c in self.hops(k, u, t):
                    c.wait_recv()

            @pl.when(u >= self.kept)
            def _():
                for c in self.hops(k, u - self.kept, t + way):
                    c.wait_send()

            base, w = j * self.rows + p * chunk, lax.rem(u, self.kept)
            row_encode(
                lambda r, n: self._rows(base, r, n) + row_decode(self.cr.at[k, u], self.sr.at[k, u], r, n),
                self.cs.at[k, w],
                self.sc.at[k, w],
                chunk,
            )
            for c in self.hops(k, u, t + way):
                c.start()

    def relay(self, p, produce=None, beside=None):
        n = self.slots()

        def one(v, _):
            self.step(v, produce)
            if beside is not None:
                beside(v)
            return 0

        lax.fori_loop(p * n, (p + 1) * n, one, 0)

    def total(self, p, put):
        nt, t, chunk = self.st.nt, self.t, self.chunk
        right, left = (nt - 1 - t) * self.parts + p, t * self.parts + p
        from_left, from_right = t > 0, t < nt - 1

        @pl.when(from_left)
        def _():
            for c in self.hops(0, right, t):
                c.wait_recv()

        @pl.when(from_right)
        def _():
            for c in self.hops(1, left, t):
                c.wait_recv()

        at_r = jnp.where(from_left, right, 0)
        at_l = jnp.where(from_right, left, 0)
        base = t * self.rows + p * chunk

        def body(i, _):
            r = pl.multiple_of(i * 16, 16)
            x = self._rows(base, r, 16)
            a = row_decode(self.cr.at[0, at_r], self.sr.at[0, at_r], r, 16)
            b = row_decode(self.cr.at[1, at_l], self.sr.at[1, at_l], r, 16)
            put(r, x + jnp.where(from_left, a, 0.0) + jnp.where(from_right, b, 0.0))
            return 0

        lax.fori_loop(0, chunk // 16, body, 0)

    def finish(self):
        nt, t = self.st.nt, self.t

        def step(v, _):
            s, k = v // 2, lax.rem(v, 2)
            j = jnp.where(k == 0, nt - 1 - s, s)
            later = s + self.kept // self.parts
            i = jnp.where(k == 0, nt - 1 - later, later)
            waited = (later < nt - 1) & jnp.where(k == 0, t < i, t > i)

            @pl.when(jnp.where(k == 0, t < j, t > j) & jnp.logical_not(waited))
            def _():
                for p in range(self.parts):
                    for c in self.hops(k, s * self.parts + p, t + 1 - 2 * k):
                        c.wait_send()

            return 0

        lax.fori_loop(0, 2 * (nt - 1), step, 0)


class ChipGather:
    def __init__(self, st, w, full, rows):
        self.st, self.w, self.full, self.rows = st, w, full, rows
        self.hs = st.scratch(DMA((st.nd,)))
        self.hr = st.scratch(DMA((st.nd,)))
        self.hl = st.scratch(DMA((1,)))
        st.links |= {"chips", "twin"}

    def bind(self, get):
        self.x, self.o, self.ss, self.rs, ls = (get(h) for h in (self.w, self.full, self.hs, self.hr, self.hl))
        nd = self.st.nd
        d = lax.axis_index("dp")
        twin = {"dp": d + 1 - 2 * lax.rem(d, 2)}
        nc = nd // 2

        def at(i):
            return self.o.at[pl.ds(pl.multiple_of(i * self.rows, self.rows), self.rows)]

        self.own = lambda: pltpu.make_async_copy(self.x, at(d), ls.at[0])
        self.out = lambda i: remote(self.x, at(d), self.ss.at[i], self.rs.at[i], {"dp": lax.rem(d + 2 * i, nd)})

        def fwd(i):
            src = self.x if i == 0 else at(lax.rem(d - 2 * i + nd, nd))
            dst = at(lax.rem(d - 2 * i + nd, nd))
            j = 0 if i == 0 else nc + i
            return remote(src, dst, self.ss.at[j], self.rs.at[j], twin)

        self.fwd, self.nc = fwd, nc
        return self

    def start(self):
        for i in range(1, self.nc):
            self.out(i).start()
        self.fwd(0).start()
        self.own().start()

    def forward(self, i):
        self.out(i).wait_recv()
        self.fwd(i).start()

    def forwards(self):
        return [functools.partial(self.forward, i) for i in range(1, self.nc)]

    def arrived(self):
        for i in range(self.nc):
            self.fwd(i).wait_recv()
        self.own().wait()

    def finish(self):
        for i in range(self.nc):
            self.fwd(i).wait_send()
        for i in range(1, self.nc):
            self.out(i).wait_send()


class ChipScatter:
    def __init__(self, st, g, rows, width):
        self.st, self.g, self.rows, self.width = st, g, rows, width
        nc = self.nc = st.nd // 2
        self.hm = st.scratch(VMEM((nc, rows, width), jnp.float32))
        self.hc = [st.scratch(VMEM((nc - 1, rows, width), jnp.int16)) for _ in range(2)]
        self.hk = [st.scratch(VMEM((nc - 1, 1, width), jnp.float32)) for _ in range(2)]
        self.ht = [st.scratch(DMA((nc,))) for _ in range(2)]
        self.hd = [st.scratch(DMA((2, nc - 1))) for _ in range(2)]
        st.links |= {"chips", "twin"}

    def bind(self, get):
        self.x, self.tw = get(self.g), get(self.hm)
        (self.cs, self.cr), (self.sc, self.sr), (self.ts, self.tr), (self.ss, self.rs) = (
            [get(h) for h in hs] for hs in (self.hc, self.hk, self.ht, self.hd)
        )
        self.d = lax.axis_index("dp")
        self.core = lax.rem(self.d, 2)
        return self

    def at(self, i):
        return pl.ds(pl.multiple_of(i * self.rows, self.rows), self.rows)

    def chip(self, i):
        return lax.rem(self.d // 2 + 1 + i, self.nc)

    def gift(self, i):
        twin = {"dp": self.d + 1 - 2 * self.core}
        src = self.x.at[self.at(2 * self.chip(i) + 1 - self.core)]
        return remote(src, self.tw.at[i], self.ts.at[i], self.tr.at[i], twin)

    def sums(self, i):
        where = {"dp": lax.rem(self.d + 2 * (i + 1), self.st.nd)}
        return (
            remote(self.cs.at[i], self.cr.at[i], self.ss.at[0, i], self.rs.at[0, i], where),
            remote(self.sc.at[i], self.sr.at[i], self.ss.at[1, i], self.rs.at[1, i], where),
        )

    def give(self):
        for i in range(self.nc):
            self.gift(i).start()

    def combine(self, i):
        self.gift(i).wait_recv()
        rows = self.at(2 * self.chip(i) + self.core)
        over_cols(
            self.width,
            lambda cols: col_encode(self.x[rows, cols] + self.tw[i, :, cols], self.cs.at[i], self.sc.at[i], cols),
        )
        for c in self.sums(i):
            c.start()

    def combines(self):
        return [functools.partial(self.combine, i) for i in range(self.nc - 1)]

    def total(self, put):
        n = self.nc - 1
        self.gift(n).wait_recv()
        for i in range(n):
            for c in self.sums(i):
                c.wait_recv()

        def tile(cols):
            x = self.x[self.at(self.d), cols] + self.tw[n, :, cols]
            for i in range(n):
                x = x + col_decode(self.cr.at[i], self.sr.at[i], cols)
            put(cols, x)

        over_cols(self.width, tile)

    def finish(self):
        for i in range(self.nc):
            self.gift(i).wait_send()
        for i in range(self.nc - 1):
            for c in self.sums(i):
                c.wait_send()


class FullSum:
    def __init__(self, st, x, out, shape):
        self.st, self.x, self.out = st, x, out
        self.ha = st.scratch(VMEM((st.nt,) + shape, jnp.float32))
        self.hm = st.scratch(VMEM(shape, jnp.float32))
        self.hb = st.scratch(VMEM((st.nd,) + shape, jnp.float32))
        self.hs = st.scratch(DMA((2, max(st.nd, st.nt))))
        self.hr = st.scratch(DMA((2, max(st.nd, st.nt))))
        st.links |= {"tp", "dp"}

    def run(self, get):
        nd, nt = self.st.nd, self.st.nt
        x, o, a, m, b, ss, rs = (get(h) for h in (self.x, self.out, self.ha, self.hm, self.hb, self.hs, self.hr))
        for k, (axis, n, src, got, dst) in enumerate((("tp", nt, x, a, m), ("dp", nd, m, b, o))):
            me = lax.axis_index(axis)
            cs = [
                remote(src, got.at[me], ss.at[k, i], rs.at[k, i], {axis: lax.rem(me + i, n)}) for i in range(1, n)
            ]
            for c in cs:
                c.start()
            got[me] = src[...]
            for c in cs:
                c.wait()
            total = got[0]
            for i in range(1, n):
                total = total + got[i]
            dst[...] = total


def lane_take(x, offset):
    base = offset // 128 * 128
    wide = min(256, x.shape[-1] - base)
    slab = x[:, base : base + wide]
    if wide % 128:
        slab = jnp.concatenate([slab, jnp.zeros((x.shape[0], -wide % 128), x.dtype)], axis=1)
        wide = slab.shape[-1]
    if offset > base:
        slab = pltpu.roll(slab, wide - (offset - base), 1)
    slab = slab[:, :128]
    return jnp.where(lax.broadcasted_iota(jnp.int32, slab.shape, 1) < HD, slab, 0.0)


def lane_place(x, offset, width):
    base = offset // 128 * 128
    wide = min(256, width - base)
    slab = x if wide == 128 else jnp.concatenate([x, jnp.zeros_like(x)], axis=1)
    if offset > base:
        slab = pltpu.roll(slab, offset - base, 1)
    slab = slab[:, :wide]
    pieces = []
    if base:
        pieces.append(jnp.zeros((x.shape[0], base), x.dtype))
    pieces.append(slab)
    if base + wide < width:
        pieces.append(jnp.zeros((x.shape[0], width - base - wide), x.dtype))
    return jnp.concatenate(pieces, axis=1) if len(pieces) > 1 else slab


def turned(u, cosine, sine):
    wide = u.shape[-1]
    lane = lax.rem(lax.broadcasted_iota(jnp.int32, u.shape, 1), HD)
    swap = jnp.where(lane < HD // 2, pltpu.roll(u, wide - HD // 2, 1), pltpu.roll(u, HD // 2, 1))
    return u * cosine + swap * sine


def nt_dot(a, b):
    return lax.dot_general(a, b, (((1,), (1,)), ((), ())), preferred_element_type=jnp.float32)


def per_tile(count, size, fn):
    def body(i, _):
        fn(pl.multiple_of(i * size, size))
        return 0

    lax.fori_loop(0, count, body, 0)


def in_turn(*lists):
    for i in range(max(len(x) for x in lists)):
        for x in lists:
            if i < len(x):
                x[i]()


class Fused(Stage):
    def body(self, fn):
        self.tasks = [lambda get: iter(fn(get) or ())]


def inverse_rms(x):
    return lax.rsqrt(jnp.mean(x * x, axis=-1, keepdims=True) + norm_eps)


def tn_dot(a, b):
    return lax.dot_general(a, b, (((0,), (0,)), ((), ())), preferred_element_type=jnp.float32)


def across(x, count):
    return jnp.concatenate([x] * count, axis=1) if count > 1 else x


def masked_scores(keys, queries, first, begin, span, group):
    s = nt_dot(keys, queries) * (1.0 / math.sqrt(HD))
    key = lax.broadcasted_iota(jnp.int32, s.shape, 0) + first
    own = lax.rem(lax.broadcasted_iota(jnp.int32, s.shape, 1), 128) + (first + 2 * span)
    return s, (key >= across(begin, group)) & (key <= own)


def attention_stage(nd, nt, tokens, attn_gain, ffn_gain, out_grad, begin, cosine, sine, w_attn, w_gate, w_up, w_down_t, heads):
    st = Fused("attend", 1, nd, nt)
    low, f32 = jnp.bfloat16, jnp.float32
    own, width = tokens.shape
    span = own * nt
    shard = w_attn.shape[0]
    n_q, n_kv = heads
    group = n_q // n_kv
    tiles = span // 128
    qw, kvw = n_q * HD, n_kv * HD
    reach = 2 * span + 128
    parts = 2
    piece = own // parts

    h_tok, h_g1, h_g2 = st.inp(tokens), st.inp(attn_gain[None]), st.inp(ffn_gain[None])
    h_og, h_begin = st.inp(out_grad), st.inp(begin)
    h_cos, h_sin = st.inp(cosine), st.inp(sine)
    h_wa, h_wg, h_wu, h_wd = st.inp(w_attn), st.inp(w_gate), st.inp(w_up), st.inp(w_down_t)

    o_h1, o_h2, o_gr = (st.out((span, width), low) for _ in range(3))
    o_wa = st.out((nd * shard, w_attn.shape[1]), low)
    o_wg, o_wu, o_wd = (st.out((nd * shard, w.shape[1]), low, pl.ANY) for w in (w_gate, w_up, w_down_t))
    o_q = st.out((n_kv, tiles, group * 128, 128), low)
    o_k, o_v = (st.out((n_kv, 3 * span, 128), low) for _ in range(2))
    o_kt = st.out((n_kv, 128, 3 * span), low)
    o_ctx = st.out((span, qw), low)
    o_ch = st.out((n_kv, tiles, group * 128, 128), low)
    o_lse = st.out((n_kv, tiles, 1, group * 128), f32)
    o_res = st.out((own, width), f32)

    h_win = st.scratch(VMEM((3, span, 2 * kvw), low))
    h_ks = st.scratch(DMA((2,)))
    h_kr = st.scratch(DMA((2,)))
    h_vt = st.scratch(VMEM((n_kv, 128, 3 * span), low))
    h_part = st.scratch(VMEM((span, width), f32))

    ag1 = LineGather(st, o_h1, own, parts)
    ag2 = LineGather(st, o_h2, own, parts)
    ag3 = LineGather(st, o_gr, own, parts)
    rs1 = LineScatter(st, h_part, own, width, parts)
    wa = ChipGather(st, h_wa, o_wa, shard)
    wg = ChipGather(st, h_wg, o_wg, shard)
    wu = ChipGather(st, h_wu, o_wu, shard)
    wd = ChipGather(st, h_wd, o_wd, shard)
    st.links.add("near")

    def fn(get):
        d, t = lax.axis_index("dp"), lax.axis_index("tp")
        for x in (ag1, ag2, ag3, rs1, wa, wg, wu, wd):
            x.bind(get)
        tok, g1, g2, h1, h2 = get(h_tok), get(h_g1), get(h_g2), get(o_h1), get(o_h2)
        wa_ref, win, q, k, v, kt, vt, ch = (get(h) for h in (o_wa, h_win, o_q, o_k, o_v, o_kt, h_vt, o_ch))
        ctx, lse, res, part = get(o_ctx), get(o_lse), get(o_res), get(h_part)
        cos_ref, sin_ref, begin_ref = get(h_cos), get(h_sin), get(h_begin)

        wa.start()

        def first_norm(p):
            def tile(r):
                x = tok[pl.ds(p * piece + r, 16), :].astype(f32)
                at = pl.ds(pl.multiple_of(t * own + p * piece + r, 16), 16)
                h1[at, :] = (x * inverse_rms(x) * g1[...]).astype(low)

            per_tile(piece // 16, 16, tile)

        for p in range(parts):
            first_norm(p)
            ag1.start(p)
        get(o_gr)[pl.ds(pl.multiple_of(t * own, own), own), :] = get(h_og)[...]
        in_turn(ag1.arrivals(), wa.forwards())
        for p in range(parts):
            ag3.start(p)
        wa.arrived()

        def project(r):
            rows = pl.ds(r, 128)
            x = dot(h1[rows, :], wa_ref[:, : qw + 2 * kvw])
            x = turned(x, cos_ref[rows, :], sin_ref[rows, :])
            for h in range(n_q):
                q[h // group, r // 128, h % group * 128 : (h % group + 1) * 128, :] = lane_take(x, h * HD).astype(low)
            win[2, rows, :] = x[:, qw:].astype(low)

        per_tile(tiles, 128, project)

        def ahead(i):
            return remote(win.at[2], win.at[2 - i], get(h_ks).at[i - 1], get(h_kr).at[i - 1], {"dp": d + i})

        for i in (2, 1):
            when(d + i < nd, lambda: ahead(i).start())

        def unpack(b):
            def tile(r):
                x = win[b, pl.ds(r, 128), :].astype(f32)
                at = pl.ds(pl.multiple_of(b * span + r, 128), 128)
                for g in range(n_kv):
                    y = lane_take(x, g * HD)
                    k[g, at, :] = y.astype(low)
                    kt[g, :, at] = y.T.astype(low)
                    y = lane_take(x, kvw + g * HD)
                    v[g, at, :] = y.astype(low)
                    vt[g, :, at] = y.T.astype(low)

            per_tile(tiles, 128, tile)

        unpack(2)
        for i in (1, 2):

            @pl.when(d < i)
            def _():
                win[2 - i] = jnp.zeros((span, 2 * kvw), low)

            when(d >= i, lambda: ahead(i).wait_recv())
            unpack(2 - i)
        wd.start()
        wg.start()

        def attend(u, _):
            g, i = u // tiles, lax.rem(u, tiles)
            at = pl.multiple_of(i * 128, 128)
            keys = pl.ds(at, reach)
            s, seen = masked_scores(k[g, keys, :], q[g, i], at, begin_ref[:, pl.ds(at, 128)], span, group)
            s = jnp.where(seen, s, masked_score)
            top = jnp.max(s, axis=0, keepdims=True)
            e = jnp.exp(s - top)
            total = jnp.sum(e, axis=0, keepdims=True)
            p = (e * (1.0 / total)).astype(low)
            lse[g, i] = top + jnp.log(total)
            ch[g, i] = dot(vt[g, :, keys], p).T.astype(low)
            return 0

        half = max(1, n_kv * tiles // 2)
        arrive3 = ag3.arrivals()
        lax.fori_loop(0, half, attend, 0)
        cut = len(arrive3) // 2
        for x in arrive3[:cut]:
            x()
        lax.fori_loop(half, n_kv * tiles, attend, 0)
        for x in arrive3[cut:]:
            x()

        def pack(r):
            x = 0.0
            for h in range(n_q):
                at = h % group * 128
                x = x + lane_place(ch[h // group, r // 128, at : at + 128, :].astype(f32), h * HD, qw)
            ctx[pl.ds(r, 128), :] = x.astype(low)

        per_tile(tiles, 128, pack)

        def out_rows(j):
            rows = pl.ds(pl.multiple_of(j * own, own), own)
            for c in range(0, width, 512):
                part[rows, c : c + 512] = nt_dot(ctx[rows, :], wa_ref[c : c + 512, qw + 2 * kvw :])

        rs1.relay(0, out_rows)
        in_turn(wd.forwards(), wg.forwards())
        wu.start()
        out_rows(t)

        def second_norm(p):
            def put(r, x):
                at = pl.ds(p * piece + r, 16)
                x = x + tok[at, :].astype(f32)
                res[at, :] = x
                rows = pl.ds(pl.multiple_of(t * own + p * piece + r, 16), 16)
                h2[rows, :] = (x * inverse_rms(x) * g2[...]).astype(low)

            rs1.total(p, put)
            ag2.start(p)

        for p in range(parts):
            if p:
                rs1.relay(p)
            second_norm(p)
        in_turn(ag2.arrivals(), wu.forwards())
        for x in (wd, wg, wu):
            x.arrived()
        for x in (ag1, ag2, ag3, rs1, wa, wg, wu, wd):
            x.finish()
        for i in (2, 1):
            when(d + i < nd, lambda: ahead(i).wait_send())

    st.body(fn)
    return st.run()


def ffn_stage(nd, nt, hidden2, grad_rows, w_gate, w_up, w_down_t, residual, ffn_gain, out_grad):
    st = Fused("ffn", 2, nd, nt)
    low, f32 = jnp.bfloat16, jnp.float32
    span, width = hidden2.shape
    own = span // nt
    units = w_gate.shape[1]
    shard = width // nd
    parts = 2
    piece = own // parts
    tile_u = 256

    h_h2, h_gr, h_wg, h_wu, h_wd = (st.inp(x) for x in (hidden2, grad_rows, w_gate, w_up, w_down_t))
    h_res, h_gain, h_og = st.inp(residual), st.inp(ffn_gain[None]), st.inp(out_grad)
    o_ia = st.out((span, units), low)
    o_rl = st.out((span, width), low)
    o_rg = st.out((own, width), f32)
    o_fg = st.out((1, width), f32)
    o_dd = st.out((units, shard), f32)
    o_dg, o_du = (st.out((shard, units), f32) for _ in range(2))
    h_gl, h_ul = (st.scratch(VMEM((span, units), low)) for _ in range(2))
    h_part = st.scratch(VMEM((span, width), f32))
    h_ga, h_gb = (st.scratch(VMEM((width, units), f32)) for _ in range(2))
    rs = LineScatter(st, h_part, own, width, parts)
    ag = LineGather(st, o_rl, own, parts)
    sd, sg, su = ChipScatter(st, h_ga, shard, units), ChipScatter(st, h_gb, shard, units), ChipScatter(st, h_ga, shard, units)

    def fn(get):
        t = lax.axis_index("tp")
        for x in (rs, ag, sd, sg, su):
            x.bind(get)
        h2, gr, wg, wu, wd, res, gain, og = (get(h) for h in (h_h2, h_gr, h_wg, h_wu, h_wd, h_res, h_gain, h_og))
        ia, rl, rg, fg, gl, ul, part, ga, gb = (get(h) for h in (o_ia, o_rl, o_rg, o_fg, h_gl, h_ul, h_part, h_ga, h_gb))

        def act(c):
            cols = pl.ds(c, tile_u)
            gate = dot(h2[...], wg[:, cols])
            up = dot(h2[...], wu[:, cols])
            back = dot(gr[...], wd[:, cols])
            sig = jax.nn.sigmoid(gate)
            ia[:, cols] = (gate * sig * up).astype(low)
            gl[:, cols] = (back * up * (sig * (1.0 + gate * (1.0 - sig)))).astype(low)
            ul[:, cols] = (back * gate * sig).astype(low)

        per_tile(units // tile_u, tile_u, act)

        def rows_back(j):
            rows = pl.ds(pl.multiple_of(j * own, own), own)
            for c in range(0, width, 512):
                part[rows, c : c + 512] = nt_dot(gl[rows, :], wg[c : c + 512, :]) + nt_dot(ul[rows, :], wu[c : c + 512, :])

        blocks_w = width // 256

        def weight_part(dst, x, y, v):
            @pl.when(v < blocks_w)
            def _():
                cols = pl.ds(pl.multiple_of(v * 256, 256), 256)
                dst[cols, :] = tn_dot(x[:, cols], y[...])

        n = rs.slots()
        rs.relay(0, rows_back, lambda v: weight_part(ga, gr, ia, v))
        per_tile(max(0, blocks_w - n), 256, lambda r: weight_part(ga, gr, ia, n + r // 256))
        sd.give()
        rows_back(t)
        fg[...] = jnp.zeros_like(fg)

        def joined(p):
            def put(r, x):
                at = pl.ds(p * piece + r, 16)
                y = res[at, :]
                inverse = inverse_rms(y)
                normed = y * inverse
                fg[...] += jnp.sum(x * normed, axis=0, keepdims=True)
                e = x * gain[...]
                back = inverse * (e - normed * jnp.mean(e * normed, axis=-1, keepdims=True))
                y = og[at, :].astype(f32) + back
                rg[at, :] = y
                rl[pl.ds(pl.multiple_of(t * own + p * piece + r, 16), 16), :] = y.astype(low)

            rs.total(p, put)
            ag.start(p)

        joined(0)
        rs.relay(1, None, lambda v: weight_part(gb, h2, gl, v - n))
        per_tile(max(0, blocks_w - n), 256, lambda r: weight_part(gb, h2, gl, n + r // 256))
        sg.give()
        joined(1)
        arrivals = ag.arrivals()
        for x in sd.combines():
            x()
        for i in range(st.nd // 2):
            sd.gift(i).wait_send()
        for x in arrivals[:2]:
            x()

        def put_down(cols, x):
            get(o_dd)[cols, :] = x.T

        in_turn(sg.combines(), arrivals[2:])
        sd.total(put_down)
        per_tile(blocks_w, 256, lambda r: weight_part(ga, h2, ul, r // 256))
        su.give()

        def put_gate(cols, x):
            get(o_dg)[:, cols] = x

        def put_up(cols, x):
            get(o_du)[:, cols] = x

        for x in su.combines():
            x()
        sg.total(put_gate)
        su.total(put_up)
        for i in range(st.nd // 2 - 1):
            for c in sd.sums(i):
                c.wait_send()
        sg.finish()
        su.finish()
        rs.finish()
        ag.finish()

    st.body(fn)
    return st.run()


def back_stage(
    nd, nt, tokens, attn_gain, begin, cosine, sine, w_attn, w_down_t, inner_act, residual, residual_rows, residual_grad,
    ffn_part_sum, hidden1, queries, keys, values, keys_t, context, context_heads, log_total, heads,
):
    st = Fused("back", 3, nd, nt)
    low, f32 = jnp.bfloat16, jnp.float32
    own, width = tokens.shape
    span = own * nt
    shard = width // nd
    units = inner_act.shape[1]
    n_q, n_kv = heads
    group = n_q // n_kv
    tiles = span // 128
    qw, kvw = n_q * HD, n_kv * HD
    qkvw = qw + 2 * kvw
    reach = 2 * span + 128
    parts = 2
    piece = own // parts

    h_tok, h_gain, h_begin, h_cos, h_sin = (st.inp(x) for x in (tokens, attn_gain[None], begin, cosine, sine))
    h_wa, h_wd, h_ia, h_res, h_rl, h_rg = (
        st.inp(x) for x in (w_attn, w_down_t, inner_act, residual, residual_rows, residual_grad)
    )
    h_fg, h_h1, h_q, h_k, h_v, h_kt, h_ctx, h_ch, h_lse = (
        st.inp(x)
        for x in (ffn_part_sum, hidden1, queries, keys, values, keys_t, context, context_heads, log_total)
    )
    o_out = st.out((own, width), low)
    o_tg = st.out((own, width), f32)
    o_gains = st.out((1, 2 * width), f32)
    o_sum = st.out((shard, qkvw + qw), f32)
    h_fp = h_part = st.scratch(VMEM((span, width), f32))
    h_dc = st.scratch(VMEM((n_kv, tiles, group * 128, 128), low))
    h_delta = st.scratch(VMEM((n_kv, tiles, 1, group * 128), f32))
    h_dq = st.scratch(VMEM((n_kv, tiles, group * 128, 128), f32))
    h_dk, h_dv = (st.scratch(VMEM((n_kv, 3 * span, 128), f32)) for _ in range(2))
    h_kvs, h_kvr = (st.scratch(VMEM((2, span, 2 * kvw), jnp.int16)) for _ in range(2))
    h_kss, h_ksr = (st.scratch(VMEM((2, tiles, 1, 2 * kvw), f32)) for _ in range(2))
    h_kd = [st.scratch(DMA((2, 2))) for _ in range(2)]
    h_low = st.scratch(VMEM((span, qkvw), low))
    h_g = st.scratch(VMEM((width, qkvw + qw), f32))
    h_mine = st.scratch(VMEM((1, 2 * width), f32))
    rf = LineScatter(st, h_fp, own, width, parts)
    rs = LineScatter(st, h_part, own, width, parts)
    sa = ChipScatter(st, h_g, shard, qkvw + qw)
    full = FullSum(st, h_mine, o_gains, (1, 2 * width))
    st.links.add("near")

    def fn(get):
        d, t = lax.axis_index("dp"), lax.axis_index("tp")
        for x in (rf, rs, sa):
            x.bind(get)
        tok, gain, begin_ref, cos_ref, sin_ref = (get(h) for h in (h_tok, h_gain, h_begin, h_cos, h_sin))
        wa, wd, ia, res, rl, rg = (get(h) for h in (h_wa, h_wd, h_ia, h_res, h_rl, h_rg))
        h1, q, k, v, kt, ctx, ch, lse = (get(h) for h in (h_h1, h_q, h_k, h_v, h_kt, h_ctx, h_ch, h_lse))
        fp, part, dc, delta, dq, dk, dv = (get(h) for h in (h_fp, h_part, h_dc, h_delta, h_dq, h_dk, h_dv))
        kvs, kvr, kss, ksr, (ks, kr) = get(h_kvs), get(h_kvr), get(h_kss), get(h_ksr), (get(h) for h in h_kd)
        xl, gw, mine = get(h_low), get(h_g), get(h_mine)

        def context_back(r):
            rows = pl.ds(r, 128)
            x = dot(rl[rows, :], wa[:, qkvw:])
            i = r // 128
            for h in range(n_q):
                g, at = h // group, pl.ds(h % group * 128, 128)
                y = lane_take(x, h * HD).astype(low)
                dc[g, i, at, :] = y
                z = y.astype(f32) * ch[g, i, at, :].astype(f32)
                delta[g, i, :, at] = jnp.sum(z.T, axis=0, keepdims=True)

        per_tile(tiles, 128, context_back)

        def ffn_rows(r):
            cols = pl.ds(r, 512)
            fp[:, cols] = nt_dot(ia[...], wd[cols, :])

        per_tile(width // 512, 512, ffn_rows)
        dk[...] = jnp.zeros_like(dk)
        dv[...] = jnp.zeros_like(dv)
        count = n_kv * tiles
        slots = rf.slots() * parts
        per = -(-slots // count)

        def attend(u, _):
            def pump(w, _):
                pl.when(w < slots)(lambda: rf.step(w))
                return 0

            lax.fori_loop(u * per, u * per + per, pump, 0)
            g, i = u // tiles, lax.rem(u, tiles)
            at = pl.multiple_of(i * 128, 128)
            keys = pl.ds(at, reach)
            qq, dd = q[g, i], dc[g, i]
            s, seen = masked_scores(k[g, keys, :], qq, at, begin_ref[:, pl.ds(at, 128)], span, group)
            p = jnp.where(seen, jnp.exp(s - lse[g, i]), 0.0)
            ds = (p * (nt_dot(v[g, keys, :], dd) - delta[g, i])).astype(low)
            dv[g, keys, :] += dot(p.astype(low), dd)
            dk[g, keys, :] += dot(ds, qq)
            dq[g, i] = dot(kt[g, :, keys], ds).T
            return 0

        lax.fori_loop(0, count, attend, 0)
        scale = 1.0 / math.sqrt(HD)

        def kv_rows(b, r):
            at = pl.ds(pl.multiple_of(b * span + r, 128), 128)
            x = 0.0
            for g in range(n_kv):
                x = x + lane_place(dk[g, at, :] * scale, g * HD, 2 * kvw)
                x = x + lane_place(dv[g, at, :], kvw + g * HD, 2 * kvw)
            return x

        def back(i):
            where = {"dp": d - i}
            return (
                remote(kvs.at[i - 1], kvr.at[i - 1], ks.at[0, i - 1], kr.at[0, i - 1], where),
                remote(kss.at[i - 1], ksr.at[i - 1], ks.at[1, i - 1], kr.at[1, i - 1], where),
            )

        for i in (2, 1):

            @pl.when(d >= i)
            def _():
                def tile(r):
                    x = kv_rows(2 - i, r)
                    col_encode(x, kvs.at[i - 1, pl.ds(r, 128)], kss.at[i - 1, r // 128], slice(None))

                per_tile(tiles, 128, tile)
                for c in back(i):
                    c.start()

        def query_rows(r):
            rows = pl.ds(r, 128)
            x = 0.0
            for h in range(n_q):
                at = h % group * 128
                x = x + lane_place(dq[h // group, r // 128, at : at + 128, :] * scale, h * HD, qw)
            pad = jnp.zeros((128, 2 * kvw), f32)
            x = turned(jnp.concatenate([x, pad], axis=1), cos_ref[rows, :], -sin_ref[rows, :])
            xl[rows, :] = x.astype(low)

        per_tile(tiles, 128, query_rows)

        def put_out(p):
            def put(r, x):
                at = pl.ds(p * piece + r, 16)
                get(o_out)[at, :] = (res[at, :] + x).astype(low)

            rf.total(p, put)

        for p in range(parts):
            put_out(p)

        def weight_q(r):
            cols = pl.ds(r, 256)
            gw[cols, qkvw:] = tn_dot(rl[:, cols], ctx[...])

        per_tile(width // 256, 256, weight_q)
        for i in (1, 2):

            @pl.when(d + i < nd)
            def _():
                for c in back(i):
                    c.wait_recv()

        near1, near2 = d + 1 < nd, d + 2 < nd

        def kv_total(r):
            rows = pl.ds(r, 128)
            x = kv_rows(2, r)
            a = col_decode(kvr.at[0, rows], ksr.at[0, r // 128], slice(None))
            b = col_decode(kvr.at[1, rows], ksr.at[1, r // 128], slice(None))
            x = x + jnp.where(near1, a, 0.0) + jnp.where(near2, b, 0.0)
            pad = jnp.zeros((128, qw), f32)
            x = turned(jnp.concatenate([pad, x], axis=1), cos_ref[rows, :], -sin_ref[rows, :])
            xl[rows, qw:] = x[:, qw:].astype(low)

        per_tile(tiles, 128, kv_total)

        def hidden_rows(j):
            rows = pl.ds(pl.multiple_of(j * own, own), own)
            for c in range(0, width, 512):
                part[rows, c : c + 512] = nt_dot(xl[rows, :], wa[c : c + 512, :qkvw])

        blocks_w = width // 256

        def weight_part(v):
            @pl.when(v < blocks_w)
            def _():
                cols = pl.ds(pl.multiple_of(v * 256, 256), 256)
                gw[cols, :qkvw] = tn_dot(h1[:, cols], xl[...])

        n = rs.slots()
        rs.relay(0, hidden_rows, weight_part)
        per_tile(max(0, blocks_w - n), 256, lambda r: weight_part(n + r // 256))
        sa.give()
        hidden_rows(t)
        mine[...] = jnp.zeros_like(mine)
        mine[:, width:] = get(h_fg)[...]

        def last(p):
            def put(r, x):
                at = pl.ds(p * piece + r, 16)
                y = tok[at, :].astype(f32)
                inverse = inverse_rms(y)
                normed = y * inverse
                mine[:, :width] += jnp.sum(x * normed, axis=0, keepdims=True)
                e = x * gain[...]
                e = inverse * (e - normed * jnp.mean(e * normed, axis=-1, keepdims=True))
                get(o_tg)[at, :] = rg[at, :] + e

            rs.total(p, put)

        combines = sa.combines()
        combines[0]()
        last(0)
        for x in combines[1:]:
            x()
        rs.relay(1)
        last(1)
        full.run(get)

        def put_sum(cols, x):
            get(o_sum)[:, cols] = x

        sa.total(put_sum)
        for x in (rf, rs, sa):
            x.finish()
        for i in (2, 1):

            @pl.when(d >= i)
            def _():
                for c in back(i):
                    c.wait_send()

    st.body(fn)
    return st.run()


def rope_tables(position_ids, head_size):
    half_size = head_size // 2
    inverse = rope_base ** (-(jnp.arange(half_size, dtype=jnp.float32) * 2.0 / head_size))
    angles = position_ids.astype(jnp.float32)[:, None] * inverse[None, :]
    return (jnp.cos(angles), jnp.sin(angles))


def dot(a, b):
    return jnp.dot(a, b, preferred_element_type=jnp.float32)


def on_device(
    nd, nt, tokens, positions, attn_gain, w_query, w_key, w_value, w_out, ffn_gain, w_gate, w_up, w_down, out_grad
):
    span = tokens.shape[0] * nt
    width = tokens.shape[1]
    heads = (w_query.shape[1] // HD, w_key.shape[1] // HD)
    qw, kvw = w_query.shape[1], w_key.shape[1]
    w_attn = jnp.concatenate([w_query, w_key, w_value, w_out.T], axis=1)
    w_down_t = w_down.T
    cosine, sine = rope_tables(positions, HD)
    turn = heads[0] + heads[1]
    still = jnp.ones((span, kvw), jnp.float32)
    cosine = jnp.concatenate([jnp.tile(cosine, (1, 2 * turn)), still], axis=1)
    sine = jnp.concatenate([jnp.tile(jnp.concatenate([-sine, sine], axis=1), (1, turn)), 0.0 * still], axis=1)
    begin = (2 * span + jnp.arange(span, dtype=jnp.int32) - positions)[None]
    (hidden1, hidden2, grad_rows, attn_full, gate_full, up_full, down_full_t, queries, keys, values, keys_t, context, context_heads, log_total, residual) = (
        attention_stage(nd, nt, tokens, attn_gain, ffn_gain, out_grad, begin, cosine, sine, w_attn, w_gate, w_up, w_down_t, heads)
    )
    inner_act, residual_rows, residual_grad, ffn_gain_part, down_sum, gate_sum, up_sum = ffn_stage(
        nd, nt, hidden2, grad_rows, gate_full, up_full, down_full_t, residual, ffn_gain, out_grad
    )
    output, tokens_grad, gains, attn_sum = back_stage(
        nd, nt, tokens, attn_gain, begin, cosine, sine, attn_full, down_full_t, inner_act, residual, residual_rows,
        residual_grad, ffn_gain_part, hidden1, queries, keys, values, keys_t, context, context_heads, log_total, heads,
    )
    cuts = (qw, qw + kvw, qw + 2 * kvw)
    return (
        output,
        tokens_grad,
        gains[0, :width],
        attn_sum[:, : cuts[0]],
        attn_sum[:, cuts[0] : cuts[1]],
        attn_sum[:, cuts[1] : cuts[2]],
        attn_sum[:, cuts[2] :].T,
        gains[0, width:],
        gate_sum,
        up_sum,
        down_sum,
    )


def solution(mesh):
    return jax.shard_map(
        functools.partial(on_device, mesh.shape["dp"], mesh.shape["tp"]),
        mesh=mesh,
        in_specs=(
            P(("dp", "tp"), None),
            P("dp"),
            P(),
            P("dp", "tp"),
            P("dp", "tp"),
            P("dp", "tp"),
            P("tp", "dp"),
            P(),
            P("dp", "tp"),
            P("dp", "tp"),
            P("tp", "dp"),
            P(("dp", "tp"), None),
        ),
        out_specs=(
            P(("dp", "tp"), None),
            P(("dp", "tp"), None),
            P(),
            P("dp", "tp"),
            P("dp", "tp"),
            P("dp", "tp"),
            P("tp", "dp"),
            P(),
            P("dp", "tp"),
            P("dp", "tp"),
            P("tp", "dp"),
        ),
        check_vma=False,
    )
```

time: 997 us -> 384 us (0.39)
  waiting for transfers between devices: 767 us -> 0 us
  Pallas kernels: 0 us -> 362 us
  matrix products: 95.3 us -> 0 us
  blocking collectives: 64.9 us -> 0 us
  other arithmetic: 21.3 us -> 1.79 us
  starting transfers between devices: 16.1 us -> 0 us
  between operations: 15.5 us -> 0.73 us
  local copies, waits for them, and re-layouts: 7.17 us -> 18 us
    reduce_scatter x11 -> x0, waiting for transfers between devices: 506 us -> none  [the longest x1 65.6 us: on_device(): lax.psum_scatter(w_gate_grad, 'dp', scatter_dimension=0, tiled=True)]
    pallas_call x0 -> x3, Pallas kernels: none -> 362 us  [run(): pl.pallas_call(kernel, out_shape=[jax.ShapeDtypeStruct(s, t) for s, t, _...]
    all_gather x9 -> x0, waiting for transfers between devices: 233 us -> none  [the longest x1 37.8 us: on_device(): lax.all_gather((normed2 * ffn_gain).astype(jnp.bfloat16), 'tp', axis=0, t...]
    dot_general x27 -> x0, matrix products: 95.3 us -> none  [the longest x1 7.21 us: on_device(): jnp.dot(grad_rows, down_back.T, preferred_element_type=jnp.float32)]
    psum x1 -> x0, blocking collectives: 42.9 us -> none  [on_device(): gain_sums = lax.psum((attn_gain_part, ffn_gain_part), ('dp', 'tp'))]
    ppermute x4 -> x0, waiting for transfers between devices: 23.2 us -> none  [passed_along(): return lax.ppermute(block, axis, route)]
    all_gather x2 -> x0, blocking collectives: 22.1 us -> none  [the longest x1 12.1 us: on_device(): lax.all_gather(w_key, 'dp', axis=0, tiled=True)]
    ppermute x4 -> x0, starting transfers between devices: 14.7 us -> none  [passed_along(): return lax.ppermute(block, axis, route)]
  transfers between devices with their start and end apart: 24 -> 0, of which waited for: 22 -> 0; matrix products, arithmetic and copies ran while one was open for 7% -> 0% of each run, Pallas kernels for 0% -> 0%
where the time goes in v2:
time: 384 us; the launch traced here: 383 us
  Pallas kernels  362 us (94%)
  local copies, waits for them, and re-layouts  18 us (5%)
    pallas_call x3, Pallas kernels, run(): pl.pallas_call(kernel, out_shape=[jax.ShapeDtypeStruct(s, t) for s, t, _...  362 us

profile of v2, /device:TPU:1, one launch (start us, length us, event | category | flops | bytes accessed | tf_op | source)
XLA Modules:
  0.0 382.6 jit_solution(16615126810783993240)
XLA Ops:
  0.7 1.3 fusion.2
  2.0 1.3 broadcast_in_dim.6.refs_1_
  3.3 1.3 broadcast_in_dim.16.refs_2_.refs_6_
  4.6 0.4 fusion
  5.0 2.0 concatenate.15.refs_7_
  7.0 0.1 tile.20
  7.1 0.4 copy.25
  7.5 1.3 concatenate.14.refs_6_.refs_4_
  8.8 0.1 tile.8
  9.0 0.4 copy.24
  9.4 1.3 concatenate.12.refs_5_.refs_3_
  10.7 125.8 %attend.1 = (bf16[512,1536]{1,0:T(8,128)(2,1)}, bf16[512,1536]{1,0:T(8,128)(2,1)}, bf16[512,1536]{1,0:T(8,128)(2,1)}, bf16[1536,1152]{1,0:T(8,128)(2,1)}, bf16[1...) custom-call(bf16[128,1536]{1,0:T(8,128)(2,1)} %refs_0_.3, ...), custom_call_target="tpu_custom_call" | custom-call | tf_op jit(solution)/shard_map/attend/pallas_call | solution.py:100
  136.5 124.6 %ffn.1 = (bf16[512,1024]{1,0:T(8,128)(2,1)}, bf16[512,1536]{1,0:T(8,128)(2,1)}, f32[128,1536]{1,0:T(8,128)}, f32[1,1536]{1,0:T(1,128)}, f32[1024,192]{1,0:T(8,12...) custom-call(bf16[512,1536]{1,0:T(8,128)(2,1)} %get-tuple-element.39.refs_0_, bf16[512,1536]{1,0:T(8,128)(2,1)} %get-tuple-element.40.refs_1_, ...), custom_call_target="tpu_custom_call" | custom-call | tf_op jit(solution)/shard_map/ffn/pallas_call | solution.py:100
  261.2 111.6 %back.1 = (bf16[128,1536]{1,0:T(8,128)(2,1)}, f32[128,1536]{1,0:T(8,128)}, f32[1,3072]{1,0:T(1,128)}, f32[192,1152]{1,0:T(8,128)}) custom-call(bf16[128,1536]{1,0:T(8,128)(2,1)} %refs_0_.3, f32[1,1536]{1,0:T(1,128)} %broadcast_in_dim.6.refs_1_, s32[1,512]{1,0:T(1,128)} %bitcast.12, f32[512,768]{1,0:T(8,128)} %concatenate.12.refs_5_.refs_3_, ...), custom_call_target="tpu_custom_call" | custom-call | tf_op jit(solution)/shard_map/back/pallas_call | solution.py:100
  372.7 0.0 copy-start
  372.7 1.4 slice_reduce_fusion
  374.2 1.8 fusion.1
  376.0 0.0 copy-start.4
  376.0 2.0 slice_bitcast_fusion
  377.9 0.0 copy-start.3
  378.0 0.0 copy-done
  378.0 1.2 copy.26
  379.2 0.0 copy-done.4
  379.2 0.0 copy-start.2
  379.2 0.7 copy.31
  379.9 0.0 copy-done.3
  379.9 0.0 copy-start.1
  379.9 0.9 copy.32
  380.8 0.0 copy-done.2
  380.8 0.9 copy.33
  381.7 0.0 copy-done.1
  381.7 0.9 copy.34
  (2 shorter events, 0.0 us)
Async XLA Ops:
  372.7 5.2 %copy-start = (f32[1024,192]{1,0:T(8,128)S(1)}, f32[1024,192]{1,0:T(8,128)}, u32[]{:S(2)}) copy-start(f32[1024,192]{1,0:T(8,128)} %get-tuple-element.84) | copy-start | bytes 2359300
  376.0 3.2 copy-start.4
  377.9 2.0 copy-start.3
  379.2 1.6 copy-start.2
  379.9 1.8 copy-start.1

commit v3 on v2

--- a/solution.py
+++ b/solution.py
@@ -104,7 +104,7 @@
             out_specs=[pl.BlockSpec(memory_space=sp) for _, _, sp in self.outs],
             scratch_shapes=self.scr,
             compiler_params=pltpu.CompilerParams(
-                collective_id=self.cid, has_side_effects=True, vmem_limit_bytes=63 << 20
+                collective_id=self.cid, has_side_effects=True, vmem_limit_bytes=67_000_000
             ),
             name=self.name,
         )(*[x for x, _ in self.ins])
@@ -204,6 +204,19 @@
             when(ok, lambda: self.hop(owner, k, s, p, t).wait_recv())
             if s < nt - 2:
                 self._send(s + 1, p, k, way)
+
+    def arrive_at(self, v):
+        nt, t = self.st.nt, self.t
+        s, p = v // self.parts, lax.rem(v, self.parts)
+        for k, way in enumerate((1, -1)):
+            owner = t - way * (s + 1)
+            ok = (owner >= 0) & (owner < nt) & (s < nt - 1)
+            where = t + way
+
+            @pl.when(ok)
+            def _():
+                self.hop(owner, k, s, p, t).wait_recv()
+                when((where >= 0) & (where < nt) & (s < nt - 2), lambda: self.hop(owner, k, s + 1, p, where).start())
 
     def arrivals(self):
         return [
@@ -411,82 +424,156 @@
             self.out(i).wait_send()
 
 
-class ChipScatter:
-    def __init__(self, st, g, rows, width):
-        self.st, self.g, self.rows, self.width = st, g, rows, width
+class GradScatter:
+    def __init__(self, st, shard, widths, sums):
         nc = self.nc = st.nd // 2
-        self.hm = st.scratch(VMEM((nc, rows, width), jnp.float32))
-        self.hc = [st.scratch(VMEM((nc - 1, rows, width), jnp.int16)) for _ in range(2)]
-        self.hk = [st.scratch(VMEM((nc - 1, 1, width), jnp.float32)) for _ in range(2)]
-        self.ht = [st.scratch(DMA((nc,))) for _ in range(2)]
-        self.hd = [st.scratch(DMA((2, nc - 1))) for _ in range(2)]
+        self.st, self.shard, self.widths = st, shard, widths
+        self.m = math.lcm(2 * shard, 128) // (2 * shard)
+        self.chunks = nc // self.m
+        wide = max(widths)
+        self.hg = st.scratch(VMEM((2, 2 * self.m * shard, wide), jnp.float32))
+        self.ht = st.scratch(VMEM((2, self.m, shard, wide), jnp.float32))
+        self.hs = st.scratch(VMEM((2, self.m, shard, wide), jnp.int16))
+        self.hk = st.scratch(VMEM((2, self.m, 1, wide), jnp.float32))
+        self.hcr = [st.scratch(VMEM((nc - 1, shard, w), jnp.int16)) for w in widths]
+        self.hkr = [st.scratch(VMEM((nc - 1, 1, w), jnp.float32)) for w in widths]
+        self.ha = sums
+        self.hgs = [st.scratch(DMA((2, self.m))) for _ in range(2)]
+        self.hss = st.scratch(DMA((2, 2, self.m)))
+        self.hsr = st.scratch(DMA((len(widths), 2, nc - 1)))
+        self.hf = st.scratch(pltpu.SemaphoreType.REGULAR)
         st.links |= {"chips", "twin"}
 
     def bind(self, get):
-        self.x, self.tw = get(self.g), get(self.hm)
-        (self.cs, self.cr), (self.sc, self.sr), (self.ts, self.tr), (self.ss, self.rs) = (
-            [get(h) for h in hs] for hs in (self.hc, self.hk, self.ht, self.hd)
+        self.g, self.t, self.cs, self.sc, self.ss, self.sr, self.free = (
+            get(h) for h in (self.hg, self.ht, self.hs, self.hk, self.hss, self.hsr, self.hf)
         )
-        self.d = lax.axis_index("dp")
-        self.core = lax.rem(self.d, 2)
+        self.cr, self.kr, self.acc = ([get(h) for h in hs] for hs in (self.hcr, self.hkr, self.ha))
+        self.gs, self.gr = (get(h) for h in self.hgs)
+        d = self.d = lax.axis_index("dp")
+        self.core, self.chip = lax.rem(d, 2), d // 2
+        self.twin = {"dp": d + 1 - 2 * self.core}
         return self
 
-    def at(self, i):
-        return pl.ds(pl.multiple_of(i * self.rows, self.rows), self.rows)
-
-    def chip(self, i):
-        return lax.rem(self.d // 2 + 1 + i, self.nc)
-
-    def gift(self, i):
-        twin = {"dp": self.d + 1 - 2 * self.core}
-        src = self.x.at[self.at(2 * self.chip(i) + 1 - self.core)]
-        return remote(src, self.tw.at[i], self.ts.at[i], self.tr.at[i], twin)
-
-    def sums(self, i):
-        where = {"dp": lax.rem(self.d + 2 * (i + 1), self.st.nd)}
+    def chunk(self, i):
+        return lax.rem(self.chip // self.m + 1 + i, self.chunks)
+
+    def half(self, e, core):
+        return pl.ds(pl.multiple_of((2 * e + core) * self.shard, self.shard), self.shard)
+
+    def gift(self, a, r, e):
+        cols = pl.ds(0, self.widths[a])
+        return remote(
+            self.g.at[r, self.half(e, 1 - self.core), cols], self.t.at[r, e, :, cols], self.gs.at[r, e], self.gr.at[r, e],
+            self.twin,
+        )
+
+    def sums(self, a, r, e, dest):
+        cols, nc = pl.ds(0, self.widths[a]), self.nc
+        slot = jnp.maximum(lax.rem(dest - self.chip + nc, nc) - 1, 0)
+        where = {"dp": 2 * dest + self.core}
         return (
-            remote(self.cs.at[i], self.cr.at[i], self.ss.at[0, i], self.rs.at[0, i], where),
-            remote(self.sc.at[i], self.sr.at[i], self.ss.at[1, i], self.rs.at[1, i], where),
+            remote(self.cs.at[r, e, :, cols], self.cr[a].at[slot], self.ss.at[0, r, e], self.sr.at[a, 0, slot], where),
+            remote(self.sc.at[r, e, :, cols], self.kr[a].at[slot], self.ss.at[1, r, e], self.sr.at[a, 1, slot], where),
         )
 
-    def give(self):
-        for i in range(self.nc):
-            self.gift(i).start()
-
-    def combine(self, i):
-        self.gift(i).wait_recv()
-        rows = self.at(2 * self.chip(i) + self.core)
-        over_cols(
-            self.width,
-            lambda cols: col_encode(self.x[rows, cols] + self.tw[i, :, cols], self.cs.at[i], self.sc.at[i], cols),
-        )
-        for c in self.sums(i):
-            c.start()
-
-    def combines(self):
-        return [functools.partial(self.combine, i) for i in range(self.nc - 1)]
-
-    def total(self, put):
+    def compute(self, a, i, pieces):
+        n = a * self.chunks + i
+        r = lax.rem(n, 2)
+        rows = 2 * self.m * self.shard
+
+        @pl.when(n >= 2)
+        def _():
+            for e in range(self.m):
+                self.gift(a, r, e).wait_send() if a == 0 else self._sent(a, i, r, e)
+            pl.semaphore_wait(self.free, 1)
+
+        cols = pl.ds(pl.multiple_of(self.chunk(i) * rows, 128), rows)
+        at = 0
+        for x, y in pieces:
+            z = y()
+            self.g[r, :, at : at + z.shape[1]] = tn_dot(x[:, cols], z)
+            at += z.shape[1]
+        for e in range(self.m):
+            self.gift(a, r, e).start()
+
+    def _sent(self, a, i, r, e):
+        pl.when(i >= 2)(lambda: self.gift(a, r, e).wait_send())
+        pl.when(i < 2)(lambda: self.gift(a - 1, r, e).wait_send())
+
+    def combine(self, a, i):
+        n = a * self.chunks + i
+        r = lax.rem(n, 2)
+        for e in range(self.m):
+            self.gift(a, r, e).wait_recv()
+            dest = self.chunk(i) * self.m + e
+            away = dest != self.chip
+
+            def past(b, j):
+                old = self.chunk(j) * self.m + e
+
+                @pl.when(old != self.chip)
+                def _():
+                    for c in self.sums(b, r, e, old):
+                        c.wait_send()
+
+            pl.when(i >= 2)(lambda: past(a, i - 2))
+            if a:
+                pl.when(i < 2)(lambda: past(a - 1, i - 2 + self.chunks))
+            own = self.half(e, self.core)
+
+            @pl.when(away)
+            def _():
+                over_cols(
+                    self.widths[a],
+                    lambda cols: col_encode(
+                        self.g[r, own, cols] + self.t[r, e, :, cols], self.cs.at[r, e], self.sc.at[r, e], cols
+                    ),
+                )
+                for c in self.sums(a, r, e, dest):
+                    c.start()
+
+            @pl.when(jnp.logical_not(away))
+            def _():
+                over_cols(self.widths[a], lambda cols: self._keep(a, r, e, own, cols))
+
+        @pl.when(n + 2 < len(self.widths) * self.chunks)
+        def _():
+            pl.semaphore_signal(self.free, inc=1, device_id=self.twin, device_id_type=MESH)
+
+    def _keep(self, a, r, e, own, cols):
+        self.acc[a][:, cols] = self.g[r, own, cols] + self.t[r, e, :, cols]
+
+    def slot(self, a, w, pieces):
+        pl.when(w < self.chunks)(lambda: self.compute(a, w, pieces))
+        pl.when((w >= 1) & (w <= self.chunks))(lambda: self.combine(a, w - 1))
+
+    def collect(self, a, put):
         n = self.nc - 1
-        self.gift(n).wait_recv()
         for i in range(n):
-            for c in self.sums(i):
+            for c in self.sums(a, 0, 0, lax.rem(self.chip + 1 + i, self.nc)):
                 c.wait_recv()
 
         def tile(cols):
-            x = self.x[self.at(self.d), cols] + self.tw[n, :, cols]
+            x = self.acc[a][:, cols]
             for i in range(n):
-                x = x + col_decode(self.cr.at[i], self.sr.at[i], cols)
+                x = x + col_decode(self.cr[a].at[i], self.kr[a].at[i], cols)
             put(cols, x)
 
-        over_cols(self.width, tile)
+        over_cols(self.widths[a], tile)
 
     def finish(self):
-        for i in range(self.nc):
-            self.gift(i).wait_send()
-        for i in range(self.nc - 1):
-            for c in self.sums(i):
-                c.wait_send()
+        a = len(self.widths) - 1
+        for i in range(max(0, self.chunks - 2), self.chunks):
+            r = (a * self.chunks + i) % 2
+            for e in range(self.m):
+                self.gift(a, r, e).wait_send()
+                dest = self.chunk(i) * self.m + e
+
+                @pl.when(dest != self.chip)
+                def _():
+                    for c in self.sums(a, r, e, dest):
+                        c.wait_send()
 
 
 class FullSum:
@@ -597,84 +684,117 @@
     return s, (key >= across(begin, group)) & (key <= own)
 
 
-def attention_stage(nd, nt, tokens, attn_gain, ffn_gain, out_grad, begin, cosine, sine, w_attn, w_gate, w_up, w_down_t, heads):
-    st = Fused("attend", 1, nd, nt)
+def layer(
+    nd, nt, tokens, attn_gain, ffn_gain, out_grad, begin, cosine, sine, w_attn, w_gate, w_up, w_down_t, heads
+):
+    st = Fused("layer", 1, nd, nt)
     low, f32 = jnp.bfloat16, jnp.float32
     own, width = tokens.shape
     span = own * nt
-    shard = w_attn.shape[0]
+    shard, units = w_gate.shape
     n_q, n_kv = heads
     group = n_q // n_kv
     tiles = span // 128
     qw, kvw = n_q * HD, n_kv * HD
+    qkvw = qw + 2 * kvw
     reach = 2 * span + 128
     parts = 2
     piece = own // parts
+    scale = 1.0 / math.sqrt(HD)
 
     h_tok, h_g1, h_g2 = st.inp(tokens), st.inp(attn_gain[None]), st.inp(ffn_gain[None])
     h_og, h_begin = st.inp(out_grad), st.inp(begin)
     h_cos, h_sin = st.inp(cosine), st.inp(sine)
-    h_wa, h_wg, h_wu, h_wd = st.inp(w_attn), st.inp(w_gate), st.inp(w_up), st.inp(w_down_t)
-
-    o_h1, o_h2, o_gr = (st.out((span, width), low) for _ in range(3))
-    o_wa = st.out((nd * shard, w_attn.shape[1]), low)
-    o_wg, o_wu, o_wd = (st.out((nd * shard, w.shape[1]), low, pl.ANY) for w in (w_gate, w_up, w_down_t))
-    o_q = st.out((n_kv, tiles, group * 128, 128), low)
-    o_k, o_v = (st.out((n_kv, 3 * span, 128), low) for _ in range(2))
-    o_kt = st.out((n_kv, 128, 3 * span), low)
-    o_ctx = st.out((span, qw), low)
-    o_ch = st.out((n_kv, tiles, group * 128, 128), low)
-    o_lse = st.out((n_kv, tiles, 1, group * 128), f32)
-    o_res = st.out((own, width), f32)
-
-    h_win = st.scratch(VMEM((3, span, 2 * kvw), low))
-    h_ks = st.scratch(DMA((2,)))
-    h_kr = st.scratch(DMA((2,)))
-    h_vt = st.scratch(VMEM((n_kv, 128, 3 * span), low))
-    h_part = st.scratch(VMEM((span, width), f32))
-
-    ag1 = LineGather(st, o_h1, own, parts)
-    ag2 = LineGather(st, o_h2, own, parts)
-    ag3 = LineGather(st, o_gr, own, parts)
-    rs1 = LineScatter(st, h_part, own, width, parts)
-    wa = ChipGather(st, h_wa, o_wa, shard)
-    wg = ChipGather(st, h_wg, o_wg, shard)
-    wu = ChipGather(st, h_wu, o_wu, shard)
-    wd = ChipGather(st, h_wd, o_wd, shard)
+    s_wa, s_wg, s_wu, s_wd = (st.inp(w, pl.ANY) for w in (w_attn, w_gate, w_up, w_down_t))
+
+    o_out = st.out((own, width), low)
+    o_tg = st.out((own, width), f32)
+    o_gains = st.out((1, 2 * width), f32)
+    o_dd = st.out((units, shard), f32)
+    o_dg, o_du = (st.out((shard, units), f32) for _ in range(2))
+    o_da = st.out((shard, qkvw + qw), f32)
+
+    def room(shape, dtype=f32):
+        return st.scratch(VMEM(shape, dtype))
+
+    h_h1, h_h2, h_gr, h_rl = (room((span, width), low) for _ in range(4))
+    h_wa = room((width, qkvw + qw), low)
+    h_wg, h_wu, h_wd = (room((width, units), low) for _ in range(3))
+    h_q, h_dc, h_ch = (room((n_kv, tiles, group * 128, 128), low) for _ in range(3))
+    h_k, h_v = (room((n_kv, 3 * span, 128), low) for _ in range(2))
+    h_kt, h_vt = (room((n_kv, 128, 3 * span), low) for _ in range(2))
+    h_win = room((3, span, 2 * kvw), low)
+    h_ctx = room((span, qw), low)
+    h_lse, h_delta = (room((n_kv, tiles, 1, group * 128)) for _ in range(2))
+    h_res, h_rg = (room((own, width)) for _ in range(2))
+    h_part = room((span, width))
+    h_ia, h_gl, h_ul = (room((span, units), low) for _ in range(3))
+    h_dq = room((n_kv, tiles, group * 128, 128))
+    h_dk, h_dv = (room((n_kv, 3 * span, 128)) for _ in range(2))
+    h_kvs, h_kvr = (room((2, span, 2 * kvw), jnp.int16) for _ in range(2))
+    h_kss, h_ksr = (room((2, tiles, 1, 2 * kvw)) for _ in range(2))
+    h_mine = room((1, 2 * width))
+    h_fs, h_fr = (st.scratch(DMA((2,))) for _ in range(2))
+    h_bs, h_br = (st.scratch(DMA((2, 2))) for _ in range(2))
+    h_ready = st.scratch(pltpu.SemaphoreType.REGULAR)
+
+    ag1 = LineGather(st, h_h1, own, parts)
+    ag2 = LineGather(st, h_h2, own, parts)
+    ag3 = LineGather(st, h_gr, own, parts)
+    ag4 = LineGather(st, h_rl, own, parts)
+    rs = LineScatter(st, h_part, own, width, parts)
+    wa = ChipGather(st, s_wa, h_wa, shard)
+    wg = ChipGather(st, s_wg, h_wg, shard)
+    wu = ChipGather(st, s_wu, h_wu, shard)
+    wd = ChipGather(st, s_wd, h_wd, shard)
+    gs = GradScatter(st, shard, (units, units, units, qkvw + qw), (room((shard, units)), o_dg, o_du, o_da))
+    full = FullSum(st, h_mine, o_gains, (1, 2 * width))
     st.links.add("near")
 
     def fn(get):
         d, t = lax.axis_index("dp"), lax.axis_index("tp")
-        for x in (ag1, ag2, ag3, rs1, wa, wg, wu, wd):
+        for x in (ag1, ag2, ag3, ag4, rs, wa, wg, wu, wd, gs):
             x.bind(get)
-        tok, g1, g2, h1, h2 = get(h_tok), get(h_g1), get(h_g2), get(o_h1), get(o_h2)
-        wa_ref, win, q, k, v, kt, vt, ch = (get(h) for h in (o_wa, h_win, o_q, o_k, o_v, o_kt, h_vt, o_ch))
-        ctx, lse, res, part = get(o_ctx), get(o_lse), get(o_res), get(h_part)
-        cos_ref, sin_ref, begin_ref = get(h_cos), get(h_sin), get(h_begin)
+        tok, g1, g2, og, begin_ref, cos_ref, sin_ref = (get(h) for h in (h_tok, h_g1, h_g2, h_og, h_begin, h_cos, h_sin))
+        h1, h2, gr, rl = (get(h) for h in (h_h1, h_h2, h_gr, h_rl))
+        wa_ref, wg_ref, wu_ref, wd_ref = (get(h) for h in (h_wa, h_wg, h_wu, h_wd))
+        q, k, v, kt, vt, win, ctx, ch, lse = (get(h) for h in (h_q, h_k, h_v, h_kt, h_vt, h_win, h_ctx, h_ch, h_lse))
+        dc, delta, dq, dk, dv = (get(h) for h in (h_dc, h_delta, h_dq, h_dk, h_dv))
+        res, rg, part, ia, gl, ul, mine = (get(h) for h in (h_res, h_rg, h_part, h_ia, h_gl, h_ul, h_mine))
+        xl = ul.at[:, pl.ds(0, qkvw)]
+        kvs, kvr, kss, ksr, fs, fr, bs, br = (
+            get(h) for h in (h_kvs, h_kvr, h_kss, h_ksr, h_fs, h_fr, h_bs, h_br)
+        )
+
+        def own_rows(p, r, n=16):
+            return pl.ds(pl.multiple_of(t * own + p * piece + r, n), n)
+
+        def rows_of(j):
+            return pl.ds(pl.multiple_of(j * own, own), own)
 
         wa.start()
-
-        def first_norm(p):
+        for p in range(parts):
+
             def tile(r):
                 x = tok[pl.ds(p * piece + r, 16), :].astype(f32)
-                at = pl.ds(pl.multiple_of(t * own + p * piece + r, 16), 16)
-                h1[at, :] = (x * inverse_rms(x) * g1[...]).astype(low)
+                h1[own_rows(p, r), :] = (x * inverse_rms(x) * g1[...]).astype(low)
 
             per_tile(piece // 16, 16, tile)
-
-        for p in range(parts):
-            first_norm(p)
             ag1.start(p)
-        get(o_gr)[pl.ds(pl.multiple_of(t * own, own), own), :] = get(h_og)[...]
+        gr[rows_of(t), :] = og[...]
         in_turn(ag1.arrivals(), wa.forwards())
         for p in range(parts):
             ag3.start(p)
         wa.arrived()
 
+        def turn_rows(x, rows, way):
+            cosine, sine = across(cos_ref[rows, :], 2), across(sin_ref[rows, :], 2)
+            lane = lax.broadcasted_iota(jnp.int32, x.shape, 1)
+            return jnp.where(lane < qw + kvw, turned(x, cosine, way * sine), x)
+
         def project(r):
             rows = pl.ds(r, 128)
-            x = dot(h1[rows, :], wa_ref[:, : qw + 2 * kvw])
-            x = turned(x, cos_ref[rows, :], sin_ref[rows, :])
+            x = turn_rows(dot(h1[rows, :], wa_ref[:, :qkvw]), rows, 1.0)
             for h in range(n_q):
                 q[h // group, r // 128, h % group * 128 : (h % group + 1) * 128, :] = lane_take(x, h * HD).astype(low)
             win[2, rows, :] = x[:, qw:].astype(low)
@@ -682,7 +802,7 @@
         per_tile(tiles, 128, project)
 
         def ahead(i):
-            return remote(win.at[2], win.at[2 - i], get(h_ks).at[i - 1], get(h_kr).at[i - 1], {"dp": d + i})
+            return remote(win.at[2], win.at[2 - i], fs.at[i - 1], fr.at[i - 1], {"dp": d + i})
 
         for i in (2, 1):
             when(d + i < nd, lambda: ahead(i).start())
@@ -747,228 +867,115 @@
         per_tile(tiles, 128, pack)
 
         def out_rows(j):
-            rows = pl.ds(pl.multiple_of(j * own, own), own)
             for c in range(0, width, 512):
-                part[rows, c : c + 512] = nt_dot(ctx[rows, :], wa_ref[c : c + 512, qw + 2 * kvw :])
-
-        rs1.relay(0, out_rows)
+                part[rows_of(j), c : c + 512] = nt_dot(ctx[rows_of(j), :], wa_ref[c : c + 512, qkvw:])
+
+        rs.relay(0, out_rows)
         in_turn(wd.forwards(), wg.forwards())
         wu.start()
         out_rows(t)
 
-        def second_norm(p):
+        for p in range(parts):
+
             def put(r, x):
                 at = pl.ds(p * piece + r, 16)
                 x = x + tok[at, :].astype(f32)
                 res[at, :] = x
-                rows = pl.ds(pl.multiple_of(t * own + p * piece + r, 16), 16)
-                h2[rows, :] = (x * inverse_rms(x) * g2[...]).astype(low)
-
-            rs1.total(p, put)
+                h2[own_rows(p, r), :] = (x * inverse_rms(x) * g2[...]).astype(low)
+
+            if p:
+                rs.relay(p)
+            rs.total(p, put)
             ag2.start(p)
-
-        for p in range(parts):
-            if p:
-                rs1.relay(p)
-            second_norm(p)
-        in_turn(ag2.arrivals(), wu.forwards())
-        for x in (wd, wg, wu):
-            x.arrived()
-        for x in (ag1, ag2, ag3, rs1, wa, wg, wu, wd):
-            x.finish()
-        for i in (2, 1):
-            when(d + i < nd, lambda: ahead(i).wait_send())
-
-    st.body(fn)
-    return st.run()
-
-
-def ffn_stage(nd, nt, hidden2, grad_rows, w_gate, w_up, w_down_t, residual, ffn_gain, out_grad):
-    st = Fused("ffn", 2, nd, nt)
-    low, f32 = jnp.bfloat16, jnp.float32
-    span, width = hidden2.shape
-    own = span // nt
-    units = w_gate.shape[1]
-    shard = width // nd
-    parts = 2
-    piece = own // parts
-    tile_u = 256
-
-    h_h2, h_gr, h_wg, h_wu, h_wd = (st.inp(x) for x in (hidden2, grad_rows, w_gate, w_up, w_down_t))
-    h_res, h_gain, h_og = st.inp(residual), st.inp(ffn_gain[None]), st.inp(out_grad)
-    o_ia = st.out((span, units), low)
-    o_rl = st.out((span, width), low)
-    o_rg = st.out((own, width), f32)
-    o_fg = st.out((1, width), f32)
-    o_dd = st.out((units, shard), f32)
-    o_dg, o_du = (st.out((shard, units), f32) for _ in range(2))
-    h_gl, h_ul = (st.scratch(VMEM((span, units), low)) for _ in range(2))
-    h_part = st.scratch(VMEM((span, width), f32))
-    h_ga, h_gb = (st.scratch(VMEM((width, units), f32)) for _ in range(2))
-    rs = LineScatter(st, h_part, own, width, parts)
-    ag = LineGather(st, o_rl, own, parts)
-    sd, sg, su = ChipScatter(st, h_ga, shard, units), ChipScatter(st, h_gb, shard, units), ChipScatter(st, h_ga, shard, units)
-
-    def fn(get):
-        t = lax.axis_index("tp")
-        for x in (rs, ag, sd, sg, su):
-            x.bind(get)
-        h2, gr, wg, wu, wd, res, gain, og = (get(h) for h in (h_h2, h_gr, h_wg, h_wu, h_wd, h_res, h_gain, h_og))
-        ia, rl, rg, fg, gl, ul, part, ga, gb = (get(h) for h in (o_ia, o_rl, o_rg, o_fg, h_gl, h_ul, h_part, h_ga, h_gb))
+        rs.finish()
+        wd.arrived()
+
+        def back_act(c):
+            part[:, pl.ds(c, 256)] = dot(gr[...], wd_ref[:, pl.ds(c, 256)])
+
+        arrive2 = ag2.arrivals()
+        for x in arrive2[:parts]:
+            x()
+        per_tile(units // 256, 256, back_act)
+        in_turn(arrive2[parts:], wu.forwards())
+        wg.arrived()
+        wu.arrived()
 
         def act(c):
-            cols = pl.ds(c, tile_u)
-            gate = dot(h2[...], wg[:, cols])
-            up = dot(h2[...], wu[:, cols])
-            back = dot(gr[...], wd[:, cols])
+            cols = pl.ds(c, 256)
+            gate = dot(h2[...], wg_ref[:, cols])
+            up = dot(h2[...], wu_ref[:, cols])
+            back = part[:, cols]
             sig = jax.nn.sigmoid(gate)
             ia[:, cols] = (gate * sig * up).astype(low)
             gl[:, cols] = (back * up * (sig * (1.0 + gate * (1.0 - sig)))).astype(low)
             ul[:, cols] = (back * gate * sig).astype(low)
 
-        per_tile(units // tile_u, tile_u, act)
+        per_tile(units // 256, 256, act)
 
         def rows_back(j):
-            rows = pl.ds(pl.multiple_of(j * own, own), own)
+            rows = rows_of(j)
             for c in range(0, width, 512):
-                part[rows, c : c + 512] = nt_dot(gl[rows, :], wg[c : c + 512, :]) + nt_dot(ul[rows, :], wu[c : c + 512, :])
-
-        blocks_w = width // 256
-
-        def weight_part(dst, x, y, v):
-            @pl.when(v < blocks_w)
-            def _():
-                cols = pl.ds(pl.multiple_of(v * 256, 256), 256)
-                dst[cols, :] = tn_dot(x[:, cols], y[...])
+                part[rows, c : c + 512] = nt_dot(gl[rows, :], wg_ref[c : c + 512, :]) + nt_dot(
+                    ul[rows, :], wu_ref[c : c + 512, :]
+                )
 
         n = rs.slots()
-        rs.relay(0, rows_back, lambda v: weight_part(ga, gr, ia, v))
-        per_tile(max(0, blocks_w - n), 256, lambda r: weight_part(ga, gr, ia, n + r // 256))
-        sd.give()
+        last_slot = gs.chunks + 1
+        grads = (
+            ((gr, lambda: ia[...]),),
+            ((h2, lambda: gl[...]),),
+            ((h2, lambda: ul[...]),),
+            ((h1, lambda: xl[...]), (rl, lambda: ctx[...])),
+        )
+
+        def beside(a, shift=0):
+            every = max(1, n // last_slot)
+
+            def go(w):
+                w = w - shift
+                pl.when((lax.rem(w, every) == 0) & (w < every * last_slot))(lambda: gs.slot(a, w // every, grads[a]))
+
+            return go
+
+        rs.relay(0, rows_back, beside(0))
         rows_back(t)
-        fg[...] = jnp.zeros_like(fg)
-
-        def joined(p):
+        mine[...] = jnp.zeros_like(mine)
+
+        for p in range(parts):
+
             def put(r, x):
                 at = pl.ds(p * piece + r, 16)
                 y = res[at, :]
                 inverse = inverse_rms(y)
                 normed = y * inverse
-                fg[...] += jnp.sum(x * normed, axis=0, keepdims=True)
-                e = x * gain[...]
+                mine[:, width:] += jnp.sum(x * normed, axis=0, keepdims=True)
+                e = x * g2[...]
                 back = inverse * (e - normed * jnp.mean(e * normed, axis=-1, keepdims=True))
                 y = og[at, :].astype(f32) + back
                 rg[at, :] = y
-                rl[pl.ds(pl.multiple_of(t * own + p * piece + r, 16), 16), :] = y.astype(low)
-
+                rl[own_rows(p, r), :] = y.astype(low)
+
+            if p:
+                rs.relay(p, None, beside(p, p * n))
             rs.total(p, put)
-            ag.start(p)
-
-        joined(0)
-        rs.relay(1, None, lambda v: weight_part(gb, h2, gl, v - n))
-        per_tile(max(0, blocks_w - n), 256, lambda r: weight_part(gb, h2, gl, n + r // 256))
-        sg.give()
-        joined(1)
-        arrivals = ag.arrivals()
-        for x in sd.combines():
-            x()
-        for i in range(st.nd // 2):
-            sd.gift(i).wait_send()
-        for x in arrivals[:2]:
-            x()
-
-        def put_down(cols, x):
-            get(o_dd)[cols, :] = x.T
-
-        in_turn(sg.combines(), arrivals[2:])
-        sd.total(put_down)
-        per_tile(blocks_w, 256, lambda r: weight_part(ga, h2, ul, r // 256))
-        su.give()
-
-        def put_gate(cols, x):
-            get(o_dg)[:, cols] = x
-
-        def put_up(cols, x):
-            get(o_du)[:, cols] = x
-
-        for x in su.combines():
-            x()
-        sg.total(put_gate)
-        su.total(put_up)
-        for i in range(st.nd // 2 - 1):
-            for c in sd.sums(i):
-                c.wait_send()
-        sg.finish()
-        su.finish()
+            ag4.start(p)
         rs.finish()
-        ag.finish()
-
-    st.body(fn)
-    return st.run()
-
-
-def back_stage(
-    nd, nt, tokens, attn_gain, begin, cosine, sine, w_attn, w_down_t, inner_act, residual, residual_rows, residual_grad,
-    ffn_part_sum, hidden1, queries, keys, values, keys_t, context, context_heads, log_total, heads,
-):
-    st = Fused("back", 3, nd, nt)
-    low, f32 = jnp.bfloat16, jnp.float32
-    own, width = tokens.shape
-    span = own * nt
-    shard = width // nd
-    units = inner_act.shape[1]
-    n_q, n_kv = heads
-    group = n_q // n_kv
-    tiles = span // 128
-    qw, kvw = n_q * HD, n_kv * HD
-    qkvw = qw + 2 * kvw
-    reach = 2 * span + 128
-    parts = 2
-    piece = own // parts
-
-    h_tok, h_gain, h_begin, h_cos, h_sin = (st.inp(x) for x in (tokens, attn_gain[None], begin, cosine, sine))
-    h_wa, h_wd, h_ia, h_res, h_rl, h_rg = (
-        st.inp(x) for x in (w_attn, w_down_t, inner_act, residual, residual_rows, residual_grad)
-    )
-    h_fg, h_h1, h_q, h_k, h_v, h_kt, h_ctx, h_ch, h_lse = (
-        st.inp(x)
-        for x in (ffn_part_sum, hidden1, queries, keys, values, keys_t, context, context_heads, log_total)
-    )
-    o_out = st.out((own, width), low)
-    o_tg = st.out((own, width), f32)
-    o_gains = st.out((1, 2 * width), f32)
-    o_sum = st.out((shard, qkvw + qw), f32)
-    h_fp = h_part = st.scratch(VMEM((span, width), f32))
-    h_dc = st.scratch(VMEM((n_kv, tiles, group * 128, 128), low))
-    h_delta = st.scratch(VMEM((n_kv, tiles, 1, group * 128), f32))
-    h_dq = st.scratch(VMEM((n_kv, tiles, group * 128, 128), f32))
-    h_dk, h_dv = (st.scratch(VMEM((n_kv, 3 * span, 128), f32)) for _ in range(2))
-    h_kvs, h_kvr = (st.scratch(VMEM((2, span, 2 * kvw), jnp.int16)) for _ in range(2))
-    h_kss, h_ksr = (st.scratch(VMEM((2, tiles, 1, 2 * kvw), f32)) for _ in range(2))
-    h_kd = [st.scratch(DMA((2, 2))) for _ in range(2)]
-    h_low = st.scratch(VMEM((span, qkvw), low))
-    h_g = st.scratch(VMEM((width, qkvw + qw), f32))
-    h_mine = st.scratch(VMEM((1, 2 * width), f32))
-    rf = LineScatter(st, h_fp, own, width, parts)
-    rs = LineScatter(st, h_part, own, width, parts)
-    sa = ChipScatter(st, h_g, shard, qkvw + qw)
-    full = FullSum(st, h_mine, o_gains, (1, 2 * width))
-    st.links.add("near")
-
-    def fn(get):
-        d, t = lax.axis_index("dp"), lax.axis_index("tp")
-        for x in (rf, rs, sa):
-            x.bind(get)
-        tok, gain, begin_ref, cos_ref, sin_ref = (get(h) for h in (h_tok, h_gain, h_begin, h_cos, h_sin))
-        wa, wd, ia, res, rl, rg = (get(h) for h in (h_wa, h_wd, h_ia, h_res, h_rl, h_rg))
-        h1, q, k, v, kt, ctx, ch, lse = (get(h) for h in (h_h1, h_q, h_k, h_v, h_kt, h_ctx, h_ch, h_lse))
-        fp, part, dc, delta, dq, dk, dv = (get(h) for h in (h_fp, h_part, h_dc, h_delta, h_dq, h_dk, h_dv))
-        kvs, kvr, kss, ksr, (ks, kr) = get(h_kvs), get(h_kvr), get(h_kss), get(h_ksr), (get(h) for h in h_kd)
-        xl, gw, mine = get(h_low), get(h_g), get(h_mine)
+
+        def ffn_rows(r):
+            cols = pl.ds(r, 512)
+            part[:, cols] = nt_dot(ia[...], wd_ref[cols, :])
+
+        def while_gathered(w, _):
+            ag4.arrive_at(w)
+            pl.when(w < width // 512)(lambda: ffn_rows(pl.multiple_of(w * 512, 512)))
+            gs.slot(2, w, grads[2])
+            return 0
+
+        lax.fori_loop(0, max((nt - 1) * parts, last_slot, width // 512), while_gathered, 0)
 
         def context_back(r):
-            rows = pl.ds(r, 128)
-            x = dot(rl[rows, :], wa[:, qkvw:])
+            x = dot(rl[pl.ds(r, 128), :], wa_ref[:, qkvw:])
             i = r // 128
             for h in range(n_q):
                 g, at = h // group, pl.ds(h % group * 128, 128)
@@ -978,21 +985,15 @@
                 delta[g, i, :, at] = jnp.sum(z.T, axis=0, keepdims=True)
 
         per_tile(tiles, 128, context_back)
-
-        def ffn_rows(r):
-            cols = pl.ds(r, 512)
-            fp[:, cols] = nt_dot(ia[...], wd[cols, :])
-
-        per_tile(width // 512, 512, ffn_rows)
         dk[...] = jnp.zeros_like(dk)
         dv[...] = jnp.zeros_like(dv)
         count = n_kv * tiles
-        slots = rf.slots() * parts
+        slots = n * parts
         per = -(-slots // count)
 
-        def attend(u, _):
+        def attend_back(u, _):
             def pump(w, _):
-                pl.when(w < slots)(lambda: rf.step(w))
+                pl.when(w < slots)(lambda: rs.step(w))
                 return 0
 
             lax.fori_loop(u * per, u * per + per, pump, 0)
@@ -1008,8 +1009,7 @@
             dq[g, i] = dot(kt[g, :, keys], ds).T
             return 0
 
-        lax.fori_loop(0, count, attend, 0)
-        scale = 1.0 / math.sqrt(HD)
+        lax.fori_loop(0, count, attend_back, 0)
 
         def kv_rows(b, r):
             at = pl.ds(pl.multiple_of(b * span + r, 128), 128)
@@ -1019,11 +1019,11 @@
                 x = x + lane_place(dv[g, at, :], kvw + g * HD, 2 * kvw)
             return x
 
-        def back(i):
+        def behind(i):
             where = {"dp": d - i}
             return (
-                remote(kvs.at[i - 1], kvr.at[i - 1], ks.at[0, i - 1], kr.at[0, i - 1], where),
-                remote(kss.at[i - 1], ksr.at[i - 1], ks.at[1, i - 1], kr.at[1, i - 1], where),
+                remote(kvs.at[i - 1], kvr.at[i - 1], bs.at[0, i - 1], br.at[0, i - 1], where),
+                remote(kss.at[i - 1], ksr.at[i - 1], bs.at[1, i - 1], br.at[1, i - 1], where),
             )
 
         for i in (2, 1):
@@ -1031,11 +1031,11 @@
             @pl.when(d >= i)
             def _():
                 def tile(r):
-                    x = kv_rows(2 - i, r)
-                    col_encode(x, kvs.at[i - 1, pl.ds(r, 128)], kss.at[i - 1, r // 128], slice(None))
+                    at = kvs.at[i - 1, pl.ds(r, 128)]
+                    col_encode(kv_rows(2 - i, r), at, kss.at[i - 1, r // 128], slice(None))
 
                 per_tile(tiles, 128, tile)
-                for c in back(i):
+                for c in behind(i):
                     c.start()
 
         def query_rows(r):
@@ -1045,31 +1045,30 @@
                 at = h % group * 128
                 x = x + lane_place(dq[h // group, r // 128, at : at + 128, :] * scale, h * HD, qw)
             pad = jnp.zeros((128, 2 * kvw), f32)
-            x = turned(jnp.concatenate([x, pad], axis=1), cos_ref[rows, :], -sin_ref[rows, :])
-            xl[rows, :] = x.astype(low)
+            xl[rows, :] = turn_rows(jnp.concatenate([x, pad], axis=1), rows, -1.0).astype(low)
 
         per_tile(tiles, 128, query_rows)
-
-        def put_out(p):
+        for p in range(parts):
+
             def put(r, x):
                 at = pl.ds(p * piece + r, 16)
                 get(o_out)[at, :] = (res[at, :] + x).astype(low)
 
-            rf.total(p, put)
-
-        for p in range(parts):
-            put_out(p)
-
-        def weight_q(r):
-            cols = pl.ds(r, 256)
-            gw[cols, qkvw:] = tn_dot(rl[:, cols], ctx[...])
-
-        per_tile(width // 256, 256, weight_q)
+            rs.total(p, put)
+        rs.finish()
+        ready = get(h_ready)
+        for ok, where in ((t > 0, t - 1), (t < nt - 1, t + 1)):
+            when(ok, lambda: pl.semaphore_signal(ready, inc=1, device_id={"tp": where}, device_id_type=MESH))
+
+        def put_down(cols, x):
+            get(o_dd)[cols, :] = x.T
+
+        gs.collect(0, put_down)
         for i in (1, 2):
 
             @pl.when(d + i < nd)
             def _():
-                for c in back(i):
+                for c in behind(i):
                     c.wait_recv()
 
         near1, near2 = d + 1 < nd, d + 2 < nd
@@ -1081,65 +1080,56 @@
             b = col_decode(kvr.at[1, rows], ksr.at[1, r // 128], slice(None))
             x = x + jnp.where(near1, a, 0.0) + jnp.where(near2, b, 0.0)
             pad = jnp.zeros((128, qw), f32)
-            x = turned(jnp.concatenate([pad, x], axis=1), cos_ref[rows, :], -sin_ref[rows, :])
+            x = turn_rows(jnp.concatenate([pad, x], axis=1), rows, -1.0)
             xl[rows, qw:] = x[:, qw:].astype(low)
 
         per_tile(tiles, 128, kv_total)
 
         def hidden_rows(j):
-            rows = pl.ds(pl.multiple_of(j * own, own), own)
             for c in range(0, width, 512):
-                part[rows, c : c + 512] = nt_dot(xl[rows, :], wa[c : c + 512, :qkvw])
-
-        blocks_w = width // 256
-
-        def weight_part(v):
-            @pl.when(v < blocks_w)
-            def _():
-                cols = pl.ds(pl.multiple_of(v * 256, 256), 256)
-                gw[cols, :qkvw] = tn_dot(h1[:, cols], xl[...])
-
-        n = rs.slots()
-        rs.relay(0, hidden_rows, weight_part)
-        per_tile(max(0, blocks_w - n), 256, lambda r: weight_part(n + r // 256))
-        sa.give()
+                part[rows_of(j), c : c + 512] = nt_dot(xl[rows_of(j), :], wa_ref[c : c + 512, :qkvw])
+
+        pl.semaphore_wait(ready, (t > 0).astype(jnp.int32) + (t < nt - 1).astype(jnp.int32))
+        rs.relay(0, hidden_rows, beside(3))
         hidden_rows(t)
-        mine[...] = jnp.zeros_like(mine)
-        mine[:, width:] = get(h_fg)[...]
-
-        def last(p):
+
+        def put_gate(cols, x):
+            get(o_dg)[:, cols] = x
+
+        def put_up(cols, x):
+            get(o_du)[:, cols] = x
+
+        def put_attn(cols, x):
+            get(o_da)[:, cols] = x
+
+        for p in range(parts):
+
             def put(r, x):
                 at = pl.ds(p * piece + r, 16)
                 y = tok[at, :].astype(f32)
                 inverse = inverse_rms(y)
                 normed = y * inverse
                 mine[:, :width] += jnp.sum(x * normed, axis=0, keepdims=True)
-                e = x * gain[...]
+                e = x * g1[...]
                 e = inverse * (e - normed * jnp.mean(e * normed, axis=-1, keepdims=True))
                 get(o_tg)[at, :] = rg[at, :] + e
 
+            if p:
+                rs.relay(p)
+            else:
+                gs.collect(1, put_gate)
+                gs.collect(2, put_up)
             rs.total(p, put)
-
-        combines = sa.combines()
-        combines[0]()
-        last(0)
-        for x in combines[1:]:
-            x()
-        rs.relay(1)
-        last(1)
         full.run(get)
-
-        def put_sum(cols, x):
-            get(o_sum)[:, cols] = x
-
-        sa.total(put_sum)
-        for x in (rf, rs, sa):
+        gs.collect(3, put_attn)
+        for x in (ag1, ag2, ag3, ag4, rs, wa, wg, wu, wd, gs):
             x.finish()
         for i in (2, 1):
+            when(d + i < nd, lambda: ahead(i).wait_send())
 
             @pl.when(d >= i)
             def _():
-                for c in back(i):
+                for c in behind(i):
                     c.wait_send()
 
     st.body(fn)
@@ -1167,20 +1157,11 @@
     w_attn = jnp.concatenate([w_query, w_key, w_value, w_out.T], axis=1)
     w_down_t = w_down.T
     cosine, sine = rope_tables(positions, HD)
-    turn = heads[0] + heads[1]
-    still = jnp.ones((span, kvw), jnp.float32)
-    cosine = jnp.concatenate([jnp.tile(cosine, (1, 2 * turn)), still], axis=1)
-    sine = jnp.concatenate([jnp.tile(jnp.concatenate([-sine, sine], axis=1), (1, turn)), 0.0 * still], axis=1)
+    cosine = jnp.tile(cosine, (1, 2 * heads[0]))
+    sine = jnp.tile(jnp.concatenate([-sine, sine], axis=1), (1, heads[0]))
     begin = (2 * span + jnp.arange(span, dtype=jnp.int32) - positions)[None]
-    (hidden1, hidden2, grad_rows, attn_full, gate_full, up_full, down_full_t, queries, keys, values, keys_t, context, context_heads, log_total, residual) = (
-        attention_stage(nd, nt, tokens, attn_gain, ffn_gain, out_grad, begin, cosine, sine, w_attn, w_gate, w_up, w_down_t, heads)
-    )
-    inner_act, residual_rows, residual_grad, ffn_gain_part, down_sum, gate_sum, up_sum = ffn_stage(
-        nd, nt, hidden2, grad_rows, gate_full, up_full, down_full_t, residual, ffn_gain, out_grad
-    )
-    output, tokens_grad, gains, attn_sum = back_stage(
-        nd, nt, tokens, attn_gain, begin, cosine, sine, attn_full, down_full_t, inner_act, residual, residual_rows,
-        residual_grad, ffn_gain_part, hidden1, queries, keys, values, keys_t, context, context_heads, log_total, heads,
+    output, tokens_grad, gains, down_sum, gate_sum, up_sum, attn_sum = layer(
+        nd, nt, tokens, attn_gain, ffn_gain, out_grad, begin, cosine, sine, w_attn, w_gate, w_up, w_down_t, heads
     )
     cuts = (qw, qw + kvw, qw + 2 * kvw)
     return (

time: 384 us -> 351 us (0.914)
  Pallas kernels: 362 us -> 331 us
    pallas_call x3 -> x1, Pallas kernels: 362 us -> 331 us  [run(): pl.pallas_call(kernel, out_shape=[jax.ShapeDtypeStruct(s, t) for s, t, _...]
    unnamed x15 -> x29, local copies, waits for them, and re-layouts: 4.6 us -> 7.95 us
where the time goes in v3:
time: 351 us; the launch traced here: 350 us
  Pallas kernels  331 us (94%)
  local copies, waits for them, and re-layouts  17.6 us (5%)
    pallas_call x1, Pallas kernels, run(): pl.pallas_call(kernel, out_shape=[jax.ShapeDtypeStruct(s, t) for s, t, _...  331 us
    unnamed x29, local copies, waits for them, and re-layouts  7.95 us

profile of v3, /device:TPU:1, one launch (start us, length us, event | category | flops | bytes accessed | tf_op | source)
XLA Modules:
  0.0 350.2 jit_solution(8147072029970632074)
XLA Ops:
  0.7 0.6 copy-done.11
  1.3 0.6 fusion.2
  1.9 0.0 copy-done.9
  1.9 0.6 broadcast_in_dim.11.refs_1_
  2.5 0.1 copy-done.10
  2.6 0.6 broadcast_in_dim.12.refs_2_
  3.2 0.4 fusion
  3.6 0.0 copy-start.5
  3.6 0.0 copy-start.6
  3.7 0.0 copy-start.7
  3.7 0.4 copy-done.8
  4.1 0.5 copy-done.5
  4.6 0.1 copy-done.6
  4.6 0.1 copy-done.7
  4.7 0.9 concatenate.7.refs_7_
  5.6 0.1 tile.20
  5.7 1.2 copy.25.refs_6_
  6.8 0.1 tile.8
  6.9 1.2 copy.24.refs_5_
  8.1 330.8 %layer.1 = (bf16[128,1536]{1,0:T(8,128)(2,1)}, f32[128,1536]{1,0:T(8,128)}, f32[1,3072]{1,0:T(1,128)}, f32[1024,192]{1,0:T(8,128)}, f32[192,1024]{1,0:T(8,128)},...) custom-call(bf16[128,1536]{1,0:T(8,128)(2,1)} %refs_0_.1, f32[1,1536]{1,0:T(1,128)} %broadcast_in_dim.11.refs_1_, ...), custom_call_target="tpu_custom_call" | custom-call | tf_op jit(solution)/shard_map/layer/pallas_call | solution.py:100
  338.8 1.4 slice_reduce_fusion
  340.3 1.8 fusion.1
  342.1 1.9 slice_bitcast_fusion
  344.0 0.0 copy-done
  344.0 1.2 copy.26
  345.2 0.7 copy.31
  345.9 0.5 copy-done.3
  346.5 0.9 copy.32
  347.4 0.5 copy-done.2
  347.9 0.9 copy.33
  348.8 0.5 copy-done.1
  349.3 0.9 copy.34
  (12 shorter events, 0.0 us)
Async XLA Ops:
  0.6 0.7 copy-start.11
  0.7 1.3 copy-start.9
  1.9 0.7 copy-start.10
  3.2 0.9 copy-start.8
  3.6 0.9 copy-start.5
  3.6 1.0 copy-start.6
  3.7 1.0 copy-start.7
  338.8 5.2 %copy-start = (f32[1024,192]{1,0:T(8,128)S(1)}, f32[1024,192]{1,0:T(8,128)}, u32[]{:S(2)}) copy-start(f32[1024,192]{1,0:T(8,128)} %get-tuple-element.46) | copy-start | bytes 2359300
  344.0 1.2 copy-start.4
  345.2 1.3 copy-start.3
  346.5 1.4 copy-start.2
  347.9 1.4 copy-start.1

commit v4 on v3

--- a/solution.py
+++ b/solution.py
@@ -233,18 +233,16 @@
                     when(ok, lambda: self.hop(owner, k, s, p, where).wait_send())
 
 
-class LineScatter:
+class LineSum:
     def __init__(self, st, part, rows, width, parts):
         self.st, self.part, self.rows, self.width, self.parts = st, part, rows, width, parts
         nt = st.nt
         self.chunk = rows // parts
-        shape = (2, (nt - 1) * parts, self.chunk, width)
-        self.kept = min(2, nt - 1) * parts
-        few = (2, self.kept, self.chunk, width)
-        self.hc = [st.scratch(VMEM(x, jnp.int16)) for x in (few, shape)]
-        self.hk = [st.scratch(VMEM(x[:2] + (8, 128), jnp.float32)) for x in (few, shape)]
-        self.hd = [st.scratch(DMA((2, 2, (nt - 1) * parts))) for _ in range(2)]
-        st.links.add("line")
+        shape = (nt, parts, self.chunk, width)
+        self.hc = [st.scratch(VMEM(shape, jnp.int16)) for _ in range(2)]
+        self.hk = [st.scratch(VMEM(shape[:2] + (8, 128), jnp.float32)) for _ in range(2)]
+        self.hd = [st.scratch(DMA((2, nt, parts))) for _ in range(2)]
+        st.links.add("tp")
 
     def bind(self, get):
         self.x = get(self.part)
@@ -254,174 +252,171 @@
         self.t = lax.axis_index("tp")
         return self
 
-    def hops(self, k, u, where):
-        w = lax.rem(u, self.kept)
+    def far(self, i, j):
+        return (jnp.abs(i - j) == 3) if self.st.nt == 4 else (i != i)
+
+    def sends(self, j, p):
+        t = self.t
+        where = jnp.where(self.far(t, j), jnp.where(j > t, t + 1, t - 1), j)
+        slot = jnp.where(self.far(t, j), where, t)
         return (
-            remote(self.cs.at[k, w], self.cr.at[k, u], self.ss.at[0, k, u], self.rs.at[0, k, u], {"tp": where}),
-            remote(self.sc.at[k, w], self.sr.at[k, u], self.ss.at[1, k, u], self.rs.at[1, k, u], {"tp": where}),
+            remote(self.cs.at[j, p], self.cr.at[slot, p], self.ss.at[0, j, p], self.rs.at[0, slot, p], {"tp": where}),
+            remote(self.sc.at[j, p], self.sr.at[slot, p], self.ss.at[1, j, p], self.rs.at[1, slot, p], {"tp": where}),
         )
+
+    def arrival(self, slot, p):
+        for k, (x, y) in enumerate(((self.cs, self.cr), (self.sc, self.sr))):
+            remote(x.at[slot, p], y.at[slot, p], self.ss.at[k, slot, p], self.rs.at[k, slot, p], {"tp": self.t}).wait_recv()
+
+    def dest(self, o):
+        nt, t = self.st.nt, self.t
+        if nt != 4:
+            return lax.rem(t + 1 + o, nt)
+        inner = jnp.where(o == 2, 2, 1 + 2 * o)
+        x = jnp.where((t == 0) | (t == nt - 1), 3 - o, inner)
+        lo = lax.rem(lax.rem(t, 2) + lax.rem(x, 2), 2)
+        return 2 * lax.rem(t // 2 + x // 2, 2) + lo
 
     def _rows(self, base, r, n):
         return self.x[pl.ds(pl.multiple_of(base + r, n), n), :]
 
-    def slots(self):
-        return 4 * (self.st.nt - 1)
-
-    def step(self, v, produce=None):
+    def send(self, p, produce=None, beside=None):
         nt, t, chunk = self.st.nt, self.t, self.chunk
-        p, v = v // self.slots(), lax.rem(v, self.slots())
-        k = lax.rem(v, 2)
-        s = v // 2 - jnp.where(k == 0, t, nt - 1 - t)
-        j = jnp.where(k == 0, nt - 1 - s, s)
-        way = 1 - 2 * k
-        u = s * self.parts + p
-        first = t == jnp.where(k == 0, 0, nt - 1)
-        passing = (s >= 0) & (s < nt - 1) & jnp.where(k == 0, t < j, t > j)
-
-        @pl.when(passing)
-        def _():
+
+        def one(o, _):
+            j = self.dest(o)
             if produce is not None:
-                pl.when(p == 0)(lambda: produce(j))
-
-            @pl.when(first)
-            def _():
-                self.cr[k, u] = jnp.zeros((chunk, self.width), jnp.int16)
-                self.sr[k, u] = jnp.zeros((8, 128), jnp.float32)
-
-            @pl.when(jnp.logical_not(first))
-            def _():
-                for c in self.hops(k, u, t):
-                    c.wait_recv()
-
-            @pl.when(u >= self.kept)
-            def _():
-                for c in self.hops(k, u - self.kept, t + way):
-                    c.wait_send()
-
-            base, w = j * self.rows + p * chunk, lax.rem(u, self.kept)
-            row_encode(
-                lambda r, n: self._rows(base, r, n) + row_decode(self.cr.at[k, u], self.sr.at[k, u], r, n),
-                self.cs.at[k, w],
-                self.sc.at[k, w],
-                chunk,
-            )
-            for c in self.hops(k, u, t + way):
+                produce(j)
+            base = j * self.rows + p * chunk
+            if nt == 4:
+                relay = ((t == 1) & (j == 3)) | ((t == 2) & (j == 0))
+
+                @pl.when(relay)
+                def _():
+                    self.arrival(t, p)
+                    row_encode(
+                        lambda r, n: self._rows(base, r, n) + row_decode(self.cr.at[t, p], self.sr.at[t, p], r, n),
+                        self.cs.at[j, p],
+                        self.sc.at[j, p],
+                        chunk,
+                    )
+
+                plain = jnp.logical_not(relay)
+            else:
+                plain = True
+            when(plain, lambda: row_encode(lambda r, n: self._rows(base, r, n), self.cs.at[j, p], self.sc.at[j, p], chunk))
+            for c in self.sends(j, p):
                 c.start()
-
-    def relay(self, p, produce=None, beside=None):
-        n = self.slots()
-
-        def one(v, _):
-            self.step(v, produce)
             if beside is not None:
-                beside(v)
+                beside(o)
             return 0
 
-        lax.fori_loop(p * n, (p + 1) * n, one, 0)
+        lax.fori_loop(0, nt - 1, one, 0)
 
     def total(self, p, put):
         nt, t, chunk = self.st.nt, self.t, self.chunk
-        right, left = (nt - 1 - t) * self.parts + p, t * self.parts + p
-        from_left, from_right = t > 0, t < nt - 1
-
-        @pl.when(from_left)
-        def _():
-            for c in self.hops(0, right, t):
-                c.wait_recv()
-
-        @pl.when(from_right)
-        def _():
-            for c in self.hops(1, left, t):
-                c.wait_recv()
-
-        at_r = jnp.where(from_left, right, 0)
-        at_l = jnp.where(from_right, left, 0)
+        sources = [lax.rem(t + 1 + i, nt) for i in range(nt - 1)]
+        for i in sources:
+            pl.when(jnp.logical_not(self.far(i, t)))(lambda: self.arrival(i, p))
         base = t * self.rows + p * chunk
 
-        def body(i, _):
-            r = pl.multiple_of(i * 16, 16)
+        def body(n, _):
+            r = pl.multiple_of(n * 16, 16)
             x = self._rows(base, r, 16)
-            a = row_decode(self.cr.at[0, at_r], self.sr.at[0, at_r], r, 16)
-            b = row_decode(self.cr.at[1, at_l], self.sr.at[1, at_l], r, 16)
-            put(r, x + jnp.where(from_left, a, 0.0) + jnp.where(from_right, b, 0.0))
+            for i in sources:
+                y = row_decode(self.cr.at[i, p], self.sr.at[i, p], r, 16)
+                x = x + (jnp.where(self.far(i, t), 0.0, y) if nt == 4 else y)
+            put(r, x)
             return 0
 
         lax.fori_loop(0, chunk // 16, body, 0)
 
     def finish(self):
-        nt, t = self.st.nt, self.t
-
-        def step(v, _):
-            s, k = v // 2, lax.rem(v, 2)
-            j = jnp.where(k == 0, nt - 1 - s, s)
-            later = s + self.kept // self.parts
-            i = jnp.where(k == 0, nt - 1 - later, later)
-            waited = (later < nt - 1) & jnp.where(k == 0, t < i, t > i)
-
-            @pl.when(jnp.where(k == 0, t < j, t > j) & jnp.logical_not(waited))
-            def _():
-                for p in range(self.parts):
-                    for c in self.hops(k, s * self.parts + p, t + 1 - 2 * k):
-                        c.wait_send()
-
+        def one(o, _):
+            for p in range(self.parts):
+                for c in self.sends(self.dest(o), p):
+                    c.wait_send()
             return 0
 
-        lax.fori_loop(0, 2 * (nt - 1), step, 0)
+        lax.fori_loop(0, self.st.nt - 1, one, 0)
 
 
 class ChipGather:
     def __init__(self, st, w, full, rows):
         self.st, self.w, self.full, self.rows = st, w, full, rows
-        self.hs = st.scratch(DMA((st.nd,)))
-        self.hr = st.scratch(DMA((st.nd,)))
+        self.square = st.nd == 8
+        self.hops = 4 if self.square else st.nd // 2 - 1
+        self.hs, self.hr = (st.scratch(DMA((2 * self.hops + 1,))) for _ in range(2))
         self.hl = st.scratch(DMA((1,)))
         st.links |= {"chips", "twin"}
 
     def bind(self, get):
         self.x, self.o, self.ss, self.rs, ls = (get(h) for h in (self.w, self.full, self.hs, self.hr, self.hl))
-        nd = self.st.nd
+        nd, rows, n = self.st.nd, self.rows, self.hops
         d = lax.axis_index("dp")
-        twin = {"dp": d + 1 - 2 * lax.rem(d, 2)}
-        nc = nd // 2
-
-        def at(i):
-            return self.o.at[pl.ds(pl.multiple_of(i * self.rows, self.rows), self.rows)]
+        core, chip = lax.rem(d, 2), d // 2
+        twin = {"dp": d + 1 - 2 * core}
+
+        def at(i, part=None):
+            if part is None:
+                return self.o.at[pl.ds(pl.multiple_of(i * rows, rows), rows)]
+            return self.o.at[pl.ds(pl.multiple_of(i * rows + part * (rows // 2), rows // 2), rows // 2)]
+
+        beside = [chip + 1 - 2 * lax.rem(chip, 2), lax.rem(chip + 2, 4)]
+        near = [2 * c + core for c in beside]
+        diagonal = 2 * lax.rem(beside[0] + 2, 4) + core
+
+        def came(i):
+            if not self.square:
+                return at(lax.rem(d - 2 * i - 2 + nd, nd))
+            return at(near[i]) if i < 2 else at(diagonal, i - 2)
+
+        def hop(i):
+            if not self.square:
+                src, dst, where = self.x, at(d), lax.rem(d + 2 * i + 2, nd)
+            elif i < 2:
+                src, dst, where = self.x, at(d), near[i]
+            else:
+                src = dst = at(near[i - 2], i - 2)
+                where = near[3 - i]
+            return remote(src, dst, self.ss.at[i], self.rs.at[i], {"dp": where})
+
+        def landed(i):
+            return remote(came(i), came(i), self.ss.at[i], self.rs.at[i], twin)
+
+        def give(i):
+            src, dst = (self.x, at(d)) if i == 0 else (came(i - 1), came(i - 1))
+            return remote(src, dst, self.ss.at[n + i], self.rs.at[n + i], twin)
 
         self.own = lambda: pltpu.make_async_copy(self.x, at(d), ls.at[0])
-        self.out = lambda i: remote(self.x, at(d), self.ss.at[i], self.rs.at[i], {"dp": lax.rem(d + 2 * i, nd)})
-
-        def fwd(i):
-            src = self.x if i == 0 else at(lax.rem(d - 2 * i + nd, nd))
-            dst = at(lax.rem(d - 2 * i + nd, nd))
-            j = 0 if i == 0 else nc + i
-            return remote(src, dst, self.ss.at[j], self.rs.at[j], twin)
-
-        self.fwd, self.nc = fwd, nc
+        self.hop, self.landed, self.give = hop, landed, give
         return self
 
     def start(self):
-        for i in range(1, self.nc):
-            self.out(i).start()
-        self.fwd(0).start()
+        for i in range(2 if self.square else self.hops):
+            self.hop(i).start()
+        self.give(0).start()
         self.own().start()
 
     def forward(self, i):
-        self.out(i).wait_recv()
-        self.fwd(i).start()
+        self.landed(i).wait_recv()
+        if self.square and i < 2:
+            self.hop(i + 2).start()
+        self.give(i + 1).start()
 
     def forwards(self):
-        return [functools.partial(self.forward, i) for i in range(1, self.nc)]
+        return [functools.partial(self.forward, i) for i in range(self.hops)]
 
     def arrived(self):
-        for i in range(self.nc):
-            self.fwd(i).wait_recv()
+        for i in range(self.hops + 1):
+            self.give(i).wait_recv()
         self.own().wait()
 
     def finish(self):
-        for i in range(self.nc):
-            self.fwd(i).wait_send()
-        for i in range(1, self.nc):
-            self.out(i).wait_send()
+        for i in range(self.hops + 1):
+            self.give(i).wait_send()
+        for i in range(self.hops):
+            self.hop(i).wait_send()
 
 
 class GradScatter:
@@ -433,13 +428,14 @@
         wide = max(widths)
         self.hg = st.scratch(VMEM((2, 2 * self.m * shard, wide), jnp.float32))
         self.ht = st.scratch(VMEM((2, self.m, shard, wide), jnp.float32))
-        self.hs = st.scratch(VMEM((2, self.m, shard, wide), jnp.int16))
-        self.hk = st.scratch(VMEM((2, self.m, 1, wide), jnp.float32))
+        self.slots = self.chunks - (self.m == 1)
+        self.hs = st.scratch(VMEM((self.slots, self.m, shard, wide), jnp.int16))
+        self.hk = st.scratch(VMEM((self.slots, self.m, 1, wide), jnp.float32))
         self.hcr = [st.scratch(VMEM((nc - 1, shard, w), jnp.int16)) for w in widths]
         self.hkr = [st.scratch(VMEM((nc - 1, 1, w), jnp.float32)) for w in widths]
         self.ha = sums
         self.hgs = [st.scratch(DMA((2, self.m))) for _ in range(2)]
-        self.hss = st.scratch(DMA((2, 2, self.m)))
+        self.hss = st.scratch(DMA((2, self.slots, self.m)))
         self.hsr = st.scratch(DMA((len(widths), 2, nc - 1)))
         self.hf = st.scratch(pltpu.SemaphoreType.REGULAR)
         st.links |= {"chips", "twin"}
@@ -468,13 +464,13 @@
             self.twin,
         )
 
-    def sums(self, a, r, e, dest):
+    def sums(self, a, i, e, dest):
         cols, nc = pl.ds(0, self.widths[a]), self.nc
         slot = jnp.maximum(lax.rem(dest - self.chip + nc, nc) - 1, 0)
         where = {"dp": 2 * dest + self.core}
         return (
-            remote(self.cs.at[r, e, :, cols], self.cr[a].at[slot], self.ss.at[0, r, e], self.sr.at[a, 0, slot], where),
-            remote(self.sc.at[r, e, :, cols], self.kr[a].at[slot], self.ss.at[1, r, e], self.sr.at[a, 1, slot], where),
+            remote(self.cs.at[i, e, :, cols], self.cr[a].at[slot], self.ss.at[0, i, e], self.sr.at[a, 0, slot], where),
+            remote(self.sc.at[i, e, :, cols], self.kr[a].at[slot], self.ss.at[1, i, e], self.sr.at[a, 1, slot], where),
         )
 
     def compute(self, a, i, pieces):
@@ -508,29 +504,20 @@
             self.gift(a, r, e).wait_recv()
             dest = self.chunk(i) * self.m + e
             away = dest != self.chip
-
-            def past(b, j):
-                old = self.chunk(j) * self.m + e
-
-                @pl.when(old != self.chip)
-                def _():
-                    for c in self.sums(b, r, e, old):
-                        c.wait_send()
-
-            pl.when(i >= 2)(lambda: past(a, i - 2))
-            if a:
-                pl.when(i < 2)(lambda: past(a - 1, i - 2 + self.chunks))
             own = self.half(e, self.core)
 
             @pl.when(away)
             def _():
+                if a:
+                    for c in self.sums(a - 1, i, e, dest):
+                        c.wait_send()
                 over_cols(
                     self.widths[a],
                     lambda cols: col_encode(
-                        self.g[r, own, cols] + self.t[r, e, :, cols], self.cs.at[r, e], self.sc.at[r, e], cols
+                        self.g[r, own, cols] + self.t[r, e, :, cols], self.cs.at[i, e], self.sc.at[i, e], cols
                     ),
                 )
-                for c in self.sums(a, r, e, dest):
+                for c in self.sums(a, i, e, dest):
                     c.start()
 
             @pl.when(jnp.logical_not(away))
@@ -564,16 +551,17 @@
 
     def finish(self):
         a = len(self.widths) - 1
-        for i in range(max(0, self.chunks - 2), self.chunks):
-            r = (a * self.chunks + i) % 2
+        for i in range(self.chunks):
             for e in range(self.m):
-                self.gift(a, r, e).wait_send()
-                dest = self.chunk(i) * self.m + e
-
-                @pl.when(dest != self.chip)
-                def _():
-                    for c in self.sums(a, r, e, dest):
-                        c.wait_send()
+                if i >= self.chunks - 2:
+                    self.gift(a, (a * self.chunks + i) % 2, e).wait_send()
+                if i < self.slots:
+                    dest = self.chunk(i) * self.m + e
+
+                    @pl.when(dest != self.chip)
+                    def _():
+                        for c in self.sums(a, i, e, dest):
+                            c.wait_send()
 
 
 class FullSum:
@@ -722,7 +710,7 @@
     h_wg, h_wu, h_wd = (room((width, units), low) for _ in range(3))
     h_q, h_dc, h_ch = (room((n_kv, tiles, group * 128, 128), low) for _ in range(3))
     h_k, h_v = (room((n_kv, 3 * span, 128), low) for _ in range(2))
-    h_kt, h_vt = (room((n_kv, 128, 3 * span), low) for _ in range(2))
+    h_vt = room((n_kv, 128, 3 * span), low)
     h_win = room((3, span, 2 * kvw), low)
     h_ctx = room((span, qw), low)
     h_lse, h_delta = (room((n_kv, tiles, 1, group * 128)) for _ in range(2))
@@ -742,7 +730,7 @@
     ag2 = LineGather(st, h_h2, own, parts)
     ag3 = LineGather(st, h_gr, own, parts)
     ag4 = LineGather(st, h_rl, own, parts)
-    rs = LineScatter(st, h_part, own, width, parts)
+    rs = LineSum(st, h_part, own, width, parts)
     wa = ChipGather(st, s_wa, h_wa, shard)
     wg = ChipGather(st, s_wg, h_wg, shard)
     wu = ChipGather(st, s_wu, h_wu, shard)
@@ -758,7 +746,7 @@
         tok, g1, g2, og, begin_ref, cos_ref, sin_ref = (get(h) for h in (h_tok, h_g1, h_g2, h_og, h_begin, h_cos, h_sin))
         h1, h2, gr, rl = (get(h) for h in (h_h1, h_h2, h_gr, h_rl))
         wa_ref, wg_ref, wu_ref, wd_ref = (get(h) for h in (h_wa, h_wg, h_wu, h_wd))
-        q, k, v, kt, vt, win, ctx, ch, lse = (get(h) for h in (h_q, h_k, h_v, h_kt, h_vt, h_win, h_ctx, h_ch, h_lse))
+        q, k, v, vt, win, ctx, ch, lse = (get(h) for h in (h_q, h_k, h_v, h_vt, h_win, h_ctx, h_ch, h_lse))
         dc, delta, dq, dk, dv = (get(h) for h in (h_dc, h_delta, h_dq, h_dk, h_dv))
         res, rg, part, ia, gl, ul, mine = (get(h) for h in (h_res, h_rg, h_part, h_ia, h_gl, h_ul, h_mine))
         xl = ul.at[:, pl.ds(0, qkvw)]
@@ -782,7 +770,7 @@
             per_tile(piece // 16, 16, tile)
             ag1.start(p)
         gr[rows_of(t), :] = og[...]
-        in_turn(ag1.arrivals(), wa.forwards())
+        in_turn(ag1.arrivals(), wa.forwards() + [wd.start])
         for p in range(parts):
             ag3.start(p)
         wa.arrived()
@@ -812,9 +800,7 @@
                 x = win[b, pl.ds(r, 128), :].astype(f32)
                 at = pl.ds(pl.multiple_of(b * span + r, 128), 128)
                 for g in range(n_kv):
-                    y = lane_take(x, g * HD)
-                    k[g, at, :] = y.astype(low)
-                    kt[g, :, at] = y.T.astype(low)
+                    k[g, at, :] = lane_take(x, g * HD).astype(low)
                     y = lane_take(x, kvw + g * HD)
                     v[g, at, :] = y.astype(low)
                     vt[g, :, at] = y.T.astype(low)
@@ -822,6 +808,9 @@
             per_tile(tiles, 128, tile)
 
         unpack(2)
+        pass_d, pass_g, pass_u = wd.forwards(), wg.forwards(), wu.forwards()
+        for x in pass_d[:2]:
+            x()
         for i in (1, 2):
 
             @pl.when(d < i)
@@ -830,8 +819,10 @@
 
             when(d >= i, lambda: ahead(i).wait_recv())
             unpack(2 - i)
-        wd.start()
         wg.start()
+        wu.start()
+        for x in pass_d[2:]:
+            x()
 
         def attend(u, _):
             g, i = u // tiles, lax.rem(u, tiles)
@@ -851,11 +842,9 @@
         arrive3 = ag3.arrivals()
         lax.fori_loop(0, half, attend, 0)
         cut = len(arrive3) // 2
-        for x in arrive3[:cut]:
-            x()
+        in_turn(arrive3[:cut], pass_g[:2])
         lax.fori_loop(half, n_kv * tiles, attend, 0)
-        for x in arrive3[cut:]:
-            x()
+        in_turn(arrive3[cut:], pass_u[:2])
 
         def pack(r):
             x = 0.0
@@ -870,10 +859,17 @@
             for c in range(0, width, 512):
                 part[rows_of(j), c : c + 512] = nt_dot(ctx[rows_of(j), :], wa_ref[c : c + 512, qkvw:])
 
-        rs.relay(0, out_rows)
-        in_turn(wd.forwards(), wg.forwards())
-        wu.start()
+        rs.send(0, out_rows)
+        rs.send(1)
         out_rows(t)
+        kt = vt
+
+        def keys_back(r):
+            for g in range(n_kv):
+                kt[g, :, pl.ds(r, 128)] = k[g, pl.ds(r, 128), :].T
+
+        per_tile(3 * tiles, 128, keys_back)
+        in_turn(pass_g[2:], pass_u[2:])
 
         for p in range(parts):
 
@@ -883,11 +879,8 @@
                 res[at, :] = x
                 h2[own_rows(p, r), :] = (x * inverse_rms(x) * g2[...]).astype(low)
 
-            if p:
-                rs.relay(p)
             rs.total(p, put)
             ag2.start(p)
-        rs.finish()
         wd.arrived()
 
         def back_act(c):
@@ -897,7 +890,8 @@
         for x in arrive2[:parts]:
             x()
         per_tile(units // 256, 256, back_act)
-        in_turn(arrive2[parts:], wu.forwards())
+        for x in arrive2[parts:]:
+            x()
         wg.arrived()
         wu.arrived()
 
@@ -920,7 +914,6 @@
                     ul[rows, :], wu_ref[c : c + 512, :]
                 )
 
-        n = rs.slots()
         last_slot = gs.chunks + 1
         grads = (
             ((gr, lambda: ia[...]),),
@@ -929,17 +922,18 @@
             ((h1, lambda: xl[...]), (rl, lambda: ctx[...])),
         )
 
-        def beside(a, shift=0):
-            every = max(1, n // last_slot)
-
-            def go(w):
-                w = w - shift
-                pl.when((lax.rem(w, every) == 0) & (w < every * last_slot))(lambda: gs.slot(a, w // every, grads[a]))
-
-            return go
-
-        rs.relay(0, rows_back, beside(0))
+        def weight_grads(a, first=0):
+            def one(w, _):
+                gs.slot(a, w, grads[a])
+                return 0
+
+            lax.fori_loop(first, last_slot, one, 0)
+
+        rs.finish()
+        rs.send(0, rows_back, lambda o: gs.slot(0, o, grads[0]))
+        rs.send(1)
         rows_back(t)
+        weight_grads(0, nt - 1)
         mine[...] = jnp.zeros_like(mine)
 
         for p in range(parts):
@@ -956,11 +950,8 @@
                 rg[at, :] = y
                 rl[own_rows(p, r), :] = y.astype(low)
 
-            if p:
-                rs.relay(p, None, beside(p, p * n))
             rs.total(p, put)
             ag4.start(p)
-        rs.finish()
 
         def ffn_rows(r):
             cols = pl.ds(r, 512)
@@ -969,7 +960,7 @@
         def while_gathered(w, _):
             ag4.arrive_at(w)
             pl.when(w < width // 512)(lambda: ffn_rows(pl.multiple_of(w * 512, 512)))
-            gs.slot(2, w, grads[2])
+            gs.slot(1, w, grads[1])
             return 0
 
         lax.fori_loop(0, max((nt - 1) * parts, last_slot, width // 512), while_gathered, 0)
@@ -984,19 +975,15 @@
                 z = y.astype(f32) * ch[g, i, at, :].astype(f32)
                 delta[g, i, :, at] = jnp.sum(z.T, axis=0, keepdims=True)
 
+        rs.finish()
+        for p in range(parts):
+            rs.send(p)
         per_tile(tiles, 128, context_back)
         dk[...] = jnp.zeros_like(dk)
         dv[...] = jnp.zeros_like(dv)
         count = n_kv * tiles
-        slots = n * parts
-        per = -(-slots // count)
 
         def attend_back(u, _):
-            def pump(w, _):
-                pl.when(w < slots)(lambda: rs.step(w))
-                return 0
-
-            lax.fori_loop(u * per, u * per + per, pump, 0)
             g, i = u // tiles, lax.rem(u, tiles)
             at = pl.multiple_of(i * 128, 128)
             keys = pl.ds(at, reach)
@@ -1007,9 +994,11 @@
             dv[g, keys, :] += dot(p.astype(low), dd)
             dk[g, keys, :] += dot(ds, qq)
             dq[g, i] = dot(kt[g, :, keys], ds).T
+            gs.slot(2, u, grads[2])
             return 0
 
         lax.fori_loop(0, count, attend_back, 0)
+        weight_grads(2, count)
 
         def kv_rows(b, r):
             at = pl.ds(pl.multiple_of(b * span + r, 128), 128)
@@ -1055,15 +1044,25 @@
                 get(o_out)[at, :] = (res[at, :] + x).astype(low)
 
             rs.total(p, put)
-        rs.finish()
         ready = get(h_ready)
-        for ok, where in ((t > 0, t - 1), (t < nt - 1, t + 1)):
-            when(ok, lambda: pl.semaphore_signal(ready, inc=1, device_id={"tp": where}, device_id_type=MESH))
+        for i in range(1, nt):
+            pl.semaphore_signal(ready, inc=1, device_id={"tp": lax.rem(t + i, nt)}, device_id_type=MESH)
 
         def put_down(cols, x):
             get(o_dd)[cols, :] = x.T
 
+        def put_gate(cols, x):
+            get(o_dg)[:, cols] = x
+
+        def put_up(cols, x):
+            get(o_du)[:, cols] = x
+
+        def put_attn(cols, x):
+            get(o_da)[:, cols] = x
+
         gs.collect(0, put_down)
+        gs.collect(1, put_gate)
+        gs.collect(2, put_up)
         for i in (1, 2):
 
             @pl.when(d + i < nd)
@@ -1089,18 +1088,12 @@
             for c in range(0, width, 512):
                 part[rows_of(j), c : c + 512] = nt_dot(xl[rows_of(j), :], wa_ref[c : c + 512, :qkvw])
 
-        pl.semaphore_wait(ready, (t > 0).astype(jnp.int32) + (t < nt - 1).astype(jnp.int32))
-        rs.relay(0, hidden_rows, beside(3))
+        rs.finish()
+        pl.semaphore_wait(ready, nt - 1)
+        rs.send(0, hidden_rows)
+        rs.send(1)
         hidden_rows(t)
-
-        def put_gate(cols, x):
-            get(o_dg)[:, cols] = x
-
-        def put_up(cols, x):
-            get(o_du)[:, cols] = x
-
-        def put_attn(cols, x):
-            get(o_da)[:, cols] = x
+        weight_grads(3)
 
         for p in range(parts):
 
@@ -1114,11 +1107,6 @@
                 e = inverse * (e - normed * jnp.mean(e * normed, axis=-1, keepdims=True))
                 get(o_tg)[at, :] = rg[at, :] + e
 
-            if p:
-                rs.relay(p)
-            else:
-                gs.collect(1, put_gate)
-                gs.collect(2, put_up)
             rs.total(p, put)
         full.run(get)
         gs.collect(3, put_attn)

time: 351 us -> 305 us (0.87)
  Pallas kernels: 331 us -> 283 us
    pallas_call x1, Pallas kernels: 331 us -> 283 us  [run(): pl.pallas_call(kernel, out_shape=[jax.ShapeDtypeStruct(s, t) for s, t, _...]
where the time goes in v4:
time: 305 us; the launch traced here: 303 us
  Pallas kernels  283 us (93%)
  local copies, waits for them, and re-layouts  17.6 us (6%)
    pallas_call x1, Pallas kernels, run(): pl.pallas_call(kernel, out_shape=[jax.ShapeDtypeStruct(s, t) for s, t, _...  283 us
    unnamed x29, local copies, waits for them, and re-layouts  7.95 us

profile of v4, /device:TPU:1, one launch (start us, length us, event | category | flops | bytes accessed | tf_op | source)
XLA Modules:
  0.0 302.9 jit_solution(1021818399631585991)
XLA Ops:
  0.7 0.6 copy-done.11
  1.3 0.6 fusion.2
  1.9 0.0 copy-done.9
  1.9 0.6 broadcast_in_dim.11.refs_1_
  2.5 0.1 copy-done.10
  2.6 0.6 broadcast_in_dim.12.refs_2_
  3.2 0.4 fusion
  3.6 0.0 copy-start.5
  3.6 0.0 copy-start.6
  3.7 0.0 copy-start.7
  3.7 0.4 copy-done.8
  4.1 0.5 copy-done.5
  4.6 0.1 copy-done.6
  4.6 0.1 copy-done.7
  4.7 0.9 concatenate.7.refs_7_
  5.6 0.1 tile.20
  5.7 1.2 copy.25.refs_6_
  6.8 0.1 tile.8
  6.9 1.2 copy.24.refs_5_
  8.1 283.5 %layer.1 = (bf16[128,1536]{1,0:T(8,128)(2,1)}, f32[128,1536]{1,0:T(8,128)}, f32[1,3072]{1,0:T(1,128)}, f32[1024,192]{1,0:T(8,128)}, f32[192,1024]{1,0:T(8,128)},...) custom-call(bf16[128,1536]{1,0:T(8,128)(2,1)} %refs_0_.1, f32[1,1536]{1,0:T(1,128)} %broadcast_in_dim.11.refs_1_, ...), custom_call_target="tpu_custom_call" | custom-call | tf_op jit(solution)/shard_map/layer/pallas_call | solution.py:100
  291.5 1.4 slice_reduce_fusion
  293.0 1.8 fusion.1
  294.8 1.9 slice_bitcast_fusion
  296.7 1.2 copy.26
  297.9 0.0 copy-done.4
  297.9 0.7 copy.31
  298.7 0.5 copy-done.3
  299.2 0.9 copy.32
  300.1 0.5 copy-done.2
  300.6 0.9 copy.33
  301.5 0.5 copy-done.1
  302.0 0.9 copy.34
  (12 shorter events, 0.0 us)
Async XLA Ops:
  0.6 0.7 copy-start.11
  0.7 1.3 copy-start.9
  1.9 0.7 copy-start.10
  3.2 0.9 copy-start.8
  3.6 0.9 copy-start.5
  3.6 1.0 copy-start.6
  3.7 1.0 copy-start.7
  291.5 5.2 %copy-start = (f32[1024,192]{1,0:T(8,128)S(1)}, f32[1024,192]{1,0:T(8,128)}, u32[]{:S(2)}) copy-start(f32[1024,192]{1,0:T(8,128)} %get-tuple-element.46) | copy-start | bytes 2359300
  296.7 1.2 copy-start.4
  297.9 1.3 copy-start.3
  299.2 1.4 copy-start.2
  300.6 1.4 copy-start.1

commit v5 on v4

--- a/solution.py
+++ b/solution.py
@@ -425,14 +425,15 @@
         self.st, self.shard, self.widths = st, shard, widths
         self.m = math.lcm(2 * shard, 128) // (2 * shard)
         self.chunks = nc // self.m
-        wide = max(widths)
+        self.padded = [-(-w // 128) * 128 for w in widths]
+        wide = max(self.padded)
         self.hg = st.scratch(VMEM((2, 2 * self.m * shard, wide), jnp.float32))
         self.ht = st.scratch(VMEM((2, self.m, shard, wide), jnp.float32))
         self.slots = self.chunks - (self.m == 1)
         self.hs = st.scratch(VMEM((self.slots, self.m, shard, wide), jnp.int16))
         self.hk = st.scratch(VMEM((self.slots, self.m, 1, wide), jnp.float32))
-        self.hcr = [st.scratch(VMEM((nc - 1, shard, w), jnp.int16)) for w in widths]
-        self.hkr = [st.scratch(VMEM((nc - 1, 1, w), jnp.float32)) for w in widths]
+        self.hcr = [st.scratch(VMEM((nc - 1, shard, w), jnp.int16)) for w in self.padded]
+        self.hkr = [st.scratch(VMEM((nc - 1, 1, w), jnp.float32)) for w in self.padded]
         self.ha = sums
         self.hgs = [st.scratch(DMA((2, self.m))) for _ in range(2)]
         self.hss = st.scratch(DMA((2, self.slots, self.m)))
@@ -458,14 +459,14 @@
         return pl.ds(pl.multiple_of((2 * e + core) * self.shard, self.shard), self.shard)
 
     def gift(self, a, r, e):
-        cols = pl.ds(0, self.widths[a])
+        cols = pl.ds(0, self.padded[a])
         return remote(
             self.g.at[r, self.half(e, 1 - self.core), cols], self.t.at[r, e, :, cols], self.gs.at[r, e], self.gr.at[r, e],
             self.twin,
         )
 
     def sums(self, a, i, e, dest):
-        cols, nc = pl.ds(0, self.widths[a]), self.nc
+        cols, nc = pl.ds(0, self.padded[a]), self.nc
         slot = jnp.maximum(lax.rem(dest - self.chip + nc, nc) - 1, 0)
         where = {"dp": 2 * dest + self.core}
         return (
@@ -700,7 +701,7 @@
     o_gains = st.out((1, 2 * width), f32)
     o_dd = st.out((units, shard), f32)
     o_dg, o_du = (st.out((shard, units), f32) for _ in range(2))
-    o_da = st.out((shard, qkvw + qw), f32)
+    o_da, o_db = (st.out((shard, w), f32) for w in (2 * qw, 2 * kvw))
 
     def room(shape, dtype=f32):
         return st.scratch(VMEM(shape, dtype))
@@ -735,7 +736,7 @@
     wg = ChipGather(st, s_wg, h_wg, shard)
     wu = ChipGather(st, s_wu, h_wu, shard)
     wd = ChipGather(st, s_wd, h_wd, shard)
-    gs = GradScatter(st, shard, (units, units, units, qkvw + qw), (room((shard, units)), o_dg, o_du, o_da))
+    gs = GradScatter(st, shard, (units, units, units, 2 * qw, 2 * kvw), (room((shard, units)), o_dg, o_du, o_da, o_db))
     full = FullSum(st, h_mine, o_gains, (1, 2 * width))
     st.links.add("near")
 
@@ -761,6 +762,7 @@
             return pl.ds(pl.multiple_of(j * own, own), own)
 
         wa.start()
+        wd.start()
         for p in range(parts):
 
             def tile(r):
@@ -770,7 +772,8 @@
             per_tile(piece // 16, 16, tile)
             ag1.start(p)
         gr[rows_of(t), :] = og[...]
-        in_turn(ag1.arrivals(), wa.forwards() + [wd.start])
+        pass_a, pass_d, pass_g, pass_u = (x.forwards() for x in (wa, wd, wg, wu))
+        in_turn(ag1.arrivals(), pass_a[:2] + pass_d[:2] + pass_a[2:])
         for p in range(parts):
             ag3.start(p)
         wa.arrived()
@@ -808,8 +811,7 @@
             per_tile(tiles, 128, tile)
 
         unpack(2)
-        pass_d, pass_g, pass_u = wd.forwards(), wg.forwards(), wu.forwards()
-        for x in pass_d[:2]:
+        for x in pass_d[2:]:
             x()
         for i in (1, 2):
 
@@ -821,8 +823,6 @@
             unpack(2 - i)
         wg.start()
         wu.start()
-        for x in pass_d[2:]:
-            x()
 
         def attend(u, _):
             g, i = u // tiles, lax.rem(u, tiles)
@@ -919,7 +919,8 @@
             ((gr, lambda: ia[...]),),
             ((h2, lambda: gl[...]),),
             ((h2, lambda: ul[...]),),
-            ((h1, lambda: xl[...]), (rl, lambda: ctx[...])),
+            ((h1, lambda: xl[:, :qw]), (rl, lambda: ctx[...])),
+            ((h1, lambda: xl[:, qw:]),),
         )
 
         def weight_grads(a, first=0):
@@ -1057,12 +1058,16 @@
         def put_up(cols, x):
             get(o_du)[:, cols] = x
 
-        def put_attn(cols, x):
+        def put_query(cols, x):
             get(o_da)[:, cols] = x
+
+        def put_key(cols, x):
+            get(o_db)[:, cols] = x
 
         gs.collect(0, put_down)
         gs.collect(1, put_gate)
         gs.collect(2, put_up)
+        weight_grads(3)
         for i in (1, 2):
 
             @pl.when(d + i < nd)
@@ -1093,7 +1098,7 @@
         rs.send(0, hidden_rows)
         rs.send(1)
         hidden_rows(t)
-        weight_grads(3)
+        weight_grads(4)
 
         for p in range(parts):
 
@@ -1109,7 +1114,8 @@
 
             rs.total(p, put)
         full.run(get)
-        gs.collect(3, put_attn)
+        gs.collect(3, put_query)
+        gs.collect(4, put_key)
         for x in (ag1, ag2, ag3, ag4, rs, wa, wg, wu, wd, gs):
             x.finish()
         for i in (2, 1):
@@ -1133,6 +1139,41 @@
 
 def dot(a, b):
     return jnp.dot(a, b, preferred_element_type=jnp.float32)
+
+
+def finished(output, tokens_grad, down_sum, gate_sum, up_sum, query_sum, key_sum):
+    shard, qw, kvw = query_sum.shape[0], query_sum.shape[1] // 2, key_sum.shape[1] // 2
+
+    def columns(x, at, n):
+        base = at // 128 * 128
+        slab = x[:, base : base + -(-(at - base + n) // 128) * 128]
+        if slab.shape[1] % 128:
+            slab = jnp.concatenate([slab, jnp.zeros((shard, -slab.shape[1] % 128), slab.dtype)], axis=1)
+        if at > base:
+            slab = pltpu.roll(slab, slab.shape[1] - (at - base), 1)
+        return slab[:, :n]
+
+    def kernel(*refs):
+        (*same, qs, ks), outs = refs[:7], refs[7:]
+        for src, dst in zip(same, outs):
+            dst[...] = src[...]
+        q, k, v, o = outs[5:]
+        q[...] = qs[:, :qw]
+        o[...] = columns(qs, qw, qw).T
+        k[...] = ks[:, :kvw]
+        v[...] = columns(ks, kvw, kvw)
+
+    like = [output, tokens_grad, down_sum, gate_sum, up_sum]
+    shapes = [(x.shape, x.dtype) for x in like]
+    shapes += [((shard, qw), jnp.float32), ((shard, kvw), jnp.float32), ((shard, kvw), jnp.float32), ((qw, shard), jnp.float32)]
+    return pl.pallas_call(
+        kernel,
+        out_shape=[jax.ShapeDtypeStruct(*x) for x in shapes],
+        in_specs=[pl.BlockSpec(memory_space=VMEM)] * 7,
+        out_specs=[pl.BlockSpec(memory_space=VMEM)] * 9,
+        compiler_params=pltpu.CompilerParams(vmem_limit_bytes=66_000_000),
+        name="finish",
+    )(*like, query_sum, key_sum)
 
 
 def on_device(
@@ -1148,23 +1189,13 @@
     cosine = jnp.tile(cosine, (1, 2 * heads[0]))
     sine = jnp.tile(jnp.concatenate([-sine, sine], axis=1), (1, heads[0]))
     begin = (2 * span + jnp.arange(span, dtype=jnp.int32) - positions)[None]
-    output, tokens_grad, gains, down_sum, gate_sum, up_sum, attn_sum = layer(
+    output, tokens_grad, gains, down_sum, gate_sum, up_sum, query_sum, key_sum = layer(
         nd, nt, tokens, attn_gain, ffn_gain, out_grad, begin, cosine, sine, w_attn, w_gate, w_up, w_down_t, heads
     )
-    cuts = (qw, qw + kvw, qw + 2 * kvw)
-    return (
-        output,
-        tokens_grad,
-        gains[0, :width],
-        attn_sum[:, : cuts[0]],
-        attn_sum[:, cuts[0] : cuts[1]],
-        attn_sum[:, cuts[1] : cuts[2]],
-        attn_sum[:, cuts[2] :].T,
-        gains[0, width:],
-        gate_sum,
-        up_sum,
-        down_sum,
+    output, tokens_grad, down_sum, gate_sum, up_sum, wq, wk, wv, wo = finished(
+        output, tokens_grad, down_sum, gate_sum, up_sum, query_sum, key_sum
     )
+    return (output, tokens_grad, gains[0, :width], wq, wk, wv, wo, gains[0, width:], gate_sum, up_sum, down_sum)
 
 
 def solution(mesh):

time: 305 us -> 301 us (0.987)
  local copies, waits for them, and re-layouts: 17.6 us -> 9.36 us
  Pallas kernels: 283 us -> 289 us
    pallas_call x0 -> x1, Pallas kernels: none -> 4.7 us  [finished(): pl.pallas_call(kernel, out_shape=[jax.ShapeDtypeStruct(*x) for x in shape...]
    unnamed x29 -> x18, local copies, waits for them, and re-layouts: 7.95 us -> 4.18 us
where the time goes in v5:
time: 301 us
  Pallas kernels  289 us (96%)
  local copies, waits for them, and re-layouts  9.36 us (3%)
    pallas_call x1, Pallas kernels, run(): pl.pallas_call(kernel, out_shape=[jax.ShapeDtypeStruct(s, t) for s, t, _...  284 us

profile of v5, /device:TPU:1, one launch (start us, length us, event | category | flops | bytes accessed | tf_op | source)
XLA Modules:
  0.0 300.6 jit_solution(8645789636024205680)
XLA Ops:
  0.6 1.3 fusion.1
  2.0 0.4 fusion
  2.4 0.1 tile.20
  2.5 1.2 copy.26.refs_6_
  3.7 0.1 tile.8
  3.8 0.0 copy-start.1
  3.8 0.0 copy-start.2
  3.8 0.0 copy-start.3
  3.8 0.0 copy-start.4
  3.8 1.1 copy.25.refs_5_
  5.0 0.0 copy-done.1
  5.0 0.0 copy-done.2
  5.0 0.0 copy-done.3
  5.0 0.0 copy-done.4
  5.0 0.0 copy-start.6
  5.0 0.9 concatenate.7.refs_7_
  5.9 0.0 copy-done.6
  5.9 0.0 copy-start.7
  5.9 0.6 broadcast_in_dim.11.refs_1_
  6.5 0.1 copy-done.7
  6.6 0.6 broadcast_in_dim.12.refs_2_
  7.2 284.0 %layer.1 = (bf16[128,1536]{1,0:T(8,128)(2,1)}, f32[128,1536]{1,0:T(8,128)}, f32[1,3072]{1,0:T(1,128)}, f32[1024,192]{1,0:T(8,128)}, f32[192,1024]{1,0:T(8,128)},...) custom-call(bf16[128,1536]{1,0:T(8,128)(2,1)} %refs_0_.1, f32[1,1536]{1,0:T(1,128)} %broadcast_in_dim.11.refs_1_, ...), custom_call_target="tpu_custom_call" | custom-call | tf_op jit(solution)/shard_map/layer/pallas_call | solution.py:100
  291.2 4.7 %finish.1 = (bf16[128,1536]{1,0:T(8,128)(2,1)}, f32[128,1536]{1,0:T(8,128)}, f32[1024,192]{1,0:T(8,128)}, f32[192,1024]{1,0:T(8,128)}, f32[192,1024]{1,0:T(8,128...) custom-call(bf16[128,1536]{1,0:T(8,128)(2,1)} %get-tuple-element.28.refs_0_, ...), custom_call_target="tpu_custom_call" | custom-call | tf_op jit(solution)/shard_map/finish/pallas_call | solution.py:1169
  295.9 0.0 copy-start
  295.9 2.5 copy.28
  298.4 0.0 copy-done
  298.4 0.9 copy.27
  299.2 0.0 copy-start.5
  299.2 0.7 copy-done.5
  299.9 0.6 slice_reduce_fusion
  (2 shorter events, 0.0 us)
Async XLA Ops:
  3.8 1.2 copy-start.1
  3.8 1.2 copy-start.2
  3.8 1.2 copy-start.3
  3.8 1.2 copy-start.4
  5.0 0.9 copy-start.6
  5.9 0.7 copy-start.7
  295.9 2.5 copy-start
  299.2 0.7 copy-start.5

commit v6 on v5

--- a/solution.py
+++ b/solution.py
@@ -699,8 +699,7 @@
     o_out = st.out((own, width), low)
     o_tg = st.out((own, width), f32)
     o_gains = st.out((1, 2 * width), f32)
-    o_dd = st.out((units, shard), f32)
-    o_dg, o_du = (st.out((shard, units), f32) for _ in range(2))
+    o_dd, o_dg, o_du = (st.out((shard, units), f32) for _ in range(3))
     o_da, o_db = (st.out((shard, w), f32) for w in (2 * qw, 2 * kvw))
 
     def room(shape, dtype=f32):
@@ -736,7 +735,7 @@
     wg = ChipGather(st, s_wg, h_wg, shard)
     wu = ChipGather(st, s_wu, h_wu, shard)
     wd = ChipGather(st, s_wd, h_wd, shard)
-    gs = GradScatter(st, shard, (units, units, units, 2 * qw, 2 * kvw), (room((shard, units)), o_dg, o_du, o_da, o_db))
+    gs = GradScatter(st, shard, (units, units, units, 2 * qw, 2 * kvw), (o_dd, o_dg, o_du, o_da, o_db))
     full = FullSum(st, h_mine, o_gains, (1, 2 * width))
     st.links.add("near")
 
@@ -1050,7 +1049,7 @@
             pl.semaphore_signal(ready, inc=1, device_id={"tp": lax.rem(t + i, nt)}, device_id_type=MESH)
 
         def put_down(cols, x):
-            get(o_dd)[cols, :] = x.T
+            get(o_dd)[:, cols] = x
 
         def put_gate(cols, x):
             get(o_dg)[:, cols] = x
@@ -1159,13 +1158,13 @@
             dst[...] = src[...]
         q, k, v, o = outs[5:]
         q[...] = qs[:, :qw]
-        o[...] = columns(qs, qw, qw).T
+        o[...] = columns(qs, qw, qw)
         k[...] = ks[:, :kvw]
         v[...] = columns(ks, kvw, kvw)
 
     like = [output, tokens_grad, down_sum, gate_sum, up_sum]
     shapes = [(x.shape, x.dtype) for x in like]
-    shapes += [((shard, qw), jnp.float32), ((shard, kvw), jnp.float32), ((shard, kvw), jnp.float32), ((qw, shard), jnp.float32)]
+    shapes += [((shard, qw), jnp.float32), ((shard, kvw), jnp.float32), ((shard, kvw), jnp.float32), ((shard, qw), jnp.float32)]
     return pl.pallas_call(
         kernel,
         out_shape=[jax.ShapeDtypeStruct(*x) for x in shapes],
@@ -1195,7 +1194,7 @@
     output, tokens_grad, down_sum, gate_sum, up_sum, wq, wk, wv, wo = finished(
         output, tokens_grad, down_sum, gate_sum, up_sum, query_sum, key_sum
     )
-    return (output, tokens_grad, gains[0, :width], wq, wk, wv, wo, gains[0, width:], gate_sum, up_sum, down_sum)
+    return (output, tokens_grad, gains[0, :width], wq, wk, wv, wo.T, gains[0, width:], gate_sum, up_sum, down_sum.T)
 
 
 def solution(mesh):

time: 301 us -> 297 us (0.987)
  local copies, waits for them, and re-layouts: 9.36 us -> 6.02 us
    unnamed x18 -> x14, local copies, waits for them, and re-layouts: 4.18 us -> 0.84 us
where the time goes in v6:
time: 297 us
  Pallas kernels  288 us (97%)
  local copies, waits for them, and re-layouts  6.02 us (2%)
    pallas_call x1, Pallas kernels, run(): pl.pallas_call(kernel, out_shape=[jax.ShapeDtypeStruct(s, t) for s, t, _...  284 us

profile of v6, /device:TPU:1, one launch (start us, length us, event | category | flops | bytes accessed | tf_op | source)
XLA Modules:
  0.0 296.7 jit_solution(8158942574221857987)
XLA Ops:
  0.6 1.3 fusion.1
  2.0 0.4 fusion
  2.4 0.1 tile.20
  2.5 1.2 copy.24.refs_6_
  3.7 0.1 tile.8
  3.8 0.0 copy-start
  3.8 0.0 copy-start.1
  3.8 0.0 copy-start.2
  3.8 0.0 copy-start.3
  3.8 1.1 copy.23.refs_5_
  5.0 0.0 copy-done
  5.0 0.0 copy-done.1
  5.0 0.0 copy-done.2
  5.0 0.0 copy-done.3
  5.0 0.0 copy-start.5
  5.0 0.9 concatenate.7.refs_7_
  5.9 0.0 copy-done.5
  5.9 0.0 copy-start.6
  5.9 0.6 broadcast_in_dim.11.refs_1_
  6.5 0.1 copy-done.6
  6.6 0.6 broadcast_in_dim.12.refs_2_
  7.2 283.8 %layer.1 = (bf16[128,1536]{1,0:T(8,128)(2,1)}, f32[128,1536]{1,0:T(8,128)}, f32[1,3072]{1,0:T(1,128)}, f32[192,1024]{1,0:T(8,128)}, f32[192,1024]{1,0:T(8,128)},...) custom-call(bf16[128,1536]{1,0:T(8,128)(2,1)} %refs_0_.1, f32[1,1536]{1,0:T(1,128)} %broadcast_in_dim.11.refs_1_, ...), custom_call_target="tpu_custom_call" | custom-call | tf_op jit(solution)/shard_map/layer/pallas_call | solution.py:100
  291.0 4.4 %finish.1 = (bf16[128,1536]{1,0:T(8,128)(2,1)}, f32[128,1536]{1,0:T(8,128)}, f32[192,1024]{1,0:T(8,128)}, f32[192,1024]{1,0:T(8,128)}, f32[192,1024]{1,0:T(8,128...) custom-call(bf16[128,1536]{1,0:T(8,128)(2,1)} %get-tuple-element.28.refs_0_, ...), custom_call_target="tpu_custom_call" | custom-call | tf_op jit(solution)/shard_map/finish/pallas_call | solution.py:1168
  295.4 0.0 copy-start.4
  295.4 0.7 copy-done.4
  296.1 0.6 slice_reduce_fusion
  (2 shorter events, 0.0 us)
Async XLA Ops:
  3.8 1.2 copy-start
  3.8 1.2 copy-start.1
  3.8 1.2 copy-start.2
  3.8 1.2 copy-start.3
  5.0 0.9 copy-start.5
  5.9 0.7 copy-start.6
  295.4 0.7 copy-start.4

commit v7 on v6

--- a/solution.py
+++ b/solution.py
@@ -883,12 +883,12 @@
         wd.arrived()
 
         def back_act(c):
-            part[:, pl.ds(c, 256)] = dot(gr[...], wd_ref[:, pl.ds(c, 256)])
+            part[:, pl.ds(c, 512)] = dot(gr[...], wd_ref[:, pl.ds(c, 512)])
 
         arrive2 = ag2.arrivals()
         for x in arrive2[:parts]:
             x()
-        per_tile(units // 256, 256, back_act)
+        per_tile(units // 512, 512, back_act)
         for x in arrive2[parts:]:
             x()
         wg.arrived()

time: 297 us -> 297 us (level)
  no operation moved by 1% of the time
where the time goes in v7:
time: 297 us
  Pallas kernels  288 us (97%)
  local copies, waits for them, and re-layouts  6.02 us (2%)
    pallas_call x1, Pallas kernels, run(): pl.pallas_call(kernel, out_shape=[jax.ShapeDtypeStruct(s, t) for s, t, _...  284 us

profile of v7, /device:TPU:1, one launch (start us, length us, event | category | flops | bytes accessed | tf_op | source)
XLA Modules:
  0.0 296.7 jit_solution(8109556868786856380)
XLA Ops:
  0.6 1.3 fusion.1
  2.0 0.4 fusion
  2.4 0.1 tile.20
  2.5 1.2 copy.24.refs_6_
  3.7 0.1 tile.8
  3.8 0.0 copy-start
  3.8 0.0 copy-start.1
  3.8 0.0 copy-start.2
  3.8 0.0 copy-start.3
  3.8 1.1 copy.23.refs_5_
  5.0 0.0 copy-done
  5.0 0.0 copy-done.1
  5.0 0.0 copy-done.2
  5.0 0.0 copy-done.3
  5.0 0.0 copy-start.5
  5.0 0.9 concatenate.7.refs_7_
  5.9 0.0 copy-done.5
  5.9 0.0 copy-start.6
  5.9 0.6 broadcast_in_dim.11.refs_1_
  6.5 0.1 copy-done.6
  6.6 0.6 broadcast_in_dim.12.refs_2_
  7.2 283.8 %layer.1 = (bf16[128,1536]{1,0:T(8,128)(2,1)}, f32[128,1536]{1,0:T(8,128)}, f32[1,3072]{1,0:T(1,128)}, f32[192,1024]{1,0:T(8,128)}, f32[192,1024]{1,0:T(8,128)},...) custom-call(bf16[128,1536]{1,0:T(8,128)(2,1)} %refs_0_.1, f32[1,1536]{1,0:T(1,128)} %broadcast_in_dim.11.refs_1_, ...), custom_call_target="tpu_custom_call" | custom-call | tf_op jit(solution)/shard_map/layer/pallas_call | solution.py:100
  291.0 4.4 %finish.1 = (bf16[128,1536]{1,0:T(8,128)(2,1)}, f32[128,1536]{1,0:T(8,128)}, f32[192,1024]{1,0:T(8,128)}, f32[192,1024]{1,0:T(8,128)}, f32[192,1024]{1,0:T(8,128...) custom-call(bf16[128,1536]{1,0:T(8,128)(2,1)} %get-tuple-element.28.refs_0_, ...), custom_call_target="tpu_custom_call" | custom-call | tf_op jit(solution)/shard_map/finish/pallas_call | solution.py:1168
  295.4 0.0 copy-start.4
  295.4 0.7 copy-done.4
  296.1 0.6 slice_reduce_fusion
  (2 shorter events, 0.0 us)
Async XLA Ops:
  3.8 1.2 copy-start
  3.8 1.2 copy-start.1
  3.8 1.2 copy-start.2
  3.8 1.2 copy-start.3
  5.0 0.9 copy-start.5
  5.9 0.7 copy-start.6
  295.4 0.7 copy-start.4
